TPU v7x, 32 devices: a whole 2x2x4 slice. The times are simulated.
32 devices in a mesh: gx: 8 (over y, x, core), gy: 4 (over z).
Axes of the slice: x: 2, y: 2, z: 4, core: 2. Of those that a mesh axis runs over, the one named last changes fastest.
Arguments:
- fields: float32 [5, 128, 128, 128], P(None, 'gx', 'gy'), may hold values from -6 to 6
- patch_weight: bfloat16 [2560, 512], replicated, may hold values from -0.125 to 0.125
- trainer_of: int32 [2048, 1], P(('gx', 'gy')), may hold values from 0 to 31; in each aligned block of 64 rows (0 to 63, 64 to 127, ...) at most 4 rows name the same one
- lag_index: int32 [16, 16, 16], P('gx', 'gy'), may hold values from 0 to 1
- w_in: bfloat16 [32, 512, 2048], P(('gx', 'gy')), may hold values from -0.25 to 0.25
- b_in: float32 [32, 2048], P(('gx', 'gy')), may hold values from -3 to 3
- w_out: bfloat16 [32, 2048, 512], P(('gx', 'gy')), may hold values from -0.125 to 0.125
- b_out: float32 [32, 512], P(('gx', 'gy')), may hold values from -3 to 3
Outputs:
- new_fields: float32 [5, 128, 128, 128], P(None, 'gx', 'gy')
- patch_gradient: float32 [2560, 512], replicated
- w_in_gradient: float32 [32, 512, 2048], P(('gx', 'gy'))
- b_in_gradient: float32 [32, 2048], P(('gx', 'gy'))
- w_out_gradient: float32 [32, 2048, 512], P(('gx', 'gy'))
- b_out_gradient: float32 [32, 512], P(('gx', 'gy'))
Inputs may be any that keep to these rules, and one draw needn't show every extreme that they name: `trainer_of`: among the 64 rows of one brick, no trainer is named more than 4 times.
All inputs are finite; a program needn't handle non-finite values.
Results may differ from a plain program's by a relative error of at most 0.0062.
Values may be sent and summed in bfloat16 or wider, within the bound.
A program may use at most 128 MiB of HBM per device.

v0:
```python
import jax
import jax.numpy as jnp
from jax import lax
from jax.experimental import pallas as pl
from jax.experimental.pallas import tpu as pltpu
from jax.sharding import PartitionSpec as P

FIELDS = 5
PATCH = 8
STEPS = 3
EMBED = 512
BLOCK_ROWS = 2


time_step = 0.2
viscosity = 0.5
drift_x = 0.6
drift_y = -0.4
drift_z = 0.3
error_weight = 0.0625


def with_halo(cells, sides, width):
    for axis, dim in sides:
        count = lax.axis_size(axis)
        ends = count - 1
        head = lax.slice_in_dim(cells, 0, width, axis=dim)
        tail = lax.slice_in_dim(cells, cells.shape[dim] - width, cells.shape[dim], axis=dim)
        cells = jnp.concatenate(
            [
                lax.ppermute(tail, axis, [(i, (i + 1) % count) for i in range(ends)]),
                cells,
                lax.ppermute(head, axis, [((i + 1) % count, i) for i in range(ends)]),
            ],
            axis=dim,
        )
    return cells


def shifted(padded, dimension, offset):
    window = [slice(None)]
    for other in (1, 2, 3):
        window.append(slice(2, padded.shape[other] - 2))
    window[dimension] = slice(2 + offset, padded.shape[dimension] - 2 + offset)
    return padded[tuple(window)]


def tendency(padded):
    gradients = []
    laplacian = 0.0
    for dimension in (1, 2, 3):
        back_two = shifted(padded, dimension, -2)
        back_one = shifted(padded, dimension, -1)
        middle = shifted(padded, dimension, 0)
        ahead_one = shifted(padded, dimension, 1)
        ahead_two = shifted(padded, dimension, 2)
        gradients.append((back_two - 8.0 * back_one + 8.0 * ahead_one - ahead_two) / 12.0)
        laplacian = (
            laplacian
            + (-back_two + 16.0 * back_one - 30.0 * middle + 16.0 * ahead_one - ahead_two) / 12.0
        )
    carried = drift_x * gradients[0] + drift_y * gradients[1] + drift_z * gradients[2]
    divergence = gradients[0][1] + gradients[1][2] + gradients[2][3]
    acoustic = jnp.stack(
        [divergence, gradients[0][4], gradients[1][4], gradients[2][4], divergence]
    )
    return viscosity * laplacian - carried - acoustic


def contract_rows(left, right):
    return lax.dot_general(
        left, right, (((0,), (0,)), ((), ())), preferred_element_type=jnp.float32
    )


def contract_cols(left, right):
    return lax.dot_general(
        left, right, (((1,), (1,)), ((), ())), preferred_element_type=jnp.float32
    )


def trainer_step(source, target, valid, w_first, b_first, w_second, b_second):
    pre = jnp.dot(source, w_first, preferred_element_type=jnp.float32) + b_first
    hidden = jax.nn.silu(pre).astype(jnp.bfloat16)
    predict = jnp.dot(hidden, w_second, preferred_element_type=jnp.float32) + b_second
    error = (error_weight * (predict - target.astype(jnp.float32)) * valid).astype(jnp.bfloat16)
    b_second_grad = jnp.sum(error.astype(jnp.float32), axis=0)
    w_second_grad = contract_rows(hidden, error)
    back = contract_cols(error, w_second)
    sigma = jax.nn.sigmoid(pre)
    pre_grad = (back * sigma * (1.0 + pre * (1.0 - sigma))).astype(jnp.bfloat16)
    b_first_grad = jnp.sum(pre_grad.astype(jnp.float32), axis=0)
    w_first_grad = contract_rows(source, pre_grad)
    source_grad = contract_cols(pre_grad, w_first).astype(jnp.bfloat16)
    return (source_grad, w_first_grad, b_first_grad, w_second_grad, b_second_grad)


def patch_kernel(cells_ref, rows_ref, *turned):
    count, inner, lanes = rows_ref.shape[0], cells_ref.shape[1], turned[0].shape[1]
    for part, piece in enumerate(turned):
        cells = cells_ref[0, part * lanes : min(inner, (part + 1) * lanes), :]
        if cells.shape[0] < lanes:
            cells = jnp.concatenate(
                [cells, jnp.zeros((lanes - cells.shape[0], cells.shape[1]), cells.dtype)], axis=0
            )
        piece[...] = cells.T
    parts = []
    for offset in range(PATCH):
        for part, piece in enumerate(turned):
            rows = piece[pl.ds(offset, count, stride=PATCH), :]
            parts.append(rows[:, : min(lanes, inner - part * lanes)])
    rows_ref[...] = jnp.concatenate(parts, axis=1).astype(rows_ref.dtype)


def patchify(state):
    width_x, width_y, width_z = (state.shape[1], state.shape[2], state.shape[3])
    shaped = state.reshape(FIELDS, width_x // PATCH, PATCH, width_y // PATCH, PATCH, width_z)
    cells = shaped.transpose(1, 3, 0, 2, 4, 5).reshape(-1, FIELDS * PATCH * PATCH, width_z)
    columns, inner = cells.shape[0], cells.shape[1]
    count = width_z // PATCH
    return pl.pallas_call(
        patch_kernel,
        grid=(columns,),
        out_shape=jax.ShapeDtypeStruct((columns * count, inner * PATCH), jnp.bfloat16),
        in_specs=[pl.BlockSpec((1, inner, width_z), lambda i: (i, 0, 0))],
        out_specs=pl.BlockSpec((count, inner * PATCH), lambda i: (i, 0)),
        scratch_shapes=[pltpu.VMEM((width_z, 128), jnp.float32)] * pl.cdiv(inner, 128),
        cost_estimate=pl.CostEstimate(
            flops=8 * cells.size, bytes_accessed=6 * cells.size, transcendentals=0
        ),
    )(cells)


def pick(first, second, lag_index):
    count_x, count_y, count_z = lag_index.shape
    lag = jnp.repeat(lag_index, PATCH, axis=2)
    lag = lag.reshape(1, count_x, 1, count_y, 1, count_z * PATCH)
    shape = (FIELDS, count_x, PATCH, count_y, PATCH, count_z * PATCH)
    return jnp.where(lag == 1, second.reshape(shape), first.reshape(shape)).reshape(first.shape)


def pad_third(current):
    return jnp.pad(current, ((0, 0), (0, 0), (0, 0), (2, 2)))


def advance(fields):
    states = []
    current = fields
    for counter in range(STEPS):
        padded = with_halo(current, (("gx", 1), ("gy", 2)), 2)
        current = current + time_step * tendency(pad_third(padded))
        states.append(current)
    return states


def per_device(fields, patch_weight, trainer_of, lag_index, w_in, b_in, w_out, b_out):
    states = advance(fields)
    devices = lax.axis_size("gx") * lax.axis_size("gy")
    picked = patchify(pick(states[0], states[1], lag_index))
    embed = patch_weight.shape[1]
    weight = patch_weight.reshape(-1, PATCH, embed).transpose(1, 0, 2).reshape(-1, embed)
    target = jnp.dot(
        patchify(states[-1]), weight, preferred_element_type=jnp.float32
    ).astype(jnp.bfloat16)
    patch_count = picked.shape[0]
    block_count = patch_count // BLOCK_ROWS
    slot_count = max(2, 2 * block_count // devices)
    owners = trainer_of[:, 0]
    onehot = (owners[:, None] == jnp.arange(devices, dtype=jnp.int32)[None, :]).astype(jnp.int32)
    within_rank = jnp.sum((jnp.cumsum(onehot, axis=0) - onehot) * onehot, axis=1)
    block_slot = owners * slot_count + within_rank

    patch_slot = jnp.repeat(block_slot, BLOCK_ROWS) * BLOCK_ROWS
    patch_slot = patch_slot + jnp.arange(patch_count, dtype=jnp.int32) % BLOCK_ROWS
    slot_rows = slot_count * BLOCK_ROWS
    place = (
        jnp.arange(devices * slot_rows, dtype=jnp.int32)[:, None] == patch_slot[None, :]
    ).astype(jnp.bfloat16)

    def exchange(rows):
        packed = jnp.dot(place, rows, preferred_element_type=jnp.float32).astype(jnp.bfloat16)
        packed = packed.reshape(devices, slot_rows, rows.shape[1])
        got = lax.all_to_all(packed, ("gx", "gy"), split_axis=0, concat_axis=0, tiled=True)
        return got.reshape(devices * slot_rows, rows.shape[1])

    flat_patches = exchange(picked)
    got_target = exchange(jnp.concatenate([target, jnp.ones((patch_count, 128), jnp.bfloat16)], 1))
    source = jnp.dot(flat_patches, weight, preferred_element_type=jnp.float32).astype(
        jnp.bfloat16
    )
    valid_rows = got_target[:, embed : embed + 1].astype(jnp.float32)
    results = trainer_step(
        source, got_target[:, :embed], valid_rows, w_in[0], b_in[0], w_out[0], b_out[0]
    )
    partial_value = contract_rows(flat_patches, results[0])
    share = lax.psum_scatter(partial_value, ("gx", "gy"), scatter_dimension=0, tiled=True)
    summed = lax.all_gather(share.astype(jnp.bfloat16), ("gx", "gy"), axis=0, tiled=True)
    summed = summed.reshape(PATCH, -1, embed).transpose(1, 0, 2).reshape(-1, embed)
    patch_gradient = summed.astype(jnp.float32)
    return (
        states[-1],
        patch_gradient,
        results[1][None],
        results[2][None],
        results[3][None],
        results[4][None],
    )


def solution(mesh):
    in_specs = (
        P(None, "gx", "gy", None),
        P(),
        P(("gx", "gy"), None),
        P("gx", "gy", None),
        P(("gx", "gy"), None, None),
        P(("gx", "gy"), None),
        P(("gx", "gy"), None, None),
        P(("gx", "gy"), None),
    )
    out_specs = (
        P(None, "gx", "gy", None),
        P(),
        P(("gx", "gy"), None, None),
        P(("gx", "gy"), None),
        P(("gx", "gy"), None, None),
        P(("gx", "gy"), None),
    )
    return jax.shard_map(
        per_device, mesh=mesh, in_specs=in_specs, out_specs=out_specs, check_vma=False
    )
```

profile of v0, /device:TPU:0, one launch (start us, length us, event | category | flops | bytes accessed | tf_op | source)
XLA Modules:
  0.0 406.8 jit_solution(12653624537642688695)
XLA Ops:
  7.2 1.2 fusion.68
  8.4 2.4 collective-permute-start
  10.8 1.3 collective-permute-start.1
  12.1 0.7 fusion.62
  12.9 0.8 select_reduce_fusion
  13.8 1.8 constant_dynamic-update-slice_fusion
  15.6 0.5 collective-permute-done.1
  16.3 1.3 collective-permute-start.3
  17.6 4.6 %collective-permute-start.2 = (f32[5,20,2,128]{3,2,1,0:T(2,128)S(1)}, f32[5,20,2,128]{3,2,1,0:T(2,128)S(1)}, u32[]{:S(2)}, u32[]{:S(2)}) collective-permute-start(f32[5,20,2,128]{3,2,1,0:T(2,128)S(1)} %get-tuple-element.26), channel_id=1, source_target_pairs={{0,1},{1,2},{2,3},{4,5},{5,6},{6,7},{8,9},{9,10},{10,11},{12,13},{... | collective-permute-start | bytes 307208 | tf_op jit(solution)/shard_map/ppermute | solution.py:31
  22.5 0.3 collective-permute-done.3
  22.8 1.5 collective-permute-done.2
  24.4 1.6 select_maximum_fusion.8
  25.9 2.3 broadcast_multiply_fusion.2
  28.5 1.2 copy-done.2
  29.6 3.3 fusion.28
  32.9 0.8 fusion.67
  33.7 1.3 collective-permute-start.5
  34.9 5.9 %collective-permute-start.4 = (f32[5,2,32,128]{3,2,1,0:T(8,128)}, f32[5,2,32,128]{3,2,1,0:T(8,128)}, u32[]{:S(2)}, u32[]{:S(2)}) collective-permute-start(f32[5,2,32,128]{3,2,1,0:T(8,128)} %get-tuple-element.30), channel_id=1, source_target_pairs={{0,4},{4,8},{8,12},{12,16},{16,20},{20,24},{24,28},{1,5},{5,9},{9,... | collective-permute-start | bytes 491528 | tf_op jit(solution)/shard_map/ppermute | solution.py:31
  41.1 4.1 %copy.24 = bf16[8,320,512]{2,1,0:T(8,128)(2,1)} copy(bf16[8,320,512]{2,0,1:T(8,128)(2,1)} %bitcast.88) | data formatting | bytes 5242880 | tf_op jit(solution)/shard_map/transpose | solution.py:161
  45.2 0.9 pad_maximum_fusion.13
  46.1 1.3 collective-permute-start.7
  47.4 4.8 %collective-permute-start.6 = (f32[5,20,2,128]{3,2,1,0:T(2,128)S(1)}, f32[5,20,2,128]{3,2,1,0:T(2,128)S(1)}, u32[]{:S(2)}, u32[]{:S(2)}) collective-permute-start(f32[5,20,2,128]{3,2,1,0:T(2,128)S(1)} %get-tuple-element.24), channel_id=1, source_target_pairs={{0,1},{1,2},{2,3},{4,5},{5,6},{6,7},{8,9},{9,10},{10,11},{12,13},{... | collective-permute-start | bytes 307208 | tf_op jit(solution)/shard_map/ppermute | solution.py:31
  52.3 1.3 fusion.56
  53.6 0.9 collective-permute-done.6
  54.5 4.4 %select_maximum_fusion.4 = f32[5,20,36,132]{3,2,1,0:T(8,128)S(1)} fusion(f32[5,20,2,128]{3,2,1,0:T(2,128)S(1)} %collective-permute-done.7, f32[5,20,2,128]{3,2,1,0:T(2,128)S(1)} %collective-permute-done.6, f32[5,2,32,128]{3,2,1,0:T(8,128)} %collective-permute-done.5, f32[5,16,32,128]{3,2,1,0:T(8,128)S(1)} %fusion.28, f32[5,2,32,128]{3,2,1,0:T(8,128)} %collective-permute-done.4), kind=kLoop, calls=%fused_computation.8 | loop fusion | flops 5702400 | bytes 3744000 | tf_op jit(solution)/shard_map/concatenate | solution.py:29
  58.9 1.1 broadcast_multiply_fusion
  60.0 1.6 maximum_maximum_fusion
  61.6 0.5 broadcast_multiply_fusion.1
  62.3 4.2 %fusion.25 = f32[5,16,32,128]{3,2,1,0:T(8,128)S(1)} fusion(f32[5,16,32,128]{3,2,1,0:T(8,128)S(1)} %fusion.28, f32[5,16,32,128]{3,2,1,0:T(8,128)S(1)} %constant_dynamic-update-slice_fusion.9, f32[5,16,32,128]{3,2,1,0:T(8,128)S(1)} %get-tuple-element.13, f32[5,16,32,128]{3,2,1,0:T(8,128)S(1)} %get-tuple-element.11, ...), kind=kLoop, calls=%fused_computation.72 | loop fusion | flops 14090240 | bytes 17367040 | tf_op jit(solution)/shard_map/add | solution.py:151
  66.6 1.3 collective-permute-start.9
  67.9 3.5 collective-permute-start.8
  71.4 1.0 collective-permute-done.8
  72.5 1.3 collective-permute-start.11
  73.8 4.9 %collective-permute-start.10 = (f32[5,20,2,128]{3,2,1,0:T(2,128)S(1)}, f32[5,20,2,128]{3,2,1,0:T(2,128)S(1)}, u32[]{:S(2)}, u32[]{:S(2)}) collective-permute-start(f32[5,20,2,128]{3,2,1,0:T(2,128)S(1)} %get-tuple-element.20), channel_id=1, source_target_pairs={{0,1},{1,2},{2,3},{4,5},{5,6},{6,7},{8,9},{9,10},{10,11},{12,13},{... | collective-permute-start | bytes 307208 | tf_op jit(solution)/shard_map/ppermute | solution.py:31
  79.2 1.5 collective-permute-done.10
  80.7 3.5 select_maximum_fusion
  84.3 1.1 broadcast_multiply_fusion.5
  85.3 0.4 maximum_maximum_fusion.1
  85.7 0.5 broadcast_multiply_fusion.4
  86.5 3.1 fusion.22
  89.6 1.3 copy.25
  91.1 6.0 %shard_map.128 = bf16[128,2560]{1,0:T(8,128)(2,1)} custom-call(f32[8,320,128]{2,1,0:T(8,128)} %bitcast.87), custom_call_target="tpu_custom_call" | custom-call | flops 2621440 | bytes 1966080 | tf_op jit(solution)/shard_map/pallas_call | solution.py:121
  97.1 2.5 convolution_convert_fusion.2
  99.6 0.9 fusion.53
  100.6 13.7 %all-to-all-start.1 = ((bf16[32,8,640]{2,1,0:T(8,128)(2,1)}), bf16[32,8,640]{2,1,0:T(8,128)(2,1)}, u32[]{:S(2)}, u32[]{:S(2)}) async-start(bf16[32,8,640]{2,1,0:T(8,128)(2,1)} %fusion.53), calls=%async_computation.1 | async-start | bytes 655360 | tf_op jit(solution)/shard_map/all_to_all | solution.py:183
  114.5 2.6 copy_select_fusion
  117.1 6.0 %shard_map.127 = bf16[128,2560]{1,0:T(8,128)(2,1)} custom-call(f32[8,320,128]{2,1,0:T(8,128)} %bitcast.86), custom_call_target="tpu_custom_call" | custom-call | flops 2621440 | bytes 1966080 | tf_op jit(solution)/shard_map/pallas_call | solution.py:121
  123.1 2.6 fusion.1
  125.8 5.8 %all-to-all-start = ((bf16[32,8,2560]{2,1,0:T(8,128)(2,1)}), bf16[32,8,2560]{2,1,0:T(8,128)(2,1)S(1)}, u32[]{:S(2)}, u32[]{:S(2)}) async-start(bf16[32,8,2560]{2,1,0:T(8,128)(2,1)} %fusion.1), calls=%async_computation | async-start | bytes 2621440 | tf_op jit(solution)/shard_map/all_to_all | solution.py:183
  131.9 1.0 multiply_reduce_fusion
  132.8 29.1 %all-to-all-done = bf16[32,8,2560]{2,1,0:T(8,128)(2,1)S(1)} async-done(((bf16[32,8,2560]{2,1,0:T(8,128)(2,1)}), bf16[32,8,2560]{2,1,0:T(8,128)(2,1)S(1)}, u32[]{:S(2)}, u32[]{:S(2)}) %all-to-all-start) | async-done | bytes 1310752 | tf_op jit(solution)/shard_map/all_to_all | solution.py:183
  161.9 2.6 fusion.44
  164.5 0.7 convolution_add_fusion
  165.3 0.9 copy-done.12
  166.2 2.3 convert_reduce_fusion.1
  168.5 2.7 convert_reduce_fusion
  171.2 5.2 %fusion.16 = f32[2560,512]{1,0:T(8,128)} fusion(bf16[32,8,2560]{2,1,0:T(8,128)(2,1)S(1)} %all-to-all-done, bf16[256,2048]{1,0:T(8,128)(2,1)} %get-tuple-element.42, bf16[1,512,2048]{2,1,0:T(8,128)(2,1)S(1)} %copy-done), kind=kOutput, calls=%fused_computation.60 | convolution fusion | flops 1208090624 | bytes 9699328 | tf_op jit(solution)/shard_map/dot_general | solution.py:71
  176.4 155.4 %reduce-scatter.2.cloned.1.call-done = f32[80,512]{1,0:T(8,128)} async-done(((f32[2560,512]{1,0:T(8,128)}), f32[80,512]{1,0:T(8,128)}) %reduce-scatter.2.cloned.1.call-update) | async-done | bytes 163856 | tf_op jit(solution)/shard_map/reduce_scatter | solution.py:196
  331.8 1.6 convert_element_type.70
  333.4 2.7 convolution_bitcast_fusion.1
  336.2 2.8 convolution_bitcast_fusion
  339.0 53.0 %all-gather.2.cloned.1.call-done = bf16[2560,512]{1,0:T(8,128)(2,1)} async-done(((bf16[80,512]{1,0:T(8,128)(2,1)}), bf16[2560,512]{1,0:T(8,128)(2,1)}) %all-gather.2.cloned.1.call-update) | async-done | bytes 2621456 | tf_op jit(solution)/shard_map/all_gather | solution.py:197
  392.0 2.5 convert_bitcast_fusion
  394.5 5.4 %copy.30 = f32[320,8,512]{2,1,0:T(8,128)} copy(f32[320,8,512]{2,0,1:T(8,128)S(1)} %convert_bitcast_fusion) | data formatting | bytes 10485760 | tf_op jit(solution)/shard_map/convert_element_type | solution.py:199
  (71 shorter events, 2.7 us)
Async XLA Ops:
  7.2 157.3 %copy-start = (bf16[1,512,2048]{2,1,0:T(8,128)(2,1)S(1)}, bf16[1,512,2048]{2,1,0:T(8,128)(2,1)}, u32[]{:S(2)}) copy-start(bf16[1,512,2048]{2,1,0:T(8,128)(2,1)} %param.12) | copy-start | bytes 6291460
  8.4 5.4 %collective-permute-start = (f32[5,2,32,128]{3,2,1,0:T(8,128)S(1)}, f32[5,2,32,128]{3,2,1,0:T(8,128)S(1)}, u32[]{:S(2)}, u32[]{:S(2)}) collective-permute-start(f32[5,2,32,128]{3,2,1,0:T(8,128)S(1)} %get-tuple-element.36), channel_id=1, source_target_pairs={{0,4},{4,8},{8,12},{12,16},{16,20},{20,24},{24,28},{1,5},{5,9},{9,... | collective-permute-start | bytes 491528 | tf_op jit(solution)/shard_map/ppermute | solution.py:31
  10.8 5.4 %collective-permute-start.1 = (f32[5,2,32,128]{3,2,1,0:T(8,128)S(1)}, f32[5,2,32,128]{3,2,1,0:T(8,128)S(1)}, u32[]{:S(2)}, u32[]{:S(2)}) collective-permute-start(f32[5,2,32,128]{3,2,1,0:T(8,128)S(1)} %get-tuple-element.35), channel_id=1, source_target_pairs={{4,0},{8,4},{12,8},{16,12},{20,16},{24,20},{28,24},{5,1},{9,5},{13... | collective-permute-start | bytes 491528 | tf_op jit(solution)/shard_map/ppermute | solution.py:33
  16.3 6.6 %collective-permute-start.3 = (f32[5,20,2,128]{3,2,1,0:T(2,128)S(1)}, f32[5,20,2,128]{3,2,1,0:T(2,128)S(1)}, u32[]{:S(2)}, u32[]{:S(2)}) collective-permute-start(f32[5,20,2,128]{3,2,1,0:T(2,128)S(1)} %get-tuple-element.27), channel_id=1, source_target_pairs={{1,0},{2,1},{3,2},{5,4},{6,5},{7,6},{9,8},{10,9},{11,10},{13,12},{... | collective-permute-start | bytes 307208 | tf_op jit(solution)/shard_map/ppermute | solution.py:33
  17.6 6.8 %collective-permute-start.2 = (f32[5,20,2,128]{3,2,1,0:T(2,128)S(1)}, f32[5,20,2,128]{3,2,1,0:T(2,128)S(1)}, u32[]{:S(2)}, u32[]{:S(2)}) collective-permute-start(f32[5,20,2,128]{3,2,1,0:T(2,128)S(1)} %get-tuple-element.26), channel_id=1, source_target_pairs={{0,1},{1,2},{2,3},{4,5},{5,6},{6,7},{8,9},{9,10},{10,11},{12,13},{... | collective-permute-start | bytes 307208 | tf_op jit(solution)/shard_map/ppermute | solution.py:31
  28.3 1.3 copy-start.2
  29.6 11.2 %copy-start.11 = (s32[64,1]{0,1:T(1,128)S(1)}, s32[64,1]{0,1:T(1,128)}, u32[]{:S(2)}) copy-start(s32[64,1]{0,1:T(1,128)} %param.10) | copy-start | bytes 772
  33.7 11.6 %collective-permute-start.5 = (f32[5,2,32,128]{3,2,1,0:T(8,128)}, f32[5,2,32,128]{3,2,1,0:T(8,128)}, u32[]{:S(2)}, u32[]{:S(2)}) collective-permute-start(f32[5,2,32,128]{3,2,1,0:T(8,128)} %get-tuple-element.31), channel_id=1, source_target_pairs={{4,0},{8,4},{12,8},{16,12},{20,16},{24,20},{28,24},{5,1},{9,5},{13... | collective-permute-start | bytes 491528 | tf_op jit(solution)/shard_map/ppermute | solution.py:33
  34.9 10.3 %collective-permute-start.4 = (f32[5,2,32,128]{3,2,1,0:T(8,128)}, f32[5,2,32,128]{3,2,1,0:T(8,128)}, u32[]{:S(2)}, u32[]{:S(2)}) collective-permute-start(f32[5,2,32,128]{3,2,1,0:T(8,128)} %get-tuple-element.30), channel_id=1, source_target_pairs={{0,4},{4,8},{8,12},{12,16},{16,20},{20,24},{24,28},{1,5},{5,9},{9,... | collective-permute-start | bytes 491528 | tf_op jit(solution)/shard_map/ppermute | solution.py:31
  46.1 7.5 %collective-permute-start.7 = (f32[5,20,2,128]{3,2,1,0:T(2,128)S(1)}, f32[5,20,2,128]{3,2,1,0:T(2,128)S(1)}, u32[]{:S(2)}, u32[]{:S(2)}) collective-permute-start(f32[5,20,2,128]{3,2,1,0:T(2,128)S(1)} %get-tuple-element.25), channel_id=1, source_target_pairs={{1,0},{2,1},{3,2},{5,4},{6,5},{7,6},{9,8},{10,9},{11,10},{13,12},{... | collective-permute-start | bytes 307208 | tf_op jit(solution)/shard_map/ppermute | solution.py:33
  47.4 7.1 %collective-permute-start.6 = (f32[5,20,2,128]{3,2,1,0:T(2,128)S(1)}, f32[5,20,2,128]{3,2,1,0:T(2,128)S(1)}, u32[]{:S(2)}, u32[]{:S(2)}) collective-permute-start(f32[5,20,2,128]{3,2,1,0:T(2,128)S(1)} %get-tuple-element.24), channel_id=1, source_target_pairs={{0,1},{1,2},{2,3},{4,5},{5,6},{6,7},{8,9},{9,10},{10,11},{12,13},{... | collective-permute-start | bytes 307208 | tf_op jit(solution)/shard_map/ppermute | solution.py:31
  66.6 19.9 %copy-start.1 = (f32[5,16,32,128]{3,2,1,0:T(8,128)}, f32[5,16,32,128]{3,2,1,0:T(8,128)S(1)}, u32[]{:S(2)}) copy-start(f32[5,16,32,128]{3,2,1,0:T(8,128)S(1)} %fusion.25) | copy-start | bytes 3932164
  66.6 4.8 %collective-permute-start.9 = (f32[5,2,32,128]{3,2,1,0:T(8,128)S(1)}, f32[5,2,32,128]{3,2,1,0:T(8,128)S(1)}, u32[]{:S(2)}, u32[]{:S(2)}) collective-permute-start(f32[5,2,32,128]{3,2,1,0:T(8,128)S(1)} %get-tuple-element.29), channel_id=1, source_target_pairs={{4,0},{8,4},{12,8},{16,12},{20,16},{24,20},{28,24},{5,1},{9,5},{13... | collective-permute-start | bytes 491528 | tf_op jit(solution)/shard_map/ppermute | solution.py:33
  67.9 4.5 %collective-permute-start.8 = (f32[5,2,32,128]{3,2,1,0:T(8,128)S(1)}, f32[5,2,32,128]{3,2,1,0:T(8,128)S(1)}, u32[]{:S(2)}, u32[]{:S(2)}) collective-permute-start(f32[5,2,32,128]{3,2,1,0:T(8,128)S(1)} %get-tuple-element.28), channel_id=1, source_target_pairs={{0,4},{4,8},{8,12},{12,16},{16,20},{20,24},{24,28},{1,5},{5,9},{9,... | collective-permute-start | bytes 491528 | tf_op jit(solution)/shard_map/ppermute | solution.py:31
  72.5 6.7 %collective-permute-start.11 = (f32[5,20,2,128]{3,2,1,0:T(2,128)S(1)}, f32[5,20,2,128]{3,2,1,0:T(2,128)S(1)}, u32[]{:S(2)}, u32[]{:S(2)}) collective-permute-start(f32[5,20,2,128]{3,2,1,0:T(2,128)S(1)} %get-tuple-element.21), channel_id=1, source_target_pairs={{1,0},{2,1},{3,2},{5,4},{6,5},{7,6},{9,8},{10,9},{11,10},{13,12},{... | collective-permute-start | bytes 307208 | tf_op jit(solution)/shard_map/ppermute | solution.py:33
  73.8 7.0 %collective-permute-start.10 = (f32[5,20,2,128]{3,2,1,0:T(2,128)S(1)}, f32[5,20,2,128]{3,2,1,0:T(2,128)S(1)}, u32[]{:S(2)}, u32[]{:S(2)}) collective-permute-start(f32[5,20,2,128]{3,2,1,0:T(2,128)S(1)} %get-tuple-element.20), channel_id=1, source_target_pairs={{0,1},{1,2},{2,3},{4,5},{5,6},{6,7},{8,9},{9,10},{10,11},{12,13},{... | collective-permute-start | bytes 307208 | tf_op jit(solution)/shard_map/ppermute | solution.py:31
  89.6 1.5 copy-start.3
  97.1 17.2 %copy-start.10 = (s32[2,4,16]{2,1,0:T(4,128)S(1)}, s32[2,4,16]{2,1,0:T(4,128)}, u32[]{:S(2)}) copy-start(s32[2,4,16]{2,1,0:T(4,128)} %param.11) | copy-start | bytes 1540
  100.6 25.2 %all-to-all-start.1 = ((bf16[32,8,640]{2,1,0:T(8,128)(2,1)}), bf16[32,8,640]{2,1,0:T(8,128)(2,1)}, u32[]{:S(2)}, u32[]{:S(2)}) async-start(bf16[32,8,640]{2,1,0:T(8,128)(2,1)} %fusion.53), calls=%async_computation.1 | async-start | bytes 655360 | tf_op jit(solution)/shard_map/all_to_all | solution.py:183
  125.8 36.1 %all-to-all-start = ((bf16[32,8,2560]{2,1,0:T(8,128)(2,1)}), bf16[32,8,2560]{2,1,0:T(8,128)(2,1)S(1)}, u32[]{:S(2)}, u32[]{:S(2)}) async-start(bf16[32,8,2560]{2,1,0:T(8,128)(2,1)} %fusion.1), calls=%async_computation | async-start | bytes 2621440 | tf_op jit(solution)/shard_map/all_to_all | solution.py:183
  131.5 200.2 %reduce-scatter.2.cloned.1.call-start = ((), (), s32[]{:S(2)}) async-start(), calls=%async_computation.3 | async-start | bytes 5406720 | tf_op jit(solution)/shard_map/reduce_scatter | solution.py:196
  132.8 31.7 %copy-start.9 = (f32[1,2048]{1,0:T(1,128)S(1)}, f32[1,2048]{1,0:T(1,128)}, u32[]{:S(2)}) copy-start(f32[1,2048]{1,0:T(1,128)} %param.13) | copy-start | bytes 24580
  164.5 0.8 copy-start.7
  164.5 1.7 copy-start.12
  164.5 1.7 copy-start.13
  165.3 3.2 copy-start.5
  168.5 2.7 copy-start.14
  176.3 157.0 %copy-start.4 = (bf16[256,2048]{1,0:T(8,128)(2,1)S(1)}, bf16[256,2048]{1,0:T(8,128)(2,1)}, u32[]{:S(2)}) copy-start(bf16[256,2048]{1,0:T(8,128)(2,1)} %get-tuple-element.42) | copy-start | bytes 3145732
  176.3 157.0 %copy-start.8 = (bf16[256,512]{1,0:T(8,128)(2,1)S(1)}, bf16[256,512]{1,0:T(8,128)(2,1)}, u32[]{:S(2)}) copy-start(bf16[256,512]{1,0:T(8,128)(2,1)} %copy-done.7) | copy-start | bytes 786436
  176.4 215.7 %all-gather.2.cloned.1.call-start = ((), (), s32[]{:S(2)}) async-start(), calls=%async_computation.4 | async-start | bytes 2703360 | tf_op jit(solution)/shard_map/all_gather | solution.py:197
  333.4 2.8 copy-start.6
  333.4 2.8 copy-start.15
Sparse Core Ops, SparseCore 0:
  176.5 155.2 reduce-scatter.1
  335.2 56.8 all-gather.1
where the time goes:
time: 408 us; the launch traced here: 407 us
  waiting for transfers between devices  244 us (60%)
  starting transfers between devices  53.7 us (13%)
  other arithmetic  40 us (10%)
  matrix products  25 us (6%)
  local copies, waits for them, and re-layouts  17.6 us (4%)
  between operations  14.7 us (4%)
  Pallas kernels  12.1 us (3%)
    reduce_scatter x1, waiting for transfers between devices, per_device(): lax.psum_scatter(partial_value, ('gx', 'gy'), scatter_dimension=0, tiled=...  155 us
    all_gather x1, waiting for transfers between devices, per_device(): lax.all_gather(share.astype(jnp.bfloat16), ('gx', 'gy'), axis=0, tiled=True)  53 us
    all_to_all x2, waiting for transfers between devices, exchange(): lax.all_to_all(packed, ('gx', 'gy'), split_axis=0, concat_axis=0, tiled=T...  29.1 us
    ppermute x6, starting transfers between devices, with_halo(): lax.ppermute(tail, axis, [(i, (i + 1) % count) for i in range(ends)])  26.1 us
    all_to_all x2, starting transfers between devices, exchange(): lax.all_to_all(packed, ('gx', 'gy'), split_axis=0, concat_axis=0, tiled=T...  19.5 us
    pallas_call x2, Pallas kernels, patchify(): pl.pallas_call(patch_kernel, grid=(columns,), out_shape=jax.ShapeDtypeStr...  12.1 us
    concatenate x5, other arithmetic, with_halo(): jnp.concatenate([lax.ppermute(tail, axis, [(i, (i + 1) % count) for i in...  11.4 us
    dot_general x3, matrix products, contract_rows(): lax.dot_general(left, right, (((0,), (0,)), ((), ())), preferred_element_...  10.7 us
  transfers between devices with their start and end apart: 16, of which 10 were waited for; matrix products, arithmetic and copies ran while one was open for 5% of the time, Pallas kernels for 1%

commit v1 on v0

--- a/solution.py
+++ b/solution.py
@@ -1,3 +1,5 @@
+import functools
+
 import jax
 import jax.numpy as jnp
 from jax import lax
@@ -153,18 +155,249 @@
     return states
 
 
+def my_place():
+    return lax.axis_index("gx"), lax.axis_index("gy")
+
+
+def remote(src, dst, send_sem, recv_sem, gx, gy):
+    return pltpu.make_async_remote_copy(
+        src_ref=src,
+        dst_ref=dst,
+        send_sem=send_sem,
+        recv_sem=recv_sem,
+        device_id=(gx, gy),
+        device_id_type=pl.DeviceIdType.MESH,
+    )
+
+
+def greet_all(gx_n, gy_n):
+    gx, gy = my_place()
+    me = gx * gy_n + gy
+    devices = gx_n * gy_n
+    barrier = pltpu.get_barrier_semaphore()
+
+    def greet(step, carry):
+        other = lax.rem(me + step, devices)
+        pl.semaphore_signal(
+            barrier,
+            inc=1,
+            device_id=(other // gy_n, lax.rem(other, gy_n)),
+            device_id_type=pl.DeviceIdType.MESH,
+        )
+        return carry
+
+    lax.fori_loop(1, devices, greet, 0)
+    pl.semaphore_wait(barrier, devices - 1)
+
+
+def gradient_kernel(
+    gx_n,
+    gy_n,
+    grad_ref,
+    unplace_ref,
+    feat_ref,
+    out_ref,
+    back,
+    feats,
+    shared,
+    parts,
+    landed,
+    back_send,
+    back_recv,
+    feat_send,
+    feat_recv,
+    share_send,
+    share_recv,
+    part_send,
+    part_recv,
+    line_send,
+    plane_send,
+    pair_send,
+    out_recv,
+):
+    gx, gy = my_place()
+    me = gx * gy_n + gy
+    devices = gx_n * gy_n
+    chips = gx_n // 2
+    chip, core = gx // 2, lax.rem(gx, 2)
+    partner = gx + 1 - 2 * core
+    rows, embed = shared.shape[1], shared.shape[2]
+
+    def chip_at(step):
+        return lax.rem(chip + step, chips) * 2 + core
+
+    greet_all(gx_n, gy_n)
+
+    def back_copy(step):
+        other = lax.rem(me + step, devices)
+        return remote(
+            grad_ref.at[other],
+            back.at[me],
+            back_send.at[step],
+            back_recv.at[step],
+            other // gy_n,
+            lax.rem(other, gy_n),
+        )
+
+    def start_back(step, carry):
+        back_copy(step).start()
+        return carry
+
+    lax.fori_loop(1, devices, start_back, 0)
+
+    def feat_copy(step):
+        other = lax.rem(gx + step, gx_n)
+        return remote(
+            feat_ref.at[other], feats.at[gx], feat_send.at[step], feat_recv.at[step], other, gy
+        )
+
+    for step in range(1, gx_n):
+        feat_copy(step).start()
+    feats[gx] = feat_ref[gx]
+    back[me] = grad_ref[me]
+
+    def wait_back(step, carry):
+        back_copy(step).wait()
+        return carry
+
+    lax.fori_loop(1, devices, wait_back, 0)
+    packed = back[...].astype(jnp.float32).reshape(-1, embed).astype(jnp.bfloat16)
+    mine = jnp.dot(unplace_ref[...], packed, preferred_element_type=jnp.float32)
+    shared[gx] = mine.astype(jnp.bfloat16)
+
+    def share_copy(origin, target, slot):
+        return remote(
+            shared.at[origin], shared.at[origin], share_send.at[slot], share_recv.at[origin], target, gy
+        )
+
+    share_sends = []
+    for step in range(1, chips):
+        copy = share_copy(gx, chip_at(step), step)
+        copy.start()
+        share_sends.append(copy)
+    copy = share_copy(gx, partner, 0)
+    copy.start()
+    share_sends.append(copy)
+    for step in range(1, chips):
+        origin = chip_at(chips - step)
+        share_copy(origin, partner, chips + step).wait_recv()
+        copy = share_copy(origin, partner, chips + step)
+        copy.start()
+        share_sends.append(copy)
+    for step in range(chips):
+        share_copy(chip_at(step) + 1 - 2 * core, partner, 0).wait_recv()
+    for step in range(1, gx_n):
+        feat_copy(step).wait()
+
+    def part_of(block):
+        total = jnp.zeros((parts.shape[1], embed), jnp.float32)
+        for origin in range(gx_n):
+            total = total + jnp.dot(
+                feats[origin, block], shared[origin], preferred_element_type=jnp.float32
+            )
+        return total
+
+    def part_copy(step):
+        other = lax.rem(gy + step, gy_n)
+        return remote(
+            parts.at[other], landed.at[step], part_send.at[step], part_recv.at[step], gx, other
+        )
+
+    for step in range(1, gy_n):
+        other = lax.rem(gy + step, gy_n)
+        parts[other] = part_of(other).astype(jnp.bfloat16)
+        part_copy(step).start()
+    total = part_of(gy)
+    for step in range(1, gy_n):
+        part_copy(step).wait()
+        total = total + landed[step].astype(jnp.float32)
+    out_ref[gx, gy] = total.astype(jnp.bfloat16)
+
+    def out_copy(block_x, block_y, send_sem, target_x, target_y):
+        block = out_ref.at[block_x, block_y]
+        return remote(block, block, send_sem, out_recv.at[block_x, block_y], target_x, target_y)
+
+    sends = []
+
+    def send(*args):
+        copy = out_copy(*args)
+        copy.start()
+        sends.append(copy)
+
+    for step in range(1, gy_n):
+        send(gx, gy, line_send.at[step], gx, lax.rem(gy + step, gy_n))
+    for line in range(gy_n):
+        block_y = lax.rem(gy + line, gy_n)
+        if line > 0:
+            out_copy(gx, block_y, line_send.at[0], gx, block_y).wait_recv()
+        for step in range(1, chips):
+            send(gx, block_y, plane_send.at[line, step], chip_at(step), gy)
+        send(gx, block_y, pair_send.at[line, 0], partner, gy)
+    for line in range(gy_n):
+        block_y = lax.rem(gy + line, gy_n)
+        for step in range(1, chips):
+            block_x = chip_at(step)
+            out_copy(block_x, block_y, line_send.at[0], partner, gy).wait_recv()
+            send(block_x, block_y, pair_send.at[line, step], partner, gy)
+    for line in range(gy_n):
+        for step in range(chips):
+            block_x = chip_at(step) + 1 - 2 * core
+            out_copy(block_x, line, line_send.at[0], partner, gy).wait_recv()
+    for copy in share_sends + sends:
+        copy.wait_send()
+
+
+def patch_gradient_sum(grad_slots, unplace, feat):
+    gx_n, gy_n = lax.axis_size("gx"), lax.axis_size("gy")
+    devices, slot_rows, embed = grad_slots.shape
+    rows = unplace.shape[0]
+    part_rows = feat.shape[2]
+    chips = gx_n // 2
+    bf16 = jnp.bfloat16
+    dma = pltpu.SemaphoreType.DMA
+    whole = pl.BlockSpec(memory_space=pltpu.VMEM)
+    return pl.pallas_call(
+        functools.partial(gradient_kernel, gx_n, gy_n),
+        out_shape=jax.ShapeDtypeStruct((gx_n, gy_n, part_rows, embed), bf16),
+        in_specs=[whole] * 3,
+        out_specs=whole,
+        scratch_shapes=[
+            pltpu.VMEM((devices, slot_rows, embed), bf16),
+            pltpu.VMEM(feat.shape, bf16),
+            pltpu.VMEM((gx_n, rows, embed), bf16),
+            pltpu.VMEM((gy_n, part_rows, embed), bf16),
+            pltpu.VMEM((gy_n, part_rows, embed), bf16),
+            dma((devices,)),
+            dma((devices,)),
+            dma((gx_n,)),
+            dma((gx_n,)),
+            dma((2 * chips,)),
+            dma((gx_n,)),
+            dma((gy_n,)),
+            dma((gy_n,)),
+            dma((gy_n,)),
+            dma((gy_n, chips)),
+            dma((gy_n, chips)),
+            dma((gx_n, gy_n)),
+        ],
+        compiler_params=pltpu.CompilerParams(collective_id=1, has_side_effects=True),
+    )(grad_slots, unplace, feat)
+
+
 def per_device(fields, patch_weight, trainer_of, lag_index, w_in, b_in, w_out, b_out):
     states = advance(fields)
-    devices = lax.axis_size("gx") * lax.axis_size("gy")
+    gx_n, gy_n = lax.axis_size("gx"), lax.axis_size("gy")
+    devices = gx_n * gy_n
     picked = patchify(pick(states[0], states[1], lag_index))
     embed = patch_weight.shape[1]
     weight = patch_weight.reshape(-1, PATCH, embed).transpose(1, 0, 2).reshape(-1, embed)
+    source = jnp.dot(picked, weight, preferred_element_type=jnp.float32).astype(jnp.bfloat16)
     target = jnp.dot(
         patchify(states[-1]), weight, preferred_element_type=jnp.float32
     ).astype(jnp.bfloat16)
     patch_count = picked.shape[0]
     block_count = patch_count // BLOCK_ROWS
-    slot_count = max(2, 2 * block_count // devices)
+    slot_count = max(8 // BLOCK_ROWS, 2 * block_count // devices)
     owners = trainer_of[:, 0]
     onehot = (owners[:, None] == jnp.arange(devices, dtype=jnp.int32)[None, :]).astype(jnp.int32)
     within_rank = jnp.sum((jnp.cumsum(onehot, axis=0) - onehot) * onehot, axis=1)
@@ -173,28 +406,23 @@
     patch_slot = jnp.repeat(block_slot, BLOCK_ROWS) * BLOCK_ROWS
     patch_slot = patch_slot + jnp.arange(patch_count, dtype=jnp.int32) % BLOCK_ROWS
     slot_rows = slot_count * BLOCK_ROWS
-    place = (
-        jnp.arange(devices * slot_rows, dtype=jnp.int32)[:, None] == patch_slot[None, :]
-    ).astype(jnp.bfloat16)
-
-    def exchange(rows):
-        packed = jnp.dot(place, rows, preferred_element_type=jnp.float32).astype(jnp.bfloat16)
-        packed = packed.reshape(devices, slot_rows, rows.shape[1])
-        got = lax.all_to_all(packed, ("gx", "gy"), split_axis=0, concat_axis=0, tiled=True)
-        return got.reshape(devices * slot_rows, rows.shape[1])
-
-    flat_patches = exchange(picked)
-    got_target = exchange(jnp.concatenate([target, jnp.ones((patch_count, 128), jnp.bfloat16)], 1))
-    source = jnp.dot(flat_patches, weight, preferred_element_type=jnp.float32).astype(
-        jnp.bfloat16
-    )
-    valid_rows = got_target[:, embed : embed + 1].astype(jnp.float32)
+    slots = jnp.arange(devices * slot_rows, dtype=jnp.int32)
+    place = (slots[:, None] == patch_slot[None, :]).astype(jnp.bfloat16)
+    unplace = (patch_slot[:, None] == slots[None, :]).astype(jnp.bfloat16)
+
+    rows = jnp.concatenate([source, target, jnp.ones((patch_count, 128), jnp.bfloat16)], 1)
+    packed = jnp.dot(place, rows, preferred_element_type=jnp.float32).astype(jnp.bfloat16)
+    packed = packed.reshape(devices, slot_rows, rows.shape[1])
+    got = lax.all_to_all(packed, ("gx", "gy"), split_axis=0, concat_axis=0, tiled=True)
+    got = got.reshape(devices * slot_rows, rows.shape[1])
+    valid_rows = got[:, 2 * embed : 2 * embed + 1].astype(jnp.float32)
     results = trainer_step(
-        source, got_target[:, :embed], valid_rows, w_in[0], b_in[0], w_out[0], b_out[0]
-    )
-    partial_value = contract_rows(flat_patches, results[0])
-    share = lax.psum_scatter(partial_value, ("gx", "gy"), scatter_dimension=0, tiled=True)
-    summed = lax.all_gather(share.astype(jnp.bfloat16), ("gx", "gy"), axis=0, tiled=True)
+        got[:, :embed], got[:, embed : 2 * embed], valid_rows, w_in[0], b_in[0], w_out[0], b_out[0]
+    )
+    feat = picked.T.reshape(gx_n, gy_n, -1, patch_count)
+    summed = patch_gradient_sum(
+        results[0].reshape(devices, slot_rows, embed), unplace, feat
+    )
     summed = summed.reshape(PATCH, -1, embed).transpose(1, 0, 2).reshape(-1, embed)
     patch_gradient = summed.astype(jnp.float32)
     return (

time: 408 us -> 208 us (0.51)
  waiting for transfers between devices: 244 us -> 18.9 us
  Pallas kernels: 12.1 us -> 68.5 us
  between operations: 14.7 us -> 1.23 us
  starting transfers between devices: 53.7 us -> 46.2 us
  matrix products: 25 us -> 18.5 us
  other arithmetic: 40 us -> 35.7 us
    reduce_scatter x1 -> x0, waiting for transfers between devices: 155 us -> none  [per_device(): lax.psum_scatter(partial_value, ('gx', 'gy'), scatter_dimension=0, tiled=...]
    pallas_call x0 -> x1, Pallas kernels: none -> 56.4 us  [patch_gradient_sum(): pl.pallas_call(functools.partial(gradient_kernel, gx_n, gy_n), out_shape=...]
    all_gather x1 -> x0, waiting for transfers between devices: 53 us -> none  [per_device(): lax.all_gather(share.astype(jnp.bfloat16), ('gx', 'gy'), axis=0, tiled=True)]
    all_to_all x2 -> x1, waiting for transfers between devices: 29.1 us -> 13.5 us  [per_device(): lax.all_to_all(packed, ('gx', 'gy'), split_axis=0, concat_axis=0, tiled=T...]
    all_to_all x2 -> x1, starting transfers between devices: 19.5 us -> 10.6 us  [per_device(): lax.all_to_all(packed, ('gx', 'gy'), split_axis=0, concat_axis=0, tiled=T...]
    dot_general x3 -> x2, matrix products: 10.7 us -> 5.59 us  [contract_rows(): lax.dot_general(left, right, (((0,), (0,)), ((), ())), preferred_element_...]
  transfers between devices with their start and end apart: 16 -> 13, of which waited for: 10 -> 7; matrix products, arithmetic and copies ran while one was open for 5% -> 7% of each run, Pallas kernels for 1% -> 3%
where the time goes in v1:
time: 208 us; the launch traced here: 207 us
  Pallas kernels  68.5 us (33%)
  starting transfers between devices  46.2 us (22%)
  other arithmetic  35.7 us (17%)
  waiting for transfers between devices  18.9 us (9%)
  matrix products  18.5 us (9%)
  local copies, waits for them, and re-layouts  17.8 us (9%)
    pallas_call x1, Pallas kernels, patch_gradient_sum(): pl.pallas_call(functools.partial(gradient_kernel, gx_n, gy_n), out_shape=...  56.4 us
    ppermute x6, starting transfers between devices, with_halo(): lax.ppermute(tail, axis, [(i, (i + 1) % count) for i in range(ends)])  28 us
    all_to_all x1, waiting for transfers between devices, per_device(): lax.all_to_all(packed, ('gx', 'gy'), split_axis=0, concat_axis=0, tiled=T...  13.5 us
    pallas_call x2, Pallas kernels, patchify(): pl.pallas_call(patch_kernel, grid=(columns,), out_shape=jax.ShapeDtypeStr...  12.1 us
    concatenate x5, other arithmetic, with_halo(): jnp.concatenate([lax.ppermute(tail, axis, [(i, (i + 1) % count) for i in...  11.4 us
    add x3, other arithmetic, advance(): current = current + time_step * tendency(pad_third(padded))  10.7 us
    all_to_all x1, starting transfers between devices, per_device(): lax.all_to_all(packed, ('gx', 'gy'), split_axis=0, concat_axis=0, tiled=T...  10.6 us
    ppermute x6, starting transfers between devices, with_halo(): lax.ppermute(head, axis, [((i + 1) % count, i) for i in range(ends)])  7.73 us
  transfers between devices with their start and end apart: 13, of which 7 were waited for; matrix products, arithmetic and copies ran while one was open for 7% of the time, Pallas kernels for 3%

profile of v1, /device:TPU:0, one launch (start us, length us, event | category | flops | bytes accessed | tf_op | source)
XLA Modules:
  0.0 206.9 jit_solution(16539936649234201304)
XLA Ops:
  0.6 1.9 fusion.67
  2.5 3.1 %collective-permute-start = (f32[5,2,32,128]{3,2,1,0:T(8,128)}, f32[5,2,32,128]{3,2,1,0:T(8,128)}, u32[]{:S(2)}, u32[]{:S(2)}) collective-permute-start(f32[5,2,32,128]{3,2,1,0:T(8,128)} %get-tuple-element.36), channel_id=1, source_target_pairs={{0,4},{4,8},{8,12},{12,16},{16,20},{20,24},{24,28},{1,5},{5,9},{9,... | collective-permute-start | bytes 491528 | tf_op jit(solution)/shard_map/ppermute | solution.py:33
  5.6 1.3 collective-permute-start.1
  6.9 4.2 %copy.26 = bf16[8,320,512]{2,1,0:T(8,128)(2,1)} copy(bf16[8,320,512]{2,0,1:T(8,128)(2,1)} %bitcast.88) | data formatting | bytes 5242880 | tf_op jit(solution)/shard_map/transpose | solution.py:393
  11.5 0.2 select_reduce_fusion
  11.8 0.1 mul.294
  12.0 0.9 constant_dynamic-update-slice_fusion.1
  12.9 0.4 constant_dynamic-update-slice_fusion
  13.3 0.9 constant_dynamic-update-slice_fusion.2
  14.4 1.3 collective-permute-start.3
  15.7 4.9 %collective-permute-start.2 = (f32[5,20,2,128]{3,2,1,0:T(2,128)S(1)}, f32[5,20,2,128]{3,2,1,0:T(2,128)S(1)}, u32[]{:S(2)}, u32[]{:S(2)}) collective-permute-start(f32[5,20,2,128]{3,2,1,0:T(2,128)S(1)} %get-tuple-element.26), channel_id=1, source_target_pairs={{0,1},{1,2},{2,3},{4,5},{5,6},{6,7},{8,9},{9,10},{10,11},{12,13},{... | collective-permute-start | bytes 307208 | tf_op jit(solution)/shard_map/ppermute | solution.py:33
  20.6 0.3 broadcast_multiply_fusion.3
  21.0 0.3 collective-permute-done.3
  21.3 1.6 collective-permute-done.2
  22.9 1.6 select_maximum_fusion.8
  24.5 2.3 %broadcast_multiply_fusion.2 = (f32[5,16,32,128]{3,2,1,0:T(8,128)S(1)}, f32[5,16,32,128]{3,2,1,0:T(8,128)S(1)}, f32[5,16,32,128]{3,2,1,0:T(8,128)S(1)}) fusion(f32[5,20,36,132]{3,2,1,0:T(8,128)S(1)} %select_maximum_fusion.8, f32[5,20,2,128]{3,2,1,0:T(2,128)S(1)} %collective-permute-done.3, f32[5,20,32,128]{3,2,1,0:T(8,128)S(1)} %get-tuple-element.40, ...), kind=kLoop, calls=%fused_computation.104 | loop fusion | flops 5242880 | bytes 11018240 | tf_op jit(solution)/shard_map/div | solution.py:59
  27.0 3.3 %fusion.24 = f32[5,16,32,128]{3,2,1,0:T(8,128)S(1)} fusion(f32[5,16,32,128]{3,2,1,0:T(8,128)S(1)} %copy-done.1, f32[5,16,32,128]{3,2,1,0:T(8,128)S(1)} %constant_dynamic-update-slice_fusion.7, f32[5,16,32,128]{3,2,1,0:T(8,128)S(1)} %get-tuple-element.17, f32[5,16,32,128]{3,2,1,0:T(8,128)S(1)} %get-tuple-element.15, ...), kind=kLoop, calls=%fused_computation.72 | loop fusion | flops 14090240 | bytes 18882560 | tf_op jit(solution)/shard_map/add | solution.py:153
  30.4 1.3 collective-permute-start.5
  31.7 3.6 %collective-permute-start.4 = (f32[5,2,32,128]{3,2,1,0:T(8,128)S(1)}, f32[5,2,32,128]{3,2,1,0:T(8,128)S(1)}, u32[]{:S(2)}, u32[]{:S(2)}) collective-permute-start(f32[5,2,32,128]{3,2,1,0:T(8,128)S(1)} %get-tuple-element.30), channel_id=1, source_target_pairs={{0,4},{4,8},{8,12},{12,16},{16,20},{20,24},{24,28},{1,5},{5,9},{9,... | collective-permute-start | bytes 491528 | tf_op jit(solution)/shard_map/ppermute | solution.py:33
  35.3 1.0 collective-permute-done.4
  36.3 1.3 collective-permute-start.7
  37.6 4.9 %collective-permute-start.6 = (f32[5,20,2,128]{3,2,1,0:T(2,128)S(1)}, f32[5,20,2,128]{3,2,1,0:T(2,128)S(1)}, u32[]{:S(2)}, u32[]{:S(2)}) collective-permute-start(f32[5,20,2,128]{3,2,1,0:T(2,128)S(1)} %get-tuple-element.24), channel_id=1, source_target_pairs={{0,1},{1,2},{2,3},{4,5},{5,6},{6,7},{8,9},{9,10},{10,11},{12,13},{... | collective-permute-start | bytes 307208 | tf_op jit(solution)/shard_map/ppermute | solution.py:33
  42.6 0.2 fusion.49
  42.8 0.3 collective-permute-done.7
  43.1 1.5 collective-permute-done.6
  44.6 3.5 %select_maximum_fusion.4 = f32[5,20,36,132]{3,2,1,0:T(8,128)S(1)} fusion(f32[5,20,2,128]{3,2,1,0:T(2,128)S(1)} %collective-permute-done.7, f32[5,20,2,128]{3,2,1,0:T(2,128)S(1)} %collective-permute-done.6, f32[5,2,32,128]{3,2,1,0:T(8,128)S(1)} %collective-permute-done.5, f32[5,16,32,128]{3,2,1,0:T(8,128)S(1)} %fusion.24, ...), kind=kLoop, calls=%fused_computation.8 | loop fusion | flops 5702400 | bytes 3744000 | tf_op jit(solution)/shard_map/concatenate | solution.py:31
  48.1 1.1 broadcast_multiply_fusion
  49.2 0.4 maximum_maximum_fusion
  49.6 0.5 broadcast_multiply_fusion.1
  50.3 3.1 %fusion.21 = f32[5,16,32,128]{3,2,1,0:T(8,128)S(1)} fusion(f32[5,16,32,128]{3,2,1,0:T(8,128)S(1)} %fusion.24, f32[5,16,32,128]{3,2,1,0:T(8,128)S(1)} %constant_dynamic-update-slice_fusion.9, f32[5,16,32,128]{3,2,1,0:T(8,128)S(1)} %get-tuple-element.13, f32[5,16,32,128]{3,2,1,0:T(8,128)S(1)} %get-tuple-element.11, ...), kind=kLoop, calls=%fused_computation.68 | loop fusion | flops 14090240 | bytes 17367040 | tf_op jit(solution)/shard_map/add | solution.py:153
  53.5 0.8 fusion.65
  54.2 1.3 collective-permute-start.9
  55.5 6.6 %collective-permute-start.8 = (f32[5,2,32,128]{3,2,1,0:T(8,128)}, f32[5,2,32,128]{3,2,1,0:T(8,128)}, u32[]{:S(2)}, u32[]{:S(2)}) collective-permute-start(f32[5,2,32,128]{3,2,1,0:T(8,128)} %get-tuple-element.28), channel_id=1, source_target_pairs={{0,4},{4,8},{8,12},{12,16},{16,20},{20,24},{24,28},{1,5},{5,9},{9,... | collective-permute-start | bytes 491528 | tf_op jit(solution)/shard_map/ppermute | solution.py:33
  62.1 1.3 copy_select_fusion
  63.4 6.0 %shard_map.127 = bf16[128,2560]{1,0:T(8,128)(2,1)} custom-call(f32[8,320,128]{2,1,0:T(8,128)} %bitcast.81), custom_call_target="tpu_custom_call" | custom-call | flops 2621440 | bytes 1966080 | tf_op jit(solution)/shard_map/pallas_call | solution.py:123
  69.4 2.5 %convolution_convert_fusion.2 = bf16[128,512]{1,0:T(8,128)(2,1)S(1)} fusion(bf16[128,2560]{1,0:T(8,128)(2,1)} %shard_map.127, bf16[2560,512]{1,0:T(8,128)(2,1)} %bitcast.76), kind=kOutput, calls=%fused_computation.98 | convolution fusion | flops 335609856 | bytes 3407872 | tf_op jit(solution)/shard_map/dot_general | solution.py:394
  71.9 0.9 pad_maximum_fusion.10
  72.8 1.3 collective-permute-start.11
  74.1 4.9 %collective-permute-start.10 = (f32[5,20,2,128]{3,2,1,0:T(2,128)S(1)}, f32[5,20,2,128]{3,2,1,0:T(2,128)S(1)}, u32[]{:S(2)}, u32[]{:S(2)}) collective-permute-start(f32[5,20,2,128]{3,2,1,0:T(2,128)S(1)} %get-tuple-element.20), channel_id=1, source_target_pairs={{0,1},{1,2},{2,3},{4,5},{5,6},{6,7},{8,9},{9,10},{10,11},{12,13},{... | collective-permute-start | bytes 307208 | tf_op jit(solution)/shard_map/ppermute | solution.py:33
  79.0 1.3 fusion.50
  80.3 0.7 collective-permute-done.10
  81.0 4.4 %select_maximum_fusion = f32[5,20,36,132]{3,2,1,0:T(8,128)S(1)} fusion(f32[5,20,2,128]{3,2,1,0:T(2,128)S(1)} %collective-permute-done.11, f32[5,20,2,128]{3,2,1,0:T(2,128)S(1)} %collective-permute-done.10, f32[5,2,32,128]{3,2,1,0:T(8,128)} %collective-permute-done.9, f32[5,16,32,128]{3,2,1,0:T(8,128)S(1)} %fusion.21, f32[5,2,32,128]{3,2,1,0:T(8,128)} %collective-permute-done.8), kind=kLoop, calls=%fused_computation.4 | loop fusion | flops 5702400 | bytes 3744000 | tf_op jit(solution)/shard_map/concatenate | solution.py:31
  85.4 1.1 broadcast_multiply_fusion.5
  86.5 1.6 maximum_maximum_fusion.1
  88.1 0.5 broadcast_multiply_fusion.4
  88.8 4.2 %fusion.18 = f32[5,16,32,128]{3,2,1,0:T(8,128)S(1)} fusion(f32[5,16,32,128]{3,2,1,0:T(8,128)S(1)} %fusion.21, f32[5,16,32,128]{3,2,1,0:T(8,128)S(1)} %constant_dynamic-update-slice_fusion.11, f32[5,16,32,128]{3,2,1,0:T(8,128)S(1)} %get-tuple-element.9, f32[5,16,32,128]{3,2,1,0:T(8,128)S(1)} %get-tuple-element.7, ...), kind=kLoop, calls=%fused_computation.64 | loop fusion | flops 14090240 | bytes 17367040 | tf_op jit(solution)/shard_map/add | solution.py:153
  93.1 1.4 copy.27
  94.4 0.1 copy-done.3
  94.5 6.1 %shard_map.128 = bf16[128,2560]{1,0:T(8,128)(2,1)} custom-call(f32[8,320,128]{2,1,0:T(8,128)} %bitcast.82), custom_call_target="tpu_custom_call" | custom-call | flops 2621440 | bytes 1966080 | tf_op jit(solution)/shard_map/pallas_call | solution.py:123
  100.6 2.5 %convolution_convert_fusion.1 = bf16[128,512]{1,0:T(8,128)(2,1)S(1)} fusion(bf16[128,2560]{1,0:T(8,128)(2,1)} %shard_map.128, bf16[2560,512]{1,0:T(8,128)(2,1)} %bitcast.77), kind=kOutput, calls=%fused_computation.97 | convolution fusion | flops 335609856 | bytes 3407872 | tf_op jit(solution)/shard_map/dot_general | solution.py:395
  103.1 1.1 fusion.3
  104.2 10.6 %all-to-all-start = ((bf16[32,8,1152]{2,1,0:T(8,128)(2,1)}), bf16[32,8,1152]{2,1,0:T(8,128)(2,1)S(1)}, u32[]{:S(2)}, u32[]{:S(2)}) async-start(bf16[32,8,1152]{2,1,0:T(8,128)(2,1)} %fusion.3), calls=%async_computation | async-start | bytes 1179648 | tf_op jit(solution)/shard_map/all_to_all | solution.py:416
  114.8 0.7 fusion.59.unplace_ref
  115.5 1.1 copy.28
  116.5 13.5 %all-to-all-done = bf16[32,8,1152]{2,1,0:T(8,128)(2,1)S(1)} async-done(((bf16[32,8,1152]{2,1,0:T(8,128)(2,1)}), bf16[32,8,1152]{2,1,0:T(8,128)(2,1)S(1)}, u32[]{:S(2)}, u32[]{:S(2)}) %all-to-all-start) | async-done | bytes 589856 | tf_op jit(solution)/shard_map/all_to_all | solution.py:416
  130.2 2.3 %convolution_add_fusion = f32[256,2048]{1,0:T(8,128)S(1)} fusion(bf16[1,512,2048]{2,1,0:T(8,128)(2,1)} %param.12, f32[2048]{0:T(1024)S(1)} %bitcast.89, bf16[256,1152]{1,0:T(8,128)(2,1)S(1)} %bitcast.84), kind=kOutput, calls=%fused_computation.19 | convolution fusion | flops 537395200 | bytes 4464640 | tf_op jit(solution)/shard_map/dot_general | solution.py:85
  132.5 1.4 convert_reduce_fusion.1
  133.8 1.7 convert_reduce_fusion
  135.6 1.5 fusion.46.grad_ref
  137.0 2.8 %convolution_bitcast_fusion.1 = f32[1,512,2048]{2,1,0:T(8,128)} fusion(bf16[256,2048]{1,0:T(8,128)(2,1)S(1)} %get-tuple-element.42, bf16[256,1152]{1,0:T(8,128)(2,1)S(1)} %bitcast.86), kind=kOutput, calls=%fused_computation.16 | convolution fusion | flops 536870912 | bytes 5505024 | tf_op jit(solution)/shard_map/dot_general | solution.py:73
  139.8 2.8 %convolution_bitcast_fusion = f32[1,2048,512]{2,1,0:T(8,128)} fusion(bf16[256,512]{1,0:T(8,128)(2,1)S(1)} %get-tuple-element.44, f32[256,2048]{1,0:T(8,128)S(1)} %convolution_add_fusion), kind=kOutput, calls=%fused_computation.15 | convolution fusion | flops 539492352 | bytes 6553600 | tf_op jit(solution)/shard_map/dot_general | solution.py:73
  142.6 56.4 %shard_map.129 = bf16[8,4,80,512]{3,2,1,0:T(8,128)(2,1)} custom-call(bf16[32,8,512]{2,1,0:T(8,128)(2,1)} %fusion.46.grad_ref, bf16[128,256]{1,0:T(8,128)(2,1)} %fusion.59.unplace_ref, bf16[8,4,80,128]{3,2,1,0:T(8,128)(2,1)} %bitcast.87), custom_call_target="tpu_custom_call" | custom-call | tf_op jit(solution)/shard_map/pallas_call | solution.py:359
  199.1 2.5 %convert_bitcast_fusion = f32[320,8,512]{2,0,1:T(8,128)S(1)} fusion(bf16[8,4,80,512]{3,2,1,0:T(8,128)(2,1)} %shard_map.129), kind=kLoop, calls=%fused_computation.2 | loop fusion | flops 1310720 | bytes 7864320 | tf_op jit(solution)/shard_map/convert_element_type | solution.py:427
  201.5 5.4 %copy.33 = f32[320,8,512]{2,1,0:T(8,128)} copy(f32[320,8,512]{2,0,1:T(8,128)S(1)} %convert_bitcast_fusion) | data formatting | bytes 10485760 | tf_op jit(solution)/shard_map/convert_element_type | solution.py:427
  (52 shorter events, 1.3 us)
Async XLA Ops:
  0.6 131.8 %copy-start = (bf16[1,2048,512]{2,1,0:T(8,128)(2,1)S(1)}, bf16[1,2048,512]{2,1,0:T(8,128)(2,1)}, u32[]{:S(2)}) copy-start(bf16[1,2048,512]{2,1,0:T(8,128)(2,1)} %param.14) | copy-start | bytes 6291460
  2.5 9.4 %collective-permute-start = (f32[5,2,32,128]{3,2,1,0:T(8,128)}, f32[5,2,32,128]{3,2,1,0:T(8,128)}, u32[]{:S(2)}, u32[]{:S(2)}) collective-permute-start(f32[5,2,32,128]{3,2,1,0:T(8,128)} %get-tuple-element.36), channel_id=1, source_target_pairs={{0,4},{4,8},{8,12},{12,16},{16,20},{20,24},{24,28},{1,5},{5,9},{9,... | collective-permute-start | bytes 491528 | tf_op jit(solution)/shard_map/ppermute | solution.py:33
  5.6 7.7 %collective-permute-start.1 = (f32[5,2,32,128]{3,2,1,0:T(8,128)}, f32[5,2,32,128]{3,2,1,0:T(8,128)}, u32[]{:S(2)}, u32[]{:S(2)}) collective-permute-start(f32[5,2,32,128]{3,2,1,0:T(8,128)} %get-tuple-element.35), channel_id=1, source_target_pairs={{4,0},{8,4},{12,8},{16,12},{20,16},{24,20},{28,24},{5,1},{9,5},{13... | collective-permute-start | bytes 491528 | tf_op jit(solution)/shard_map/ppermute | solution.py:35
  6.9 4.3 %copy-start.6 = (s32[2,4,16]{2,1,0:T(4,128)S(1)}, s32[2,4,16]{2,1,0:T(4,128)}, u32[]{:S(2)}) copy-start(s32[2,4,16]{2,1,0:T(4,128)} %param.11) | copy-start | bytes 1540
  6.9 4.4 %copy-start.7 = (s32[64,1]{0,1:T(1,128)S(1)}, s32[64,1]{0,1:T(1,128)}, u32[]{:S(2)}) copy-start(s32[64,1]{0,1:T(1,128)} %param.10) | copy-start | bytes 772
  6.9 6.0 %copy-start.1 = (f32[5,16,32,128]{3,2,1,0:T(8,128)S(1)}, f32[5,16,32,128]{3,2,1,0:T(8,128)}, u32[]{:S(2)}) copy-start(f32[5,16,32,128]{3,2,1,0:T(8,128)} %param.8) | copy-start | bytes 3932164
  14.4 6.9 %collective-permute-start.3 = (f32[5,20,2,128]{3,2,1,0:T(2,128)S(1)}, f32[5,20,2,128]{3,2,1,0:T(2,128)S(1)}, u32[]{:S(2)}, u32[]{:S(2)}) collective-permute-start(f32[5,20,2,128]{3,2,1,0:T(2,128)S(1)} %get-tuple-element.27), channel_id=1, source_target_pairs={{1,0},{2,1},{3,2},{5,4},{6,5},{7,6},{9,8},{10,9},{11,10},{13,12},{... | collective-permute-start | bytes 307208 | tf_op jit(solution)/shard_map/ppermute | solution.py:35
  15.7 7.2 %collective-permute-start.2 = (f32[5,20,2,128]{3,2,1,0:T(2,128)S(1)}, f32[5,20,2,128]{3,2,1,0:T(2,128)S(1)}, u32[]{:S(2)}, u32[]{:S(2)}) collective-permute-start(f32[5,20,2,128]{3,2,1,0:T(2,128)S(1)} %get-tuple-element.26), channel_id=1, source_target_pairs={{0,1},{1,2},{2,3},{4,5},{5,6},{6,7},{8,9},{9,10},{10,11},{12,13},{... | collective-permute-start | bytes 307208 | tf_op jit(solution)/shard_map/ppermute | solution.py:33
  30.4 4.9 %collective-permute-start.5 = (f32[5,2,32,128]{3,2,1,0:T(8,128)S(1)}, f32[5,2,32,128]{3,2,1,0:T(8,128)S(1)}, u32[]{:S(2)}, u32[]{:S(2)}) collective-permute-start(f32[5,2,32,128]{3,2,1,0:T(8,128)S(1)} %get-tuple-element.31), channel_id=1, source_target_pairs={{4,0},{8,4},{12,8},{16,12},{20,16},{24,20},{28,24},{5,1},{9,5},{13... | collective-permute-start | bytes 491528 | tf_op jit(solution)/shard_map/ppermute | solution.py:35
  31.7 4.6 %collective-permute-start.4 = (f32[5,2,32,128]{3,2,1,0:T(8,128)S(1)}, f32[5,2,32,128]{3,2,1,0:T(8,128)S(1)}, u32[]{:S(2)}, u32[]{:S(2)}) collective-permute-start(f32[5,2,32,128]{3,2,1,0:T(8,128)S(1)} %get-tuple-element.30), channel_id=1, source_target_pairs={{0,4},{4,8},{8,12},{12,16},{16,20},{20,24},{24,28},{1,5},{5,9},{9,... | collective-permute-start | bytes 491528 | tf_op jit(solution)/shard_map/ppermute | solution.py:33
  36.3 6.7 %collective-permute-start.7 = (f32[5,20,2,128]{3,2,1,0:T(2,128)S(1)}, f32[5,20,2,128]{3,2,1,0:T(2,128)S(1)}, u32[]{:S(2)}, u32[]{:S(2)}) collective-permute-start(f32[5,20,2,128]{3,2,1,0:T(2,128)S(1)} %get-tuple-element.25), channel_id=1, source_target_pairs={{1,0},{2,1},{3,2},{5,4},{6,5},{7,6},{9,8},{10,9},{11,10},{13,12},{... | collective-permute-start | bytes 307208 | tf_op jit(solution)/shard_map/ppermute | solution.py:35
  37.6 7.0 %collective-permute-start.6 = (f32[5,20,2,128]{3,2,1,0:T(2,128)S(1)}, f32[5,20,2,128]{3,2,1,0:T(2,128)S(1)}, u32[]{:S(2)}, u32[]{:S(2)}) collective-permute-start(f32[5,20,2,128]{3,2,1,0:T(2,128)S(1)} %get-tuple-element.24), channel_id=1, source_target_pairs={{0,1},{1,2},{2,3},{4,5},{5,6},{6,7},{8,9},{9,10},{10,11},{12,13},{... | collective-permute-start | bytes 307208 | tf_op jit(solution)/shard_map/ppermute | solution.py:33
  54.2 17.6 %collective-permute-start.9 = (f32[5,2,32,128]{3,2,1,0:T(8,128)}, f32[5,2,32,128]{3,2,1,0:T(8,128)}, u32[]{:S(2)}, u32[]{:S(2)}) collective-permute-start(f32[5,2,32,128]{3,2,1,0:T(8,128)} %get-tuple-element.29), channel_id=1, source_target_pairs={{4,0},{8,4},{12,8},{16,12},{20,16},{24,20},{28,24},{5,1},{9,5},{13... | collective-permute-start | bytes 491528 | tf_op jit(solution)/shard_map/ppermute | solution.py:35
  55.5 16.4 %collective-permute-start.8 = (f32[5,2,32,128]{3,2,1,0:T(8,128)}, f32[5,2,32,128]{3,2,1,0:T(8,128)}, u32[]{:S(2)}, u32[]{:S(2)}) collective-permute-start(f32[5,2,32,128]{3,2,1,0:T(8,128)} %get-tuple-element.28), channel_id=1, source_target_pairs={{0,4},{4,8},{8,12},{12,16},{16,20},{20,24},{24,28},{1,5},{5,9},{9,... | collective-permute-start | bytes 491528 | tf_op jit(solution)/shard_map/ppermute | solution.py:33
  72.8 7.5 %collective-permute-start.11 = (f32[5,20,2,128]{3,2,1,0:T(2,128)S(1)}, f32[5,20,2,128]{3,2,1,0:T(2,128)S(1)}, u32[]{:S(2)}, u32[]{:S(2)}) collective-permute-start(f32[5,20,2,128]{3,2,1,0:T(2,128)S(1)} %get-tuple-element.21), channel_id=1, source_target_pairs={{1,0},{2,1},{3,2},{5,4},{6,5},{7,6},{9,8},{10,9},{11,10},{13,12},{... | collective-permute-start | bytes 307208 | tf_op jit(solution)/shard_map/ppermute | solution.py:35
  74.1 6.9 %collective-permute-start.10 = (f32[5,20,2,128]{3,2,1,0:T(2,128)S(1)}, f32[5,20,2,128]{3,2,1,0:T(2,128)S(1)}, u32[]{:S(2)}, u32[]{:S(2)}) collective-permute-start(f32[5,20,2,128]{3,2,1,0:T(2,128)S(1)} %get-tuple-element.20), channel_id=1, source_target_pairs={{0,1},{1,2},{2,3},{4,5},{5,6},{6,7},{8,9},{9,10},{10,11},{12,13},{... | collective-permute-start | bytes 307208 | tf_op jit(solution)/shard_map/ppermute | solution.py:33
  93.0 1.5 copy-start.3
  103.0 12.4 %copy-start.2 = (bf16[128,2560]{1,0:T(8,128)(2,1)S(1)}, bf16[128,2560]{1,0:T(8,128)(2,1)}, u32[]{:S(2)}) copy-start(bf16[128,2560]{1,0:T(8,128)(2,1)} %shard_map.127) | copy-start | bytes 1966084
  104.2 25.9 %copy-start.5 = (f32[1,2048]{1,0:T(1,128)S(1)}, f32[1,2048]{1,0:T(1,128)}, u32[]{:S(2)}) copy-start(f32[1,2048]{1,0:T(1,128)} %param.13) | copy-start | bytes 24580
  104.2 25.8 %all-to-all-start = ((bf16[32,8,1152]{2,1,0:T(8,128)(2,1)}), bf16[32,8,1152]{2,1,0:T(8,128)(2,1)S(1)}, u32[]{:S(2)}, u32[]{:S(2)}) async-start(bf16[32,8,1152]{2,1,0:T(8,128)(2,1)} %fusion.3), calls=%async_computation | async-start | bytes 1179648 | tf_op jit(solution)/shard_map/all_to_all | solution.py:416
  130.1 2.3 %copy-start.8 = (f32[1,512]{1,0:T(1,128)S(1)}, f32[1,512]{1,0:T(1,128)}, u32[]{:S(2)}) copy-start(f32[1,512]{1,0:T(1,128)} %param.15) | copy-start | bytes 6148
  133.8 1.7 copy-start.4

commit v2 on v1

--- a/solution.py
+++ b/solution.py
@@ -20,53 +20,7 @@
 drift_y = -0.4
 drift_z = 0.3
 error_weight = 0.0625
-
-
-def with_halo(cells, sides, width):
-    for axis, dim in sides:
-        count = lax.axis_size(axis)
-        ends = count - 1
-        head = lax.slice_in_dim(cells, 0, width, axis=dim)
-        tail = lax.slice_in_dim(cells, cells.shape[dim] - width, cells.shape[dim], axis=dim)
-        cells = jnp.concatenate(
-            [
-                lax.ppermute(tail, axis, [(i, (i + 1) % count) for i in range(ends)]),
-                cells,
-                lax.ppermute(head, axis, [((i + 1) % count, i) for i in range(ends)]),
-            ],
-            axis=dim,
-        )
-    return cells
-
-
-def shifted(padded, dimension, offset):
-    window = [slice(None)]
-    for other in (1, 2, 3):
-        window.append(slice(2, padded.shape[other] - 2))
-    window[dimension] = slice(2 + offset, padded.shape[dimension] - 2 + offset)
-    return padded[tuple(window)]
-
-
-def tendency(padded):
-    gradients = []
-    laplacian = 0.0
-    for dimension in (1, 2, 3):
-        back_two = shifted(padded, dimension, -2)
-        back_one = shifted(padded, dimension, -1)
-        middle = shifted(padded, dimension, 0)
-        ahead_one = shifted(padded, dimension, 1)
-        ahead_two = shifted(padded, dimension, 2)
-        gradients.append((back_two - 8.0 * back_one + 8.0 * ahead_one - ahead_two) / 12.0)
-        laplacian = (
-            laplacian
-            + (-back_two + 16.0 * back_one - 30.0 * middle + 16.0 * ahead_one - ahead_two) / 12.0
-        )
-    carried = drift_x * gradients[0] + drift_y * gradients[1] + drift_z * gradients[2]
-    divergence = gradients[0][1] + gradients[1][2] + gradients[2][3]
-    acoustic = jnp.stack(
-        [divergence, gradients[0][4], gradients[1][4], gradients[2][4], divergence]
-    )
-    return viscosity * laplacian - carried - acoustic
+PAD = 8
 
 
 def contract_rows(left, right):
@@ -95,64 +49,6 @@
     w_first_grad = contract_rows(source, pre_grad)
     source_grad = contract_cols(pre_grad, w_first).astype(jnp.bfloat16)
     return (source_grad, w_first_grad, b_first_grad, w_second_grad, b_second_grad)
-
-
-def patch_kernel(cells_ref, rows_ref, *turned):
-    count, inner, lanes = rows_ref.shape[0], cells_ref.shape[1], turned[0].shape[1]
-    for part, piece in enumerate(turned):
-        cells = cells_ref[0, part * lanes : min(inner, (part + 1) * lanes), :]
-        if cells.shape[0] < lanes:
-            cells = jnp.concatenate(
-                [cells, jnp.zeros((lanes - cells.shape[0], cells.shape[1]), cells.dtype)], axis=0
-            )
-        piece[...] = cells.T
-    parts = []
-    for offset in range(PATCH):
-        for part, piece in enumerate(turned):
-            rows = piece[pl.ds(offset, count, stride=PATCH), :]
-            parts.append(rows[:, : min(lanes, inner - part * lanes)])
-    rows_ref[...] = jnp.concatenate(parts, axis=1).astype(rows_ref.dtype)
-
-
-def patchify(state):
-    width_x, width_y, width_z = (state.shape[1], state.shape[2], state.shape[3])
-    shaped = state.reshape(FIELDS, width_x // PATCH, PATCH, width_y // PATCH, PATCH, width_z)
-    cells = shaped.transpose(1, 3, 0, 2, 4, 5).reshape(-1, FIELDS * PATCH * PATCH, width_z)
-    columns, inner = cells.shape[0], cells.shape[1]
-    count = width_z // PATCH
-    return pl.pallas_call(
-        patch_kernel,
-        grid=(columns,),
-        out_shape=jax.ShapeDtypeStruct((columns * count, inner * PATCH), jnp.bfloat16),
-        in_specs=[pl.BlockSpec((1, inner, width_z), lambda i: (i, 0, 0))],
-        out_specs=pl.BlockSpec((count, inner * PATCH), lambda i: (i, 0)),
-        scratch_shapes=[pltpu.VMEM((width_z, 128), jnp.float32)] * pl.cdiv(inner, 128),
-        cost_estimate=pl.CostEstimate(
-            flops=8 * cells.size, bytes_accessed=6 * cells.size, transcendentals=0
-        ),
-    )(cells)
-
-
-def pick(first, second, lag_index):
-    count_x, count_y, count_z = lag_index.shape
-    lag = jnp.repeat(lag_index, PATCH, axis=2)
-    lag = lag.reshape(1, count_x, 1, count_y, 1, count_z * PATCH)
-    shape = (FIELDS, count_x, PATCH, count_y, PATCH, count_z * PATCH)
-    return jnp.where(lag == 1, second.reshape(shape), first.reshape(shape)).reshape(first.shape)
-
-
-def pad_third(current):
-    return jnp.pad(current, ((0, 0), (0, 0), (0, 0), (2, 2)))
-
-
-def advance(fields):
-    states = []
-    current = fields
-    for counter in range(STEPS):
-        padded = with_halo(current, (("gx", 1), ("gy", 2)), 2)
-        current = current + time_step * tendency(pad_third(padded))
-        states.append(current)
-    return states
 
 
 def my_place():
@@ -384,18 +280,305 @@
     )(grad_slots, unplace, feat)
 
 
-def per_device(fields, patch_weight, trainer_of, lag_index, w_in, b_in, w_out, b_out):
-    states = advance(fields)
+def flow_kernel(
+    gx_n,
+    gy_n,
+    fields_ref,
+    mask_ref,
+    weight_ref,
+    place_ref,
+    out_ref,
+    source_ref,
+    target_ref,
+    turned_ref,
+    state_0,
+    state_1,
+    state_2,
+    face_out,
+    face_in,
+    swap,
+    cells,
+    turned,
+    source_out,
+    target_out,
+    halo_send,
+    halo_recv,
+    source_send,
+    source_recv,
+    target_send,
+    target_recv,
+):
+    gx, gy = my_place()
+    me = gx * gy_n + gy
+    devices = gx_n * gy_n
+    states = (state_0, state_1, state_2)
+    _, size_x, size_y, size_z = fields_ref.shape
+    inner = pl.ds(PAD, size_y)
+    columns, embed = mask_ref.shape[0], weight_ref.shape[1]
+    slot_rows = source_out.shape[1]
+    count_y = size_y // PATCH
+    kinds = FIELDS * PATCH * PATCH
+    rows = turned.shape[1]
+    count_z = size_z // PATCH
+
+    edges = ((gx > 0, 0), (gx < gx_n - 1, 1), (gy > 0, 2), (gy < gy_n - 1, 3))
+    for state in states:
+        for inside, side in edges:
+            @pl.when(jnp.logical_not(inside))
+            def _():
+                if side < 2:
+                    plane = pl.ds(0 if side == 0 else size_x + 2, 2)
+                    state[:, plane, inner, :] = jnp.zeros((FIELDS, 2, size_y, size_z), jnp.float32)
+                else:
+                    strip = pl.ds(0 if side == 2 else PAD + size_y, PAD)
+                    state[:, pl.ds(2, size_x), strip, :] = jnp.zeros(
+                        (FIELDS, size_x, PAD, size_z), jnp.float32
+                    )
+
+    barrier = pltpu.get_barrier_semaphore()
+
+    def greet(step, carry):
+        other = lax.rem(me + step, devices)
+        pl.semaphore_signal(
+            barrier,
+            inc=1,
+            device_id=(other // gy_n, lax.rem(other, gy_n)),
+            device_id_type=pl.DeviceIdType.MESH,
+        )
+        return carry
+
+    lax.fori_loop(1, devices, greet, 0)
+    state_0[:, pl.ds(2, size_x), inner, :] = fields_ref[...]
+    place_of = lax.broadcasted_iota(jnp.int32, (size_z, PATCH * rows), 1)
+    column_of = lax.rem(place_of, rows) // count_z
+    cell_of = column_of * size_z + lax.rem(place_of, count_z) * PATCH + place_of // rows
+    for column in range(columns):
+        row_of = lax.broadcasted_iota(jnp.int32, (size_z, PATCH * rows), 0) + column * size_z
+        swap[pl.ds(column * size_z, size_z), :] = jnp.where(row_of == cell_of, 1.0, 0.0).astype(
+            jnp.bfloat16
+        )
+    pl.semaphore_wait(barrier, devices - 1)
+
+    def halo_copy(step, side):
+        state = states[step]
+        if side == 0:
+            src, dst = state.at[:, pl.ds(2, 2), inner], state.at[:, pl.ds(size_x + 2, 2), inner]
+            target = (gx - 1, gy)
+        elif side == 1:
+            src, dst = state.at[:, pl.ds(size_x, 2), inner], state.at[:, pl.ds(0, 2), inner]
+            target = (gx + 1, gy)
+        else:
+            src, dst = face_out.at[step, side - 2], face_in.at[step, 3 - side]
+            target = (gx, gy - 1 if side == 2 else gy + 1)
+        return remote(
+            src, dst, halo_send.at[step, side], halo_recv.at[step, side ^ 1], *target
+        )
+
+    def halo_start(step):
+        state = states[step]
+        for side in (2, 3):
+            first = PAD if side == 2 else PAD + size_y - 2
+            face_out[step, side - 2] = state[:, pl.ds(2, size_x), pl.ds(first, 2), :]
+        for inside, side in edges:
+            @pl.when(inside)
+            def _():
+                halo_copy(step, side).start()
+
+    def halo_wait(step):
+        state = states[step]
+        for inside, side in edges:
+            @pl.when(inside)
+            def _():
+                copy = halo_copy(step, side)
+                copy.wait_send()
+                remote(
+                    face_in.at[step, 0] if side > 1 else state.at[:, pl.ds(0, 2), inner],
+                    face_in.at[step, 0] if side > 1 else state.at[:, pl.ds(0, 2), inner],
+                    halo_send.at[step, side],
+                    halo_recv.at[step, side],
+                    gx,
+                    gy,
+                ).wait_recv()
+                if side > 1:
+                    first = PAD - 2 if side == 2 else PAD + size_y
+                    state[:, pl.ds(2, size_x), pl.ds(first, 2), :] = face_in[step, side - 2]
+
+    lane = lax.broadcasted_iota(jnp.int32, (size_y, size_z), 1)
+
+    def advance_state(step):
+        state = states[step]
+
+        def plane(i, carry):
+            def pieces(field):
+                middle = state[field, i + 2, inner, :]
+                around = []
+                around.append([state[field, i + k, inner, :] for k in (0, 1, 3, 4)])
+                around.append(
+                    [state[field, i + 2, pl.ds(PAD + k, size_y), :] for k in (-2, -1, 1, 2)]
+                )
+                around.append(
+                    [
+                        jnp.where(lane < 2, 0.0, pltpu.roll(middle, 2, 1)),
+                        jnp.where(lane < 1, 0.0, pltpu.roll(middle, 1, 1)),
+                        jnp.where(lane >= size_z - 1, 0.0, pltpu.roll(middle, size_z - 1, 1)),
+                        jnp.where(lane >= size_z - 2, 0.0, pltpu.roll(middle, size_z - 2, 1)),
+                    ]
+                )
+                slopes = [(a - d) + 8.0 * (c - b) for a, b, c, d in around]
+                near = sum(b + c for a, b, c, d in around)
+                far = sum(a + d for a, b, c, d in around)
+                change = viscosity * (16.0 * near - far - 90.0 * middle)
+                change = change - (
+                    drift_x * slopes[0] + drift_y * slopes[1] + drift_z * slopes[2]
+                )
+                return middle, slopes, change
+
+            def put(field, value):
+                if step < STEPS - 1:
+                    states[step + 1][field, i + 2, inner, :] = value
+                else:
+                    out_ref[field, i] = value
+
+            scale = time_step / 12.0
+            middle_p, slopes_p, change_p = pieces(4)
+            spread = 0.0
+            for axis in range(3):
+                middle, slopes, change = pieces(1 + axis)
+                spread = spread + slopes[axis]
+                put(1 + axis, middle + scale * (change - slopes_p[axis]))
+            put(4, middle_p + scale * (change_p - spread))
+            middle, slopes, change = pieces(0)
+            put(0, middle + scale * (change - spread))
+            return carry
+
+        lax.fori_loop(0, size_x, plane, 0)
+
+    def column_cells(state, offset_x, offset_y, column):
+        first_x = offset_x + column // count_y * PATCH
+        first_y = offset_y + column % count_y * PATCH
+        return state[:, pl.ds(first_x, PATCH), pl.ds(first_y, PATCH), :].reshape(kinds, size_z)
+
+    def embed_cells():
+        for offset in range(PATCH):
+            turned[pl.ds(offset, kinds, stride=PATCH), :] = jnp.dot(
+                cells[...],
+                swap[:, pl.ds(offset * rows, rows)],
+                preferred_element_type=jnp.float32,
+            )
+        patches = turned[...].astype(jnp.bfloat16)
+        return patches, contract_rows(patches, weight_ref[...]).astype(jnp.bfloat16)
+
+    def scatter(step, stage, landing, send_sem, recv_sem):
+        other = lax.rem(me + step, devices)
+        return remote(
+            stage.at[other],
+            landing.at[me],
+            send_sem.at[step],
+            recv_sem.at[step],
+            other // gy_n,
+            lax.rem(other, gy_n),
+        )
+
+    def scatter_start(values, stage, landing, send_sem, recv_sem):
+        packed = jnp.dot(place_ref[...], values, preferred_element_type=jnp.float32)
+        stage[...] = packed.reshape(stage.shape).astype(jnp.bfloat16)
+
+        def start(step, carry):
+            scatter(step, stage, landing, send_sem, recv_sem).start()
+            return carry
+
+        lax.fori_loop(1, devices, start, 0)
+        landing[me] = stage[me]
+
+    def scatter_wait(*args):
+        def wait(step, carry):
+            scatter(step, *args).wait()
+            return carry
+
+        lax.fori_loop(1, devices, wait, 0)
+
+    halo_start(0)
+    halo_wait(0)
+    advance_state(0)
+    halo_start(1)
+    halo_wait(1)
+    advance_state(1)
+    halo_start(2)
+    for column in range(columns):
+        first = column_cells(state_1, 2, PAD, column)
+        second = column_cells(state_2, 2, PAD, column)
+        chosen = jnp.where(mask_ref[pl.ds(column, 1), :] > 0.5, second, first)
+        cells[:, pl.ds(column * size_z, size_z)] = chosen.astype(jnp.bfloat16)
+    patches, source = embed_cells()
+    turned_ref[...] = patches
+    source_args = (source_out, source_ref, source_send, source_recv)
+    ones = jnp.ones((rows, source_out.shape[2] - embed), jnp.bfloat16)
+    scatter_start(jnp.concatenate([source, ones], axis=1), *source_args)
+    halo_wait(2)
+    advance_state(2)
+    for column in range(columns):
+        cells[:, pl.ds(column * size_z, size_z)] = column_cells(out_ref, 0, 0, column).astype(
+            jnp.bfloat16
+        )
+    patches, target = embed_cells()
+    target_args = (target_out, target_ref, target_send, target_recv)
+    scatter_start(target, *target_args)
+    scatter_wait(*source_args)
+    scatter_wait(*target_args)
+
+
+def flow(fields, mask, weight, place, slot_rows):
     gx_n, gy_n = lax.axis_size("gx"), lax.axis_size("gy")
     devices = gx_n * gy_n
-    picked = patchify(pick(states[0], states[1], lag_index))
+    fields_n, size_x, size_y, size_z = fields.shape
+    features, embed = weight.shape
+    rows = place.shape[1]
+    bf16, f32 = jnp.bfloat16, jnp.float32
+    dma = pltpu.SemaphoreType.DMA
+    whole = pl.BlockSpec(memory_space=pltpu.VMEM)
+    padded = (fields_n, size_x + 4, size_y + 2 * PAD, size_z)
+    faces = (STEPS, 2, fields_n, size_x, 2, size_z)
+    source_shape = (devices, slot_rows, embed + 128)
+    target_shape = (devices, slot_rows, embed)
+    return pl.pallas_call(
+        functools.partial(flow_kernel, gx_n, gy_n),
+        out_shape=[
+            jax.ShapeDtypeStruct(fields.shape, f32),
+            jax.ShapeDtypeStruct(source_shape, bf16),
+            jax.ShapeDtypeStruct(target_shape, bf16),
+            jax.ShapeDtypeStruct((features, rows), bf16),
+        ],
+        in_specs=[whole] * 4,
+        out_specs=[whole] * 4,
+        scratch_shapes=[
+            pltpu.VMEM(padded, f32),
+            pltpu.VMEM(padded, f32),
+            pltpu.VMEM(padded, f32),
+            pltpu.VMEM(faces, f32),
+            pltpu.VMEM(faces, f32),
+            pltpu.VMEM((mask.shape[0] * size_z, PATCH * rows), bf16),
+            pltpu.VMEM((features // PATCH, mask.shape[0] * size_z), bf16),
+            pltpu.VMEM((features, rows), f32),
+            pltpu.VMEM(source_shape, bf16),
+            pltpu.VMEM(target_shape, bf16),
+            dma((STEPS, 4)),
+            dma((STEPS, 4)),
+            dma((devices,)),
+            dma((devices,)),
+            dma((devices,)),
+            dma((devices,)),
+        ],
+        compiler_params=pltpu.CompilerParams(
+            collective_id=0, has_side_effects=True, vmem_limit_bytes=60 * 1024 * 1024
+        ),
+    )(fields, mask, weight, place)
+
+
+def per_device(fields, patch_weight, trainer_of, lag_index, w_in, b_in, w_out, b_out):
+    gx_n, gy_n = lax.axis_size("gx"), lax.axis_size("gy")
+    devices = gx_n * gy_n
     embed = patch_weight.shape[1]
-    weight = patch_weight.reshape(-1, PATCH, embed).transpose(1, 0, 2).reshape(-1, embed)
-    source = jnp.dot(picked, weight, preferred_element_type=jnp.float32).astype(jnp.bfloat16)
-    target = jnp.dot(
-        patchify(states[-1]), weight, preferred_element_type=jnp.float32
-    ).astype(jnp.bfloat16)
-    patch_count = picked.shape[0]
+    patch_count = lag_index.size
     block_count = patch_count // BLOCK_ROWS
     slot_count = max(8 // BLOCK_ROWS, 2 * block_count // devices)
     owners = trainer_of[:, 0]
@@ -409,24 +592,21 @@
     slots = jnp.arange(devices * slot_rows, dtype=jnp.int32)
     place = (slots[:, None] == patch_slot[None, :]).astype(jnp.bfloat16)
     unplace = (patch_slot[:, None] == slots[None, :]).astype(jnp.bfloat16)
-
-    rows = jnp.concatenate([source, target, jnp.ones((patch_count, 128), jnp.bfloat16)], 1)
-    packed = jnp.dot(place, rows, preferred_element_type=jnp.float32).astype(jnp.bfloat16)
-    packed = packed.reshape(devices, slot_rows, rows.shape[1])
-    got = lax.all_to_all(packed, ("gx", "gy"), split_axis=0, concat_axis=0, tiled=True)
-    got = got.reshape(devices * slot_rows, rows.shape[1])
-    valid_rows = got[:, 2 * embed : 2 * embed + 1].astype(jnp.float32)
+    mask = jnp.repeat(lag_index.reshape(-1, lag_index.shape[2]), PATCH, axis=1)
+    mask = mask.astype(jnp.float32)
+
+    new_fields, source, target, patches = flow(fields, mask, patch_weight, place, slot_rows)
+    source = source.reshape(devices * slot_rows, -1)
+    target = target.reshape(devices * slot_rows, -1)
+    valid_rows = source[:, embed : embed + 1].astype(jnp.float32)
     results = trainer_step(
-        got[:, :embed], got[:, embed : 2 * embed], valid_rows, w_in[0], b_in[0], w_out[0], b_out[0]
-    )
-    feat = picked.T.reshape(gx_n, gy_n, -1, patch_count)
-    summed = patch_gradient_sum(
-        results[0].reshape(devices, slot_rows, embed), unplace, feat
-    )
-    summed = summed.reshape(PATCH, -1, embed).transpose(1, 0, 2).reshape(-1, embed)
-    patch_gradient = summed.astype(jnp.float32)
+        source[:, :embed], target, valid_rows, w_in[0], b_in[0], w_out[0], b_out[0]
+    )
+    feat = patches.reshape(gx_n, gy_n, -1, patch_count)
+    summed = patch_gradient_sum(results[0].reshape(devices, slot_rows, embed), unplace, feat)
+    patch_gradient = summed.reshape(-1, embed).astype(jnp.float32)
     return (
-        states[-1],
+        new_fields,
         patch_gradient,
         results[1][None],
         results[2][None],

time: 208 us -> 127 us (0.61)
  starting transfers between devices: 46.2 us -> 0 us
  Pallas kernels: 68.5 us -> 101 us
  other arithmetic: 35.7 us -> 8.66 us
  waiting for transfers between devices: 18.9 us -> 0 us
  local copies, waits for them, and re-layouts: 17.8 us -> 2.16 us
  matrix products: 18.5 us -> 14.3 us
    ppermute x12 -> x0, starting transfers between devices: 35.7 us -> none  [the longest x6 28 us: with_halo(): lax.ppermute(tail, axis, [(i, (i + 1) % count) for i in range(ends)])]
    pallas_call x2 -> x1, Pallas kernels: 12.1 us -> 44.2 us  [flow(): pl.pallas_call(functools.partial(flow_kernel, gx_n, gy_n), out_shape=[jax...]
    all_to_all x1 -> x0, waiting for transfers between devices: 13.5 us -> none  [per_device(): lax.all_to_all(packed, ('gx', 'gy'), split_axis=0, concat_axis=0, tiled=T...]
    concatenate x5 -> x0, other arithmetic: 11.4 us -> none  [with_halo(): jnp.concatenate([lax.ppermute(tail, axis, [(i, (i + 1) % count) for i in...]
    add x3 -> x0, other arithmetic: 10.7 us -> none  [advance(): current = current + time_step * tendency(pad_third(padded))]
    all_to_all x1 -> x0, starting transfers between devices: 10.6 us -> none  [per_device(): lax.all_to_all(packed, ('gx', 'gy'), split_axis=0, concat_axis=0, tiled=T...]
    div x8 -> x0, other arithmetic: 7.39 us -> none  [tendency(): (back_two - 8.0 * back_one + 8.0 * ahead_one - ahead_two) / 12.0]
    dot_general x3 -> x0, matrix products: 6.04 us -> none  [the longest x1 2.45 us: per_device(): jnp.dot(patchify(states[-1]), weight, preferred_element_type=jnp.float32)]
  transfers between devices with their start and end apart: 13 -> 0, of which waited for: 7 -> 0; matrix products, arithmetic and copies ran while one was open for 7% -> 0% of each run, Pallas kernels for 3% -> 0%
where the time goes in v2:
time: 127 us; the launch traced here: 126 us
  Pallas kernels  101 us (80%)
  matrix products  14.3 us (11%)
  other arithmetic  8.66 us (7%)
  local copies, waits for them, and re-layouts  2.16 us (2%)
    pallas_call x1, Pallas kernels, patch_gradient_sum(): pl.pallas_call(functools.partial(gradient_kernel, gx_n, gy_n), out_shape=...  56.4 us
    pallas_call x1, Pallas kernels, flow(): pl.pallas_call(functools.partial(flow_kernel, gx_n, gy_n), out_shape=[jax...  44.2 us
    dot_general x2, matrix products, contract_rows(): lax.dot_general(left, right, (((0,), (0,)), ((), ())), preferred_element_...  7.34 us
    convert_element_type x1, other arithmetic, per_device(): patch_gradient = summed.reshape(-1, embed).astype(jnp.float32)  3.27 us
    dot_general x2, matrix products, contract_cols(): lax.dot_general(left, right, (((1,), (1,)), ((), ())), preferred_element_...  3.18 us

profile of v2, /device:TPU:0, one launch (start us, length us, event | category | flops | bytes accessed | tf_op | source)
XLA Modules:
  0.0 126.5 jit_solution(3730112346615858869)
XLA Ops:
  0.6 0.0 copy-start
  0.6 0.8 convert_element_type.49
  1.5 0.7 fusion.30
  2.2 0.1 reduce_window_sum.11
  2.3 0.8 select_reduce_fusion
  3.1 0.7 add_multiply_fusion
  3.8 0.1 broadcast_in_dim.24
  3.9 0.1 mul.63
  4.0 0.1 broadcast_in_dim.23
  4.1 0.7 convert_element_type.51.mask_ref
  4.8 0.7 fusion.29.unplace_ref
  5.5 0.6 fusion.28.place_ref
  6.2 0.0 copy-start.6
  6.2 44.2 %shard_map.127 = (f32[5,16,32,128]{3,2,1,0:T(8,128)}, bf16[32,8,640]{2,1,0:T(8,128)(2,1)}, bf16[32,8,512]{2,1,0:T(8,128)(2,1)}, bf16[2560,128]{1,0:T(8,128)(2,1)}) custom-call(f32[5,16,32,128]{3,2,1,0:T(8,128)} %fields_ref.1, f32[8,128]{1,0:T(8,128)} %convert_element_type.51.mask_ref, bf16[2560,512]{1,0:T(8,128)(2,1)} %weight_ref.1, ...), custom_call_target="tpu_custom_call" | custom-call | tf_op jit(solution)/shard_map/pallas_call | solution.py:543
  50.4 0.9 convert_multiply_fusion
  51.3 0.1 copy.16
  51.3 0.0 copy-done.6
  51.3 0.0 copy-start.7
  51.3 0.0 copy-start.8
  51.3 2.4 %convolution_add_fusion = f32[256,2048]{1,0:T(8,128)S(1)} fusion(bf16[1,512,2048]{2,1,0:T(8,128)(2,1)} %param.12, f32[2048]{0:T(1024)S(1)} %bitcast.56, bf16[256,640]{1,0:T(8,128)(2,1)} %bitcast.53), kind=kOutput, calls=%fused_computation.4 | convolution fusion | flops 537395200 | bytes 4464640 | tf_op jit(solution)/shard_map/dot_general | solution.py:39
  53.8 0.0 copy-done
  53.8 0.0 copy-done.7
  53.8 0.0 copy-done.8
  53.8 0.0 copy-start.3
  53.8 1.4 %convert_reduce_fusion.1 = (f32[512]{0:T(512)}, bf16[256,512]{1,0:T(8,128)(2,1)S(1)}) fusion(f32[256]{0:T(256)S(1)} %bitcast.60, bf16[32,8,512]{2,1,0:T(8,128)(2,1)S(1)} %copy-done.7, f32[512]{0:T(512)S(1)} %bitcast.61, bf16[1,2048,512]{2,1,0:T(8,128)(2,1)S(1)} %copy-done, f32[256,2048]{1,0:T(8,128)S(1)} %convolution_add_fusion), kind=kOutput, calls=%fused_computation.22 | convolution fusion | flops 540409344 | bytes 4723712 | tf_op jit(solution)/shard_map/dot_general | solution.py:41
  55.2 0.0 copy-done.3
  55.2 0.0 copy-start.2
  55.2 1.7 %convert_reduce_fusion = (f32[2048]{0:T(1024)}, bf16[256,2048]{1,0:T(8,128)(2,1)S(1)}) fusion(f32[256,2048]{1,0:T(8,128)S(1)} %convolution_add_fusion, bf16[256,512]{1,0:T(8,128)(2,1)S(1)} %get-tuple-element.17, bf16[1,2048,512]{2,1,0:T(8,128)(2,1)S(1)} %copy-done), kind=kOutput, calls=%fused_computation.13 | convolution fusion | flops 542636032 | bytes 5513216 | tf_op jit(solution)/shard_map/dot_general | solution.py:33
  56.9 0.0 copy-done.2
  56.9 1.5 %fusion.23.grad_ref = bf16[32,8,512]{2,1,0:T(8,128)(2,1)} fusion(bf16[256,2048]{1,0:T(8,128)(2,1)S(1)} %get-tuple-element.15, bf16[1,512,2048]{2,1,0:T(8,128)(2,1)S(1)} %copy-done.2), kind=kOutput, calls=%fused_computation.21 | convolution fusion | flops 537001984 | bytes 3407872 | tf_op jit(solution)/shard_map/dot_general | solution.py:33
  58.4 56.4 %shard_map.128 = bf16[8,4,80,512]{3,2,1,0:T(8,128)(2,1)} custom-call(bf16[32,8,512]{2,1,0:T(8,128)(2,1)} %fusion.23.grad_ref, bf16[128,256]{1,0:T(8,128)(2,1)} %fusion.29.unplace_ref, bf16[8,4,80,128]{3,2,1,0:T(8,128)(2,1)} %bitcast.55), custom_call_target="tpu_custom_call" | custom-call | tf_op jit(solution)/shard_map/pallas_call | solution.py:255
  114.8 0.0 copy-start.1
  114.8 4.6 %convolution_bitcast_fusion = f32[1,2048,512]{2,1,0:T(8,128)} fusion(bf16[256,512]{1,0:T(8,128)(2,1)S(1)} %get-tuple-element.17, f32[256,2048]{1,0:T(8,128)} %copy-done.3), kind=kOutput, calls=%fused_computation | convolution fusion | flops 539492352 | bytes 6553600 | tf_op jit(solution)/shard_map/dot_general | solution.py:27
  119.4 0.0 copy-done.1
  119.4 0.0 copy-start.4
  119.4 3.3 %bitcast_convert_fusion = f32[2560,512]{1,0:T(8,128)} fusion(bf16[8,4,80,512]{3,2,1,0:T(8,128)(2,1)S(1)} %copy-done.1), kind=kLoop, calls=%fused_computation.5 | loop fusion | flops 1310720 | bytes 7864320 | tf_op jit(solution)/shard_map/convert_element_type | solution.py:607
  122.6 0.0 copy-done.4
  122.6 0.0 copy-start.5
  122.6 2.8 %convolution_bitcast_fusion.1 = f32[1,512,2048]{2,1,0:T(8,128)} fusion(bf16[256,2048]{1,0:T(8,128)(2,1)S(1)} %get-tuple-element.15, bf16[256,640]{1,0:T(8,128)(2,1)S(1)} %bitcast.54), kind=kOutput, calls=%fused_computation.1 | convolution fusion | flops 536870912 | bytes 5505024 | tf_op jit(solution)/shard_map/dot_general | solution.py:27
  125.4 0.0 copy-done.5
  125.4 1.1 copy.18
  (1 shorter events, 0.0 us)
Async XLA Ops:
  0.6 53.2 %copy-start = (bf16[1,2048,512]{2,1,0:T(8,128)(2,1)S(1)}, bf16[1,2048,512]{2,1,0:T(8,128)(2,1)}, u32[]{:S(2)}) copy-start(bf16[1,2048,512]{2,1,0:T(8,128)(2,1)} %param.14) | copy-start | bytes 6291460
  6.2 45.2 %copy-start.6 = (f32[1,2048]{1,0:T(1,128)S(1)}, f32[1,2048]{1,0:T(1,128)}, u32[]{:S(2)}) copy-start(f32[1,2048]{1,0:T(1,128)} %param.13) | copy-start | bytes 24580
  51.3 2.5 %copy-start.7 = (bf16[32,8,512]{2,1,0:T(8,128)(2,1)S(1)}, bf16[32,8,512]{2,1,0:T(8,128)(2,1)}, u32[]{:S(2)}) copy-start(bf16[32,8,512]{2,1,0:T(8,128)(2,1)} %get-tuple-element.12) | copy-start | bytes 786436
  51.3 2.5 %copy-start.8 = (f32[1,512]{1,0:T(1,128)S(1)}, f32[1,512]{1,0:T(1,128)}, u32[]{:S(2)}) copy-start(f32[1,512]{1,0:T(1,128)} %param.15) | copy-start | bytes 6148
  53.8 1.4 %copy-start.3 = (f32[256,2048]{1,0:T(8,128)}, f32[256,2048]{1,0:T(8,128)S(1)}, u32[]{:S(2)}) copy-start(f32[256,2048]{1,0:T(8,128)S(1)} %convolution_add_fusion) | copy-start | bytes 6291460
  55.2 1.7 %copy-start.2 = (bf16[1,512,2048]{2,1,0:T(8,128)(2,1)S(1)}, bf16[1,512,2048]{2,1,0:T(8,128)(2,1)}, u32[]{:S(2)}) copy-start(bf16[1,512,2048]{2,1,0:T(8,128)(2,1)} %param.12) | copy-start | bytes 6291460
  114.8 4.6 %copy-start.1 = (bf16[8,4,80,512]{3,2,1,0:T(8,128)(2,1)S(1)}, bf16[8,4,80,512]{3,2,1,0:T(8,128)(2,1)}, u32[]{:S(2)}) copy-start(bf16[8,4,80,512]{3,2,1,0:T(8,128)(2,1)} %shard_map.128) | copy-start | bytes 7864324
  119.4 3.3 %copy-start.4 = (bf16[32,8,640]{2,1,0:T(8,128)(2,1)S(1)}, bf16[32,8,640]{2,1,0:T(8,128)(2,1)}, u32[]{:S(2)}) copy-start(bf16[32,8,640]{2,1,0:T(8,128)(2,1)} %get-tuple-element.11) | copy-start | bytes 983044
  122.6 2.8 %copy-start.5 = (f32[5,16,32,128]{3,2,1,0:T(8,128)S(1)}, f32[5,16,32,128]{3,2,1,0:T(8,128)}, u32[]{:S(2)}) copy-start(f32[5,16,32,128]{3,2,1,0:T(8,128)} %get-tuple-element.24) | copy-start | bytes 3932164

commit v3 on v2

v3 whole, which is shorter than its diff:
```python
import functools

import jax
import jax.numpy as jnp
from jax import lax
from jax.experimental import pallas as pl
from jax.experimental.pallas import tpu as pltpu
from jax.sharding import PartitionSpec as P

FIELDS = 5
PATCH = 8
STEPS = 3
BLOCK_ROWS = 2
PAD = 8
CHUNKS = 2
HIDDEN_TILE = 512


time_step = 0.2
viscosity = 0.5
drift_x = 0.6
drift_y = -0.4
drift_z = 0.3
error_weight = 0.0625


def contract_rows(left, right):
    return lax.dot_general(
        left, right, (((0,), (0,)), ((), ())), preferred_element_type=jnp.float32
    )


def contract_cols(left, right):
    return lax.dot_general(
        left, right, (((1,), (1,)), ((), ())), preferred_element_type=jnp.float32
    )


def my_place():
    return lax.axis_index("gx"), lax.axis_index("gy")


def remote(src, dst, send_sem, recv_sem, gx, gy):
    return pltpu.make_async_remote_copy(
        src_ref=src,
        dst_ref=dst,
        send_sem=send_sem,
        recv_sem=recv_sem,
        device_id=(gx, gy),
        device_id_type=pl.DeviceIdType.MESH,
    )


def step_kernel(
    gx_n,
    gy_n,
    fields_hbm,
    weight_hbm,
    owner_ref,
    lag_ref,
    first_hbm,
    first_bias_ref,
    second_hbm,
    second_bias_ref,
    out_ref,
    summed_ref,
    source_hbm,
    hidden_hbm,
    error_hbm,
    slope_hbm,
    state_0,
    state_1,
    state_2,
    face_out,
    face_in,
    swap,
    cells,
    turned,
    place,
    weight,
    first,
    second,
    source_out,
    source_in,
    target_out,
    target_in,
    feat_out,
    feats,
    source_rows,
    hidden,
    steep,
    error,
    slope,
    grad_out,
    back,
    shared,
    parts,
    landed,
    load_sem,
    save_sem,
    halo_send,
    halo_recv,
    source_send,
    source_recv,
    target_send,
    target_recv,
    feat_send,
    feat_recv,
    back_send,
    back_recv,
    share_send,
    share_recv,
    part_send,
    part_recv,
    line_send,
    plane_send,
    pair_send,
    out_recv,
):
    gx, gy = my_place()
    me = gx * gy_n + gy
    devices = gx_n * gy_n
    chips = gx_n // 2
    chip, core = gx // 2, lax.rem(gx, 2)
    partner = gx + 1 - 2 * core
    states = (state_0, state_1, state_2)
    _, size_x, size_y, size_z = fields_hbm.shape
    inner = pl.ds(PAD, size_y)
    embed = weight.shape[1]
    slot_rows = source_out.shape[1]
    count_x, count_y, count_z = lag_ref.shape
    columns = count_x * count_y
    kinds = FIELDS * PATCH * PATCH
    rows = turned.shape[1]
    hidden_n = hidden.shape[1]
    width = embed // CHUNKS
    f32, bf16 = jnp.float32, jnp.bfloat16

    loads = [
        pltpu.make_async_copy(
            fields_hbm, state_0.at[:, pl.ds(2, size_x), inner, :], load_sem.at[0]
        ),
        pltpu.make_async_copy(weight_hbm, weight, load_sem.at[1]),
        pltpu.make_async_copy(first_hbm.at[0], first, load_sem.at[2]),
        pltpu.make_async_copy(second_hbm.at[0], second, load_sem.at[3]),
    ]
    for load in loads:
        load.start()

    edges = ((gx > 0, 0), (gx < gx_n - 1, 1), (gy > 0, 2), (gy < gy_n - 1, 3))
    for state in states:
        for inside, side in edges:
            @pl.when(jnp.logical_not(inside))
            def _():
                if side < 2:
                    plane = pl.ds(0 if side == 0 else size_x + 2, 2)
                    state[:, plane, inner, :] = jnp.zeros((FIELDS, 2, size_y, size_z), jnp.float32)
                else:
                    strip = pl.ds(0 if side == 2 else PAD + size_y, PAD)
                    state[:, pl.ds(2, size_x), strip, :] = jnp.zeros(
                        (FIELDS, size_x, PAD, size_z), jnp.float32
                    )

    barrier = pltpu.get_barrier_semaphore()

    def greet(step, carry):
        other = lax.rem(me + step, devices)
        pl.semaphore_signal(
            barrier,
            inc=1,
            device_id=(other // gy_n, lax.rem(other, gy_n)),
            device_id_type=pl.DeviceIdType.MESH,
        )
        return carry

    lax.fori_loop(1, devices, greet, 0)
    place_of = lax.broadcasted_iota(jnp.int32, (size_z, PATCH * rows), 1)
    column_of = lax.rem(place_of, rows) // count_z
    cell_of = column_of * size_z + lax.rem(place_of, count_z) * PATCH + place_of // rows
    for column in range(columns):
        row_of = lax.broadcasted_iota(jnp.int32, (size_z, PATCH * rows), 0) + column * size_z
        swap[pl.ds(column * size_z, size_z), :] = jnp.where(row_of == cell_of, 1.0, 0.0).astype(
            jnp.bfloat16
        )

    owner = owner_ref[...].astype(f32)
    blocks = owner.shape[1]
    tall = lax.broadcasted_iota(jnp.int32, (devices, blocks), 0).astype(f32)
    onehot = jnp.where(owner == tall, 1.0, 0.0)
    before = jnp.where(
        lax.broadcasted_iota(jnp.int32, (blocks, blocks), 0)
        < lax.broadcasted_iota(jnp.int32, (blocks, blocks), 1),
        1.0,
        0.0,
    )
    ahead = jnp.dot(onehot.astype(bf16), before.astype(bf16), preferred_element_type=f32)
    rank = jnp.sum(ahead * onehot, axis=0, keepdims=True)
    block_slot = owner * float(slot_rows // BLOCK_ROWS) + rank
    slots = place.shape[0]
    slot_block = lax.broadcasted_iota(jnp.int32, (slots, blocks), 0) // BLOCK_ROWS
    block_place = jnp.where(block_slot == slot_block.astype(f32), 1.0, 0.0)
    spread_rows = jnp.where(
        lax.broadcasted_iota(jnp.int32, (blocks, rows), 1) // BLOCK_ROWS
        == lax.broadcasted_iota(jnp.int32, (blocks, rows), 0),
        1.0,
        0.0,
    )
    row_place = jnp.dot(
        block_place.astype(bf16), spread_rows.astype(bf16), preferred_element_type=f32
    )
    same = lax.rem(lax.broadcasted_iota(jnp.int32, (slots, rows), 0), BLOCK_ROWS) == lax.rem(
        lax.broadcasted_iota(jnp.int32, (slots, rows), 1), BLOCK_ROWS
    )
    place[...] = jnp.where(same, row_place, 0.0).astype(bf16)
    pl.semaphore_wait(barrier, devices - 1)

    def halo_copy(step, side):
        state = states[step]
        if side == 0:
            src, dst = state.at[:, pl.ds(2, 2), inner], state.at[:, pl.ds(size_x + 2, 2), inner]
            target = (gx - 1, gy)
        elif side == 1:
            src, dst = state.at[:, pl.ds(size_x, 2), inner], state.at[:, pl.ds(0, 2), inner]
            target = (gx + 1, gy)
        else:
            src, dst = face_out.at[step, side - 2], face_in.at[step, 3 - side]
            target = (gx, gy - 1 if side == 2 else gy + 1)
        return remote(
            src, dst, halo_send.at[step, side], halo_recv.at[step, side ^ 1], *target
        )

    def halo_start(step):
        state = states[step]
        for side in (2, 3):
            first = PAD if side == 2 else PAD + size_y - 2
            face_out[step, side - 2] = state[:, pl.ds(2, size_x), pl.ds(first, 2), :]
        for inside, side in edges:
            @pl.when(inside)
            def _():
                halo_copy(step, side).start()

    def halo_wait(step):
        state = states[step]
        for inside, side in edges:
            @pl.when(inside)
            def _():
                copy = halo_copy(step, side)
                copy.wait_send()
                remote(
                    face_in.at[step, 0] if side > 1 else state.at[:, pl.ds(0, 2), inner],
                    face_in.at[step, 0] if side > 1 else state.at[:, pl.ds(0, 2), inner],
                    halo_send.at[step, side],
                    halo_recv.at[step, side],
                    gx,
                    gy,
                ).wait_recv()
                if side > 1:
                    first = PAD - 2 if side == 2 else PAD + size_y
                    state[:, pl.ds(2, size_x), pl.ds(first, 2), :] = face_in[step, side - 2]

    lane = lax.broadcasted_iota(jnp.int32, (size_y, size_z), 1)

    def advance_state(step):
        state = states[step]

        def plane(i, carry):
            def pieces(field):
                middle = state[field, i + 2, inner, :]
                around = []
                around.append([state[field, i + k, inner, :] for k in (0, 1, 3, 4)])
                around.append(
                    [state[field, i + 2, pl.ds(PAD + k, size_y), :] for k in (-2, -1, 1, 2)]
                )
                around.append(
                    [
                        jnp.where(lane < 2, 0.0, pltpu.roll(middle, 2, 1)),
                        jnp.where(lane < 1, 0.0, pltpu.roll(middle, 1, 1)),
                        jnp.where(lane >= size_z - 1, 0.0, pltpu.roll(middle, size_z - 1, 1)),
                        jnp.where(lane >= size_z - 2, 0.0, pltpu.roll(middle, size_z - 2, 1)),
                    ]
                )
                slopes = [(a - d) + 8.0 * (c - b) for a, b, c, d in around]
                near = sum(b + c for a, b, c, d in around)
                far = sum(a + d for a, b, c, d in around)
                change = viscosity * (16.0 * near - far - 90.0 * middle)
                change = change - (
                    drift_x * slopes[0] + drift_y * slopes[1] + drift_z * slopes[2]
                )
                return middle, slopes, change

            def put(field, value):
                if step < STEPS - 1:
                    states[step + 1][field, i + 2, inner, :] = value
                else:
                    out_ref[field, i] = value

            scale = time_step / 12.0
            middle_p, slopes_p, change_p = pieces(4)
            spread = 0.0
            for axis in range(3):
                middle, slopes, change = pieces(1 + axis)
                spread = spread + slopes[axis]
                put(1 + axis, middle + scale * (change - slopes_p[axis]))
            put(4, middle_p + scale * (change_p - spread))
            middle, slopes, change = pieces(0)
            put(0, middle + scale * (change - spread))
            return carry

        lax.fori_loop(0, size_x, plane, 0)


    def column_cells(state, offset_x, offset_y, column):
        first_x = offset_x + column // count_y * PATCH
        first_y = offset_y + column % count_y * PATCH
        return state[:, pl.ds(first_x, PATCH), pl.ds(first_y, PATCH), :].reshape(kinds, size_z)

    def turn_cells():
        for offset in range(PATCH):
            turned[pl.ds(offset, kinds, stride=PATCH), :] = jnp.dot(
                cells[...],
                swap[:, pl.ds(offset * rows, rows)],
                preferred_element_type=f32,
            )

    def embed_rows():
        return contract_rows(turned[...].astype(bf16), weight[...]).astype(bf16)

    def scatter(step, stage, landing, send_sem, recv_sem):
        other = lax.rem(me + step, devices)
        return remote(
            stage.at[other],
            landing.at[me],
            send_sem.at[step],
            recv_sem.at[step],
            other // gy_n,
            lax.rem(other, gy_n),
        )

    def scatter_start(stage, landing, *sems):
        def start(step, carry):
            scatter(step, stage, landing, *sems).start()
            return carry

        lax.fori_loop(1, devices, start, 0)
        landing[me] = stage[me]

    def scatter_wait(*args):
        def wait(step, carry):
            scatter(step, *args).wait()
            return carry

        lax.fori_loop(1, devices, wait, 0)

    def put_rows(values, stage):
        packed = jnp.dot(place[...], values, preferred_element_type=f32)
        stage[...] = packed.reshape(stage.shape).astype(bf16)

    loads[0].wait()
    halo_start(0)
    halo_wait(0)
    advance_state(0)
    halo_start(1)
    halo_wait(1)
    advance_state(1)
    halo_start(2)
    stretch = jnp.where(
        lax.broadcasted_iota(jnp.int32, (count_z, size_z), 1) // PATCH
        == lax.broadcasted_iota(jnp.int32, (count_z, size_z), 0),
        1.0,
        0.0,
    ).astype(bf16)
    for column_x in range(count_x):
        lag = lag_ref[column_x].astype(f32).astype(bf16)
        lag = jnp.dot(lag, stretch, preferred_element_type=f32)
        for column_y in range(count_y):
            column = column_x * count_y + column_y
            early = column_cells(state_1, 2, PAD, column)
            late = column_cells(state_2, 2, PAD, column)
            chosen = jnp.where(lag[column_y : column_y + 1, :] > 0.5, late, early)
            cells[:, pl.ds(column * size_z, size_z)] = chosen.astype(bf16)
    turn_cells()
    loads[1].wait()
    source = embed_rows()
    source_args = (source_out, source_in, source_send, source_recv)
    ones = jnp.ones((rows, source_out.shape[2] - embed), bf16)
    put_rows(jnp.concatenate([source, ones], axis=1), source_out)
    scatter_start(*source_args)

    part_rows = feats.shape[2]
    for block in range(devices):
        feat_out[block // gy_n, block % gy_n] = turned[
            pl.ds(block * part_rows, part_rows), :
        ].astype(bf16)

    def feat_copy(step):
        other = lax.rem(gx + step, gx_n)
        return remote(
            feat_out.at[other], feats.at[gx], feat_send.at[step], feat_recv.at[step], other, gy
        )

    for step in range(1, gx_n):
        feat_copy(step).start()
    feats[gx] = feat_out[gx]

    halo_wait(2)
    advance_state(2)
    for column in range(columns):
        cells[:, pl.ds(column * size_z, size_z)] = column_cells(out_ref, 0, 0, column).astype(bf16)
    turn_cells()
    target_args = (target_out, target_in, target_send, target_recv)
    put_rows(embed_rows(), target_out)
    scatter_start(*target_args)

    scatter_wait(*source_args)
    got = source_in[...].astype(f32).reshape(slots, source_in.shape[2])
    source_rows[...] = got[:, :embed].astype(bf16)
    valid = got[:, embed : embed + 1]
    loads[2].wait()
    loads[3].wait()
    predict = jnp.zeros((slots, embed), f32) + second_bias_ref[...]
    for tile in range(0, hidden_n, HIDDEN_TILE):
        part = pl.ds(tile, HIDDEN_TILE)
        pre = jnp.dot(source_rows[...], first[:, part], preferred_element_type=f32)
        pre = pre + first_bias_ref[:, part]
        sigma = jax.nn.sigmoid(pre)
        units = (pre * sigma).astype(bf16)
        hidden[:, part] = units
        steep[:, part] = sigma * (1.0 + pre * (1.0 - sigma))
        predict = predict + jnp.dot(units, second[part, :], preferred_element_type=f32)
    scatter_wait(*target_args)
    wanted = target_in[...].astype(f32).reshape(slots, embed)
    error[...] = (error_weight * (predict - wanted) * valid).astype(bf16)
    for tile in range(0, hidden_n, HIDDEN_TILE):
        part = pl.ds(tile, HIDDEN_TILE)
        slope[:, part] = (contract_cols(error[...], second[part, :]) * steep[:, part]).astype(bf16)
    for chunk in range(CHUNKS):
        grad = contract_cols(slope[...], first[pl.ds(chunk * width, width), :])
        grad_out[chunk] = grad.reshape(devices, slot_rows, width).astype(bf16)
        scatter_start(
            grad_out.at[chunk], back.at[chunk], back_send.at[chunk], back_recv.at[chunk]
        )
    saves = [
        pltpu.make_async_copy(source_rows, source_hbm, save_sem.at[0]),
        pltpu.make_async_copy(hidden, hidden_hbm, save_sem.at[1]),
        pltpu.make_async_copy(error, error_hbm, save_sem.at[2]),
        pltpu.make_async_copy(slope, slope_hbm, save_sem.at[3]),
    ]
    for save in saves:
        save.start()

    def chip_at(step):
        return lax.rem(chip + step, chips) * 2 + core

    sends = []

    def send(copy):
        copy.start()
        sends.append(copy)

    def share_copy(chunk, origin, target, slot):
        block = shared.at[chunk, origin]
        return remote(
            block, block, share_send.at[chunk, slot], share_recv.at[chunk, origin], target, gy
        )

    for chunk in range(CHUNKS):
        scatter_wait(
            grad_out.at[chunk], back.at[chunk], back_send.at[chunk], back_recv.at[chunk]
        )
        packed = back[chunk].astype(f32).reshape(slots, width).astype(bf16)
        mine = contract_rows(place[...], packed)
        shared[chunk, gx] = mine.astype(bf16)
        for step in range(1, chips):
            send(share_copy(chunk, gx, chip_at(step), step))
        send(share_copy(chunk, gx, partner, 0))

    for step in range(1, gx_n):
        feat_copy(step).wait()

    def part_of(chunk, block):
        total = jnp.zeros((part_rows, width), f32)
        for origin in range(gx_n):
            total = total + jnp.dot(
                feats[origin, block], shared[chunk, origin], preferred_element_type=f32
            )
        return total

    def part_copy(chunk, step):
        other = lax.rem(gy + step, gy_n)
        return remote(
            parts.at[chunk, other],
            landed.at[chunk, step],
            part_send.at[chunk, step],
            part_recv.at[chunk, step],
            gx,
            other,
        )

    own = []
    for chunk in range(CHUNKS):
        for step in range(1, chips):
            origin = chip_at(chips - step)
            share_copy(chunk, origin, partner, chips + step).wait_recv()
            send(share_copy(chunk, origin, partner, chips + step))
        for step in range(chips):
            share_copy(chunk, chip_at(step) + 1 - 2 * core, partner, 0).wait_recv()
        for step in range(1, gy_n):
            other = lax.rem(gy + step, gy_n)
            parts[chunk, other] = part_of(chunk, other).astype(bf16)
            part_copy(chunk, step).start()
        own.append(part_of(chunk, gy))

    def out_copy(chunk, block_x, block_y, send_sem, target_x, target_y):
        block = summed_ref.at[chunk, block_x, block_y]
        return remote(
            block, block, send_sem, out_recv.at[chunk, block_x, block_y], target_x, target_y
        )

    def out_wait(chunk, block_x, block_y):
        out_copy(chunk, block_x, block_y, line_send.at[0, 0], partner, gy).wait_recv()

    for chunk in range(CHUNKS):
        total = own[chunk]
        for step in range(1, gy_n):
            part_copy(chunk, step).wait()
            total = total + landed[chunk, step].astype(f32)
        summed_ref[chunk, gx, gy] = total.astype(bf16)
        for step in range(1, gy_n):
            other = lax.rem(gy + step, gy_n)
            send(out_copy(chunk, gx, gy, line_send.at[chunk, step], gx, other))
        for step in range(1, chips):
            send(out_copy(chunk, gx, gy, plane_send.at[chunk, 0, step], chip_at(step), gy))
        send(out_copy(chunk, gx, gy, pair_send.at[chunk, 0, 0], partner, gy))
    for chunk in range(CHUNKS):
        for line in range(1, gy_n):
            block_y = lax.rem(gy + line, gy_n)
            out_wait(chunk, gx, block_y)
            for step in range(1, chips):
                send(
                    out_copy(
                        chunk, gx, block_y, plane_send.at[chunk, line, step], chip_at(step), gy
                    )
                )
            send(out_copy(chunk, gx, block_y, pair_send.at[chunk, line, 0], partner, gy))
    for chunk in range(CHUNKS):
        for line in range(gy_n):
            block_y = lax.rem(gy + line, gy_n)
            for step in range(1, chips):
                block_x = chip_at(step)
                out_wait(chunk, block_x, block_y)
                send(
                    out_copy(
                        chunk, block_x, block_y, pair_send.at[chunk, line, step], partner, gy
                    )
                )
    for chunk in range(CHUNKS):
        for line in range(gy_n):
            for step in range(chips):
                out_wait(chunk, chip_at(step) + 1 - 2 * core, line)
    for copy in sends:
        copy.wait_send()
    for save in saves:
        save.wait()


def finish_kernel(source_ref, hidden_ref, error_ref, slope_ref, summed_ref, *outs):
    first_ref, first_bias_ref, second_ref, second_bias_ref, patch_ref = outs
    error, slope = error_ref[...], slope_ref[...]
    first_ref[0] = contract_rows(source_ref[...], slope)
    first_bias_ref[...] = jnp.sum(slope.astype(jnp.float32), axis=0, keepdims=True)
    second_ref[0] = contract_rows(hidden_ref[...], error)
    second_bias_ref[...] = jnp.sum(error.astype(jnp.float32), axis=0, keepdims=True)
    width = summed_ref.shape[2]
    for chunk in range(summed_ref.shape[0]):
        patch_ref[:, chunk * width : (chunk + 1) * width] = summed_ref[chunk].astype(jnp.float32)


def finish(source, hidden, error, slope, summed):
    slots, embed = source.shape
    hidden_n = hidden.shape[1]
    features, width = summed.shape[1], summed.shape[2]
    steps = hidden_n // HIDDEN_TILE
    f32 = jnp.float32
    return pl.pallas_call(
        finish_kernel,
        grid=(steps,),
        out_shape=[
            jax.ShapeDtypeStruct((1, embed, hidden_n), f32),
            jax.ShapeDtypeStruct((1, hidden_n), f32),
            jax.ShapeDtypeStruct((1, hidden_n, embed), f32),
            jax.ShapeDtypeStruct((1, embed), f32),
            jax.ShapeDtypeStruct((features, embed), f32),
        ],
        in_specs=[
            pl.BlockSpec((slots, embed), lambda i: (0, 0)),
            pl.BlockSpec((slots, HIDDEN_TILE), lambda i: (0, i)),
            pl.BlockSpec((slots, embed), lambda i: (0, 0)),
            pl.BlockSpec((slots, HIDDEN_TILE), lambda i: (0, i)),
            pl.BlockSpec((CHUNKS, features // steps, width), lambda i: (0, i, 0)),
        ],
        out_specs=[
            pl.BlockSpec((1, embed, HIDDEN_TILE), lambda i: (0, 0, i)),
            pl.BlockSpec((1, HIDDEN_TILE), lambda i: (0, i)),
            pl.BlockSpec((1, HIDDEN_TILE, embed), lambda i: (0, i, 0)),
            pl.BlockSpec((1, embed), lambda i: (0, 0)),
            pl.BlockSpec((features // steps, embed), lambda i: (i, 0)),
        ],
    )(source, hidden, error, slope, summed)


def per_device(fields, patch_weight, trainer_of, lag_index, w_in, b_in, w_out, b_out):
    gx_n, gy_n = lax.axis_size("gx"), lax.axis_size("gy")
    devices, chips = gx_n * gy_n, gx_n // 2
    fields_n, size_x, size_y, size_z = fields.shape
    features, embed = patch_weight.shape
    hidden_n = w_in.shape[2]
    rows = lag_index.size
    blocks = rows // BLOCK_ROWS
    slot_rows = max(8, 2 * blocks // devices * BLOCK_ROWS)
    slots = devices * slot_rows
    columns = lag_index.shape[0] * lag_index.shape[1]
    part_rows = features // devices
    width = embed // CHUNKS
    bf16, f32 = jnp.bfloat16, jnp.float32
    dma = pltpu.SemaphoreType.DMA
    vmem = pltpu.VMEM
    whole = pl.BlockSpec(memory_space=pltpu.VMEM)
    anywhere = pl.BlockSpec(memory_space=pl.ANY)
    padded = (fields_n, size_x + 4, size_y + 2 * PAD, size_z)
    faces = (STEPS, 2, fields_n, size_x, 2, size_z)
    source_shape = (devices, slot_rows, embed + 128)
    target_shape = (devices, slot_rows, embed)
    feat_shape = (gx_n, gy_n, part_rows, rows)
    block_shape = (CHUNKS, gx_n, gy_n, part_rows, width)
    new_fields, summed, source, hidden, error, slope = pl.pallas_call(
        functools.partial(step_kernel, gx_n, gy_n),
        out_shape=[
            jax.ShapeDtypeStruct(fields.shape, f32),
            jax.ShapeDtypeStruct(block_shape, bf16),
            jax.ShapeDtypeStruct((slots, embed), bf16),
            jax.ShapeDtypeStruct((slots, hidden_n), bf16),
            jax.ShapeDtypeStruct((slots, embed), bf16),
            jax.ShapeDtypeStruct((slots, hidden_n), bf16),
        ],
        in_specs=[anywhere, anywhere, whole, whole, anywhere, whole, anywhere, whole],
        out_specs=[whole, whole] + [anywhere] * 4,
        scratch_shapes=[
            vmem(padded, f32),
            vmem(padded, f32),
            vmem(padded, f32),
            vmem(faces, f32),
            vmem(faces, f32),
            vmem((columns * size_z, PATCH * rows), bf16),
            vmem((features // PATCH, columns * size_z), bf16),
            vmem((features, rows), f32),
            vmem((slots, rows), bf16),
            vmem((features, embed), bf16),
            vmem((embed, hidden_n), bf16),
            vmem((hidden_n, embed), bf16),
            vmem(source_shape, bf16),
            vmem(source_shape, bf16),
            vmem(target_shape, bf16),
            vmem(target_shape, bf16),
            vmem(feat_shape, bf16),
            vmem(feat_shape, bf16),
            vmem((slots, embed), bf16),
            vmem((slots, hidden_n), bf16),
            vmem((slots, hidden_n), f32),
            vmem((slots, embed), bf16),
            vmem((slots, hidden_n), bf16),
            vmem((CHUNKS, devices, slot_rows, width), bf16),
            vmem((CHUNKS, devices, slot_rows, width), bf16),
            vmem((CHUNKS, gx_n, rows, width), bf16),
            vmem((CHUNKS, gy_n, part_rows, width), bf16),
            vmem((CHUNKS, gy_n, part_rows, width), bf16),
            dma((4,)),
            dma((4,)),
            dma((STEPS, 4)),
            dma((STEPS, 4)),
            dma((devices,)),
            dma((devices,)),
            dma((devices,)),
            dma((devices,)),
            dma((gx_n,)),
            dma((gx_n,)),
            dma((CHUNKS, devices)),
            dma((CHUNKS, devices)),
            dma((CHUNKS, 2 * chips)),
            dma((CHUNKS, gx_n)),
            dma((CHUNKS, gy_n)),
            dma((CHUNKS, gy_n)),
            dma((CHUNKS, gy_n)),
            dma((CHUNKS, gy_n, chips)),
            dma((CHUNKS, gy_n, chips)),
            dma((CHUNKS, gx_n, gy_n)),
        ],
        compiler_params=pltpu.CompilerParams(
            collective_id=0, has_side_effects=True, vmem_limit_bytes=62 * 1024 * 1024
        ),
    )(fields, patch_weight, trainer_of.T, lag_index, w_in, b_in, w_out, b_out)
    first_grad, first_bias_grad, second_grad, second_bias_grad, patch_gradient = finish(
        source, hidden, error, slope, summed.reshape(CHUNKS, features, width)
    )
    return (
        new_fields,
        patch_gradient,
        first_grad,
        first_bias_grad,
        second_grad,
        second_bias_grad,
    )


def solution(mesh):
    in_specs = (
        P(None, "gx", "gy", None),
        P(),
        P(("gx", "gy"), None),
        P("gx", "gy", None),
        P(("gx", "gy"), None, None),
        P(("gx", "gy"), None),
        P(("gx", "gy"), None, None),
        P(("gx", "gy"), None),
    )
    out_specs = (
        P(None, "gx", "gy", None),
        P(),
        P(("gx", "gy"), None, None),
        P(("gx", "gy"), None),
        P(("gx", "gy"), None, None),
        P(("gx", "gy"), None),
    )
    return jax.shard_map(
        per_device, mesh=mesh, in_specs=in_specs, out_specs=out_specs, check_vma=False
    )
```

time: 127 us -> 99.1 us (0.78)
  the two profiles are of different devices: /device:TPU:0 before, /device:TPU:9 now
where the time goes in v3:
time: 99.1 us; the launch traced here: 98.8 us
  Pallas kernels  97.1 us (98%)
  local copies, waits for them, and re-layouts  1.06 us (1%)
    pallas_call x1, Pallas kernels, per_device(): pl.pallas_call(functools.partial(step_kernel, gx_n, gy_n), out_shape=[jax...  89.4 us
    pallas_call x1, Pallas kernels, finish(): pl.pallas_call(finish_kernel, grid=(steps,), out_shape=[jax.ShapeDtypeStr...  7.75 us

profile of v3, /device:TPU:9, one launch (start us, length us, event | category | flops | bytes accessed | tf_op | source)
XLA Modules:
  0.0 98.8 jit_solution(13927085389160118567)
XLA Ops:
  0.6 89.4 %shard_map.127 = (f32[5,16,32,128]{3,2,1,0:T(8,128)}, bf16[2,8,4,80,256]{4,3,2,1,0:T(8,128)(2,1)}, bf16[256,512]{1,0:T(8,128)(2,1)}, bf16[256,2048]{1,0:T(8,128)...) custom-call(f32[5,16,32,128]{3,2,1,0:T(8,128)} %fields_hbm.1, bf16[2560,512]{1,0:T(8,128)(2,1)} %weight_hbm.1, ...), custom_call_target="tpu_custom_call" | custom-call | tf_op jit(solution)/shard_map/pallas_call | solution.py:635
  90.0 0.0 copy-start
  90.0 7.8 %shard_map.128 = (f32[1,512,2048]{2,1,0:T(8,128)}, f32[1,2048]{1,0:T(1,128)}, f32[1,2048,512]{2,1,0:T(8,128)}, f32[1,512]{1,0:T(1,128)}, f32[2560,512]{1,0:T(8,128)}) custom-call(bf16[256,512]{1,0:T(8,128)(2,1)} %get-tuple-element.18.source_ref, bf16[256,2048]{1,0:T(8,128)(2,1)} %get-tuple-element.19.hidden_ref, ...), custom_call_target="tpu_custom_call" | custom-call | tf_op jit(solution)/shard_map/pallas_call | solution.py:584
  97.8 0.0 copy-done
  97.8 1.1 %copy.15 = f32[5,16,32,128]{3,2,1,0:T(8,128)} copy(f32[5,16,32,128]{3,2,1,0:T(8,128)S(1)} %copy-done) | data formatting | bytes 2621440
Async XLA Ops:
  90.0 7.8 %copy-start = (f32[5,16,32,128]{3,2,1,0:T(8,128)S(1)}, f32[5,16,32,128]{3,2,1,0:T(8,128)}, u32[]{:S(2)}) copy-start(f32[5,16,32,128]{3,2,1,0:T(8,128)} %get-tuple-element.34) | copy-start | bytes 3932164

commit v4 on v3

--- a/solution.py
+++ b/solution.py
@@ -13,6 +13,7 @@
 BLOCK_ROWS = 2
 PAD = 8
 CHUNKS = 2
+BACK_CHUNKS = 2
 HIDDEN_TILE = 512
 
 
@@ -38,6 +39,15 @@
 
 def my_place():
     return lax.axis_index("gx"), lax.axis_index("gy")
+
+
+def across(place, step):
+    bit = 1
+    while bit <= step:
+        if step & bit:
+            place = place + bit - 2 * bit * lax.rem(place // bit, 2)
+        bit *= 2
+    return place
 
 
 def remote(src, dst, send_sem, recv_sem, gx, gy):
@@ -62,8 +72,8 @@
     first_bias_ref,
     second_hbm,
     second_bias_ref,
-    out_ref,
-    summed_ref,
+    fields_out_hbm,
+    summed_hbm,
     source_hbm,
     hidden_hbm,
     error_hbm,
@@ -71,6 +81,10 @@
     state_0,
     state_1,
     state_2,
+    out_ref,
+    summed_ref,
+    valid_out,
+    valid_in,
     face_out,
     face_in,
     swap,
@@ -98,16 +112,14 @@
     landed,
     load_sem,
     save_sem,
+    valid_sems,
     halo_send,
     halo_recv,
-    source_send,
-    source_recv,
-    target_send,
-    target_recv,
+    source_sems,
+    target_sems,
     feat_send,
     feat_recv,
-    back_send,
-    back_recv,
+    back_sems,
     share_send,
     share_recv,
     part_send,
@@ -258,18 +270,18 @@
                     first = PAD - 2 if side == 2 else PAD + size_y
                     state[:, pl.ds(2, size_x), pl.ds(first, 2), :] = face_in[step, side - 2]
 
-    lane = lax.broadcasted_iota(jnp.int32, (size_y, size_z), 1)
-
-    def advance_state(step):
+    def advance_part(step, first_plane, planes, first_row, count):
         state = states[step]
+        lane = lax.broadcasted_iota(jnp.int32, (count, size_z), 1)
+        here = pl.ds(PAD + first_row, count)
 
         def plane(i, carry):
             def pieces(field):
-                middle = state[field, i + 2, inner, :]
+                middle = state[field, i + 2, here, :]
                 around = []
-                around.append([state[field, i + k, inner, :] for k in (0, 1, 3, 4)])
+                around.append([state[field, i + k, here, :] for k in (0, 1, 3, 4)])
                 around.append(
-                    [state[field, i + 2, pl.ds(PAD + k, size_y), :] for k in (-2, -1, 1, 2)]
+                    [state[field, i + 2, pl.ds(PAD + first_row + k, count), :] for k in (-2, -1, 1, 2)]
                 )
                 around.append(
                     [
@@ -290,9 +302,9 @@
 
             def put(field, value):
                 if step < STEPS - 1:
-                    states[step + 1][field, i + 2, inner, :] = value
+                    states[step + 1][field, i + 2, here, :] = value
                 else:
-                    out_ref[field, i] = value
+                    out_ref[field, i, pl.ds(first_row, count), :] = value
 
             scale = time_step / 12.0
             middle_p, slopes_p, change_p = pieces(4)
@@ -306,7 +318,16 @@
             put(0, middle + scale * (change - spread))
             return carry
 
-        lax.fori_loop(0, size_x, plane, 0)
+        lax.fori_loop(first_plane, first_plane + planes, plane, 0)
+
+    def advance_inside(step):
+        advance_part(step, 2, size_x - 4, PAD, size_y - 2 * PAD)
+
+    def advance_edges(step):
+        advance_part(step, 0, 2, 0, size_y)
+        advance_part(step, size_x - 2, 2, 0, size_y)
+        advance_part(step, 2, size_x - 4, 0, PAD)
+        advance_part(step, 2, size_x - 4, size_y - PAD, PAD)
 
 
     def column_cells(state, offset_x, offset_y, column):
@@ -325,31 +346,34 @@
     def embed_rows():
         return contract_rows(turned[...].astype(bf16), weight[...]).astype(bf16)
 
-    def scatter(step, stage, landing, send_sem, recv_sem):
+    def scatter(step, stage, landing, sems):
         other = lax.rem(me + step, devices)
         return remote(
             stage.at[other],
             landing.at[me],
-            send_sem.at[step],
-            recv_sem.at[step],
+            sems.at[0],
+            sems.at[1],
             other // gy_n,
             lax.rem(other, gy_n),
         )
 
-    def scatter_start(stage, landing, *sems):
+    def scatter_start(stage, landing, sems):
         def start(step, carry):
-            scatter(step, stage, landing, *sems).start()
+            scatter(step, stage, landing, sems).start()
             return carry
 
         lax.fori_loop(1, devices, start, 0)
         landing[me] = stage[me]
 
+    def scatter_all(stage, landing, sems):
+        others = pl.ds(0, devices - 1)
+        return remote(stage.at[others], landing.at[others], sems.at[0], sems.at[1], partner, gy)
+
     def scatter_wait(*args):
-        def wait(step, carry):
-            scatter(step, *args).wait()
-            return carry
-
-        lax.fori_loop(1, devices, wait, 0)
+        scatter_all(*args).wait_recv()
+        unsent.append(scatter_all(*args))
+
+    unsent = []
 
     def put_rows(values, stage):
         packed = jnp.dot(place[...], values, preferred_element_type=f32)
@@ -357,11 +381,16 @@
 
     loads[0].wait()
     halo_start(0)
+    filled = jnp.sum(place[...].astype(f32), axis=1, keepdims=True)
+    filled = jnp.broadcast_to(filled, (slots, valid_out.shape[2]))
+    valid_out[...] = filled.reshape(valid_out.shape).astype(bf16)
+    valid_args = (valid_out, valid_in, valid_sems)
+    scatter_start(*valid_args)
     halo_wait(0)
-    advance_state(0)
+    advance_part(0, 0, size_x, 0, size_y)
     halo_start(1)
     halo_wait(1)
-    advance_state(1)
+    advance_part(1, 0, size_x, 0, size_y)
     halo_start(2)
     stretch = jnp.where(
         lax.broadcasted_iota(jnp.int32, (count_z, size_z), 1) // PATCH
@@ -381,9 +410,8 @@
     turn_cells()
     loads[1].wait()
     source = embed_rows()
-    source_args = (source_out, source_in, source_send, source_recv)
-    ones = jnp.ones((rows, source_out.shape[2] - embed), bf16)
-    put_rows(jnp.concatenate([source, ones], axis=1), source_out)
+    source_args = (source_out, source_in, source_sems)
+    put_rows(source, source_out)
     scatter_start(*source_args)
 
     part_rows = feats.shape[2]
@@ -398,23 +426,24 @@
             feat_out.at[other], feats.at[gx], feat_send.at[step], feat_recv.at[step], other, gy
         )
 
+    halo_wait(2)
+    advance_part(2, 0, size_x, 0, size_y)
+    saves = [pltpu.make_async_copy(out_ref, fields_out_hbm, save_sem.at[4])]
+    saves[0].start()
+    for column in range(columns):
+        cells[:, pl.ds(column * size_z, size_z)] = column_cells(out_ref, 0, 0, column).astype(bf16)
+    turn_cells()
+    target_args = (target_out, target_in, target_sems)
+    put_rows(embed_rows(), target_out)
+    scatter_start(*target_args)
     for step in range(1, gx_n):
         feat_copy(step).start()
     feats[gx] = feat_out[gx]
 
-    halo_wait(2)
-    advance_state(2)
-    for column in range(columns):
-        cells[:, pl.ds(column * size_z, size_z)] = column_cells(out_ref, 0, 0, column).astype(bf16)
-    turn_cells()
-    target_args = (target_out, target_in, target_send, target_recv)
-    put_rows(embed_rows(), target_out)
-    scatter_start(*target_args)
-
     scatter_wait(*source_args)
-    got = source_in[...].astype(f32).reshape(slots, source_in.shape[2])
-    source_rows[...] = got[:, :embed].astype(bf16)
-    valid = got[:, embed : embed + 1]
+    source_rows[...] = source_in[...].astype(f32).reshape(slots, embed).astype(bf16)
+    scatter_wait(*valid_args)
+    valid = valid_in[...].astype(f32).reshape(slots, valid_in.shape[2])[:, 0:1]
     loads[2].wait()
     loads[3].wait()
     predict = jnp.zeros((slots, embed), f32) + second_bias_ref[...]
@@ -433,23 +462,23 @@
     for tile in range(0, hidden_n, HIDDEN_TILE):
         part = pl.ds(tile, HIDDEN_TILE)
         slope[:, part] = (contract_cols(error[...], second[part, :]) * steep[:, part]).astype(bf16)
-    for chunk in range(CHUNKS):
-        grad = contract_cols(slope[...], first[pl.ds(chunk * width, width), :])
-        grad_out[chunk] = grad.reshape(devices, slot_rows, width).astype(bf16)
-        scatter_start(
-            grad_out.at[chunk], back.at[chunk], back_send.at[chunk], back_recv.at[chunk]
-        )
-    saves = [
+    span = embed // BACK_CHUNKS
+    for group in range(BACK_CHUNKS):
+        grad = contract_cols(slope[...], first[pl.ds(group * span, span), :])
+        grad_out[group] = grad.reshape(devices, slot_rows, span).astype(bf16)
+        scatter_start(grad_out.at[group], back.at[group], back_sems.at[group])
+    results = [
         pltpu.make_async_copy(source_rows, source_hbm, save_sem.at[0]),
         pltpu.make_async_copy(hidden, hidden_hbm, save_sem.at[1]),
         pltpu.make_async_copy(error, error_hbm, save_sem.at[2]),
         pltpu.make_async_copy(slope, slope_hbm, save_sem.at[3]),
     ]
-    for save in saves:
+    for save in results:
         save.start()
+    saves = saves + results
 
     def chip_at(step):
-        return lax.rem(chip + step, chips) * 2 + core
+        return across(chip, step) * 2 + core
 
     sends = []
 
@@ -462,20 +491,6 @@
         return remote(
             block, block, share_send.at[chunk, slot], share_recv.at[chunk, origin], target, gy
         )
-
-    for chunk in range(CHUNKS):
-        scatter_wait(
-            grad_out.at[chunk], back.at[chunk], back_send.at[chunk], back_recv.at[chunk]
-        )
-        packed = back[chunk].astype(f32).reshape(slots, width).astype(bf16)
-        mine = contract_rows(place[...], packed)
-        shared[chunk, gx] = mine.astype(bf16)
-        for step in range(1, chips):
-            send(share_copy(chunk, gx, chip_at(step), step))
-        send(share_copy(chunk, gx, partner, 0))
-
-    for step in range(1, gx_n):
-        feat_copy(step).wait()
 
     def part_of(chunk, block):
         total = jnp.zeros((part_rows, width), f32)
@@ -486,7 +501,7 @@
         return total
 
     def part_copy(chunk, step):
-        other = lax.rem(gy + step, gy_n)
+        other = across(gy, step)
         return remote(
             parts.at[chunk, other],
             landed.at[chunk, step],
@@ -496,20 +511,6 @@
             other,
         )
 
-    own = []
-    for chunk in range(CHUNKS):
-        for step in range(1, chips):
-            origin = chip_at(chips - step)
-            share_copy(chunk, origin, partner, chips + step).wait_recv()
-            send(share_copy(chunk, origin, partner, chips + step))
-        for step in range(chips):
-            share_copy(chunk, chip_at(step) + 1 - 2 * core, partner, 0).wait_recv()
-        for step in range(1, gy_n):
-            other = lax.rem(gy + step, gy_n)
-            parts[chunk, other] = part_of(chunk, other).astype(bf16)
-            part_copy(chunk, step).start()
-        own.append(part_of(chunk, gy))
-
     def out_copy(chunk, block_x, block_y, send_sem, target_x, target_y):
         block = summed_ref.at[chunk, block_x, block_y]
         return remote(
@@ -519,45 +520,96 @@
     def out_wait(chunk, block_x, block_y):
         out_copy(chunk, block_x, block_y, line_send.at[0, 0], partner, gy).wait_recv()
 
-    for chunk in range(CHUNKS):
+    near = [chip_at(step) for step in range(1, chips)]
+    own = {}
+
+    def back_event(group):
+        scatter_wait(grad_out.at[group], back.at[group], back_sems.at[group])
+        packed = back[group].astype(f32).reshape(slots, span).astype(bf16)
+        mine = contract_rows(place[...], packed).astype(bf16)
+        for piece in range(span // width):
+            chunk = group * (span // width) + piece
+            shared[chunk, gx] = mine[:, piece * width : (piece + 1) * width]
+            for step in range(1, chips):
+                send(share_copy(chunk, gx, chip_at(step), step))
+            send(share_copy(chunk, gx, partner, 0))
+
+    def share_event(chunk):
+        for step in range(1, chips):
+            origin = chip_at(step)
+            share_copy(chunk, origin, partner, chips + step).wait_recv()
+            send(share_copy(chunk, origin, partner, chips + step))
+
+    def part_event(chunk):
+        for step in range(chips):
+            share_copy(chunk, chip_at(step) + 1 - 2 * core, partner, 0).wait_recv()
+        if chunk == 0:
+            for step in range(1, gx_n):
+                feat_copy(step).wait()
+        for step in range(1, gy_n):
+            other = across(gy, step)
+            parts[chunk, other] = part_of(chunk, other).astype(bf16)
+            part_copy(chunk, step).start()
+        own[chunk] = part_of(chunk, gy)
+
+    def spread(chunk, line):
+        block_y = across(gy, line)
+        for slot, target in enumerate(near):
+            send(out_copy(chunk, gx, block_y, plane_send.at[chunk, line, slot], target, gy))
+        send(out_copy(chunk, gx, block_y, pair_send.at[chunk, line, 0], partner, gy))
+
+    def total_event(chunk):
         total = own[chunk]
         for step in range(1, gy_n):
             part_copy(chunk, step).wait()
             total = total + landed[chunk, step].astype(f32)
         summed_ref[chunk, gx, gy] = total.astype(bf16)
         for step in range(1, gy_n):
-            other = lax.rem(gy + step, gy_n)
+            other = across(gy, step)
             send(out_copy(chunk, gx, gy, line_send.at[chunk, step], gx, other))
-        for step in range(1, chips):
-            send(out_copy(chunk, gx, gy, plane_send.at[chunk, 0, step], chip_at(step), gy))
-        send(out_copy(chunk, gx, gy, pair_send.at[chunk, 0, 0], partner, gy))
-    for chunk in range(CHUNKS):
-        for line in range(1, gy_n):
-            block_y = lax.rem(gy + line, gy_n)
-            out_wait(chunk, gx, block_y)
-            for step in range(1, chips):
-                send(
-                    out_copy(
-                        chunk, gx, block_y, plane_send.at[chunk, line, step], chip_at(step), gy
-                    )
+        spread(chunk, 0)
+
+    def line_event(chunk, line):
+        out_wait(chunk, gx, across(gy, line))
+        spread(chunk, line)
+
+    def near_event(chunk, line):
+        block_y = across(gy, line)
+        for slot, block_x in enumerate(near):
+            out_wait(chunk, block_x, block_y)
+            send(
+                out_copy(
+                    chunk, block_x, block_y, pair_send.at[chunk, line, 1 + slot], partner, gy
                 )
-            send(out_copy(chunk, gx, block_y, pair_send.at[chunk, line, 0], partner, gy))
-    for chunk in range(CHUNKS):
-        for line in range(gy_n):
-            block_y = lax.rem(gy + line, gy_n)
-            for step in range(1, chips):
-                block_x = chip_at(step)
-                out_wait(chunk, block_x, block_y)
-                send(
-                    out_copy(
-                        chunk, block_x, block_y, pair_send.at[chunk, line, step], partner, gy
-                    )
-                )
-    for chunk in range(CHUNKS):
+            )
+
+    def pair_event(chunk):
         for line in range(gy_n):
             for step in range(chips):
                 out_wait(chunk, chip_at(step) + 1 - 2 * core, line)
-    for copy in sends:
+        save = pltpu.make_async_copy(
+            summed_ref.at[chunk], summed_hbm.at[chunk], save_sem.at[5 + chunk]
+        )
+        save.start()
+        saves.append(save)
+
+    events = []
+    for chunk in range(CHUNKS):
+        if chunk * BACK_CHUNKS % CHUNKS == 0:
+            group = chunk * BACK_CHUNKS // CHUNKS
+            events.append((6.0 + 1.4 * chunk, back_event, group))
+        events.append((9.8 + 1.6 * chunk, share_event, chunk))
+        events.append((11.2 + 1.6 * chunk, part_event, chunk))
+        base = 16.0 + 2.6 * chunk
+        events.append((base, total_event, chunk))
+        events.append((base + 3.2, near_event, chunk, 0))
+        for line in range(1, gy_n):
+            events.append((base + 3.0 + 0.5 * line, line_event, chunk, line))
+            events.append((base + 6.0 + 0.5 * line, near_event, chunk, line))
+        events.append((base + 12.0, pair_event, chunk))
+    for event in sorted(events, key=lambda event: event[0]):
+        event[1](*event[2:])
+    for copy in sends + unsent:
         copy.wait_send()
     for save in saves:
         save.wait()
@@ -628,8 +680,8 @@
     anywhere = pl.BlockSpec(memory_space=pl.ANY)
     padded = (fields_n, size_x + 4, size_y + 2 * PAD, size_z)
     faces = (STEPS, 2, fields_n, size_x, 2, size_z)
-    source_shape = (devices, slot_rows, embed + 128)
-    target_shape = (devices, slot_rows, embed)
+    source_shape = (devices, slot_rows, embed)
+    valid_shape = (devices, slot_rows, 128)
     feat_shape = (gx_n, gy_n, part_rows, rows)
     block_shape = (CHUNKS, gx_n, gy_n, part_rows, width)
     new_fields, summed, source, hidden, error, slope = pl.pallas_call(
@@ -643,11 +695,15 @@
             jax.ShapeDtypeStruct((slots, hidden_n), bf16),
         ],
         in_specs=[anywhere, anywhere, whole, whole, anywhere, whole, anywhere, whole],
-        out_specs=[whole, whole] + [anywhere] * 4,
+        out_specs=[anywhere] * 6,
         scratch_shapes=[
             vmem(padded, f32),
             vmem(padded, f32),
             vmem(padded, f32),
+            vmem(fields.shape, f32),
+            vmem(block_shape, bf16),
+            vmem(valid_shape, bf16),
+            vmem(valid_shape, bf16),
             vmem(faces, f32),
             vmem(faces, f32),
             vmem((columns * size_z, PATCH * rows), bf16),
@@ -659,8 +715,8 @@
             vmem((hidden_n, embed), bf16),
             vmem(source_shape, bf16),
             vmem(source_shape, bf16),
-            vmem(target_shape, bf16),
-            vmem(target_shape, bf16),
+            vmem(source_shape, bf16),
+            vmem(source_shape, bf16),
             vmem(feat_shape, bf16),
             vmem(feat_shape, bf16),
             vmem((slots, embed), bf16),
@@ -668,23 +724,21 @@
             vmem((slots, hidden_n), f32),
             vmem((slots, embed), bf16),
             vmem((slots, hidden_n), bf16),
-            vmem((CHUNKS, devices, slot_rows, width), bf16),
-            vmem((CHUNKS, devices, slot_rows, width), bf16),
+            vmem((BACK_CHUNKS, devices, slot_rows, embed // BACK_CHUNKS), bf16),
+            vmem((BACK_CHUNKS, devices, slot_rows, embed // BACK_CHUNKS), bf16),
             vmem((CHUNKS, gx_n, rows, width), bf16),
             vmem((CHUNKS, gy_n, part_rows, width), bf16),
             vmem((CHUNKS, gy_n, part_rows, width), bf16),
             dma((4,)),
-            dma((4,)),
+            dma((5 + CHUNKS,)),
+            dma((2,)),
             dma((STEPS, 4)),
             dma((STEPS, 4)),
-            dma((devices,)),
-            dma((devices,)),
-            dma((devices,)),
-            dma((devices,)),
+            dma((2,)),
+            dma((2,)),
             dma((gx_n,)),
             dma((gx_n,)),
-            dma((CHUNKS, devices)),
-            dma((CHUNKS, devices)),
+            dma((BACK_CHUNKS, 2)),
             dma((CHUNKS, 2 * chips)),
             dma((CHUNKS, gx_n)),
             dma((CHUNKS, gy_n)),

time: 99.1 us -> 94 us (0.949)
  the two profiles are of different devices: /device:TPU:9 before, /device:TPU:0 now
where the time goes in v4:
time: 94 us; the launch traced here: 93.8 us
  Pallas kernels  92.1 us (98%)
  local copies, waits for them, and re-layouts  1.06 us (1%)
    pallas_call x1, Pallas kernels, per_device(): pl.pallas_call(functools.partial(step_kernel, gx_n, gy_n), out_shape=[jax...  84.3 us
    pallas_call x1, Pallas kernels, finish(): pl.pallas_call(finish_kernel, grid=(steps,), out_shape=[jax.ShapeDtypeStr...  7.75 us

profile of v4, /device:TPU:0, one launch (start us, length us, event | category | flops | bytes accessed | tf_op | source)
XLA Modules:
  0.0 93.8 jit_solution(17761577092432063956)
XLA Ops:
  0.6 84.3 %shard_map.127 = (f32[5,16,32,128]{3,2,1,0:T(8,128)}, bf16[2,8,4,80,256]{4,3,2,1,0:T(8,128)(2,1)}, bf16[256,512]{1,0:T(8,128)(2,1)}, bf16[256,2048]{1,0:T(8,128)...) custom-call(f32[5,16,32,128]{3,2,1,0:T(8,128)} %fields_hbm.1, bf16[2560,512]{1,0:T(8,128)(2,1)} %weight_hbm.1, ...), custom_call_target="tpu_custom_call" | custom-call | tf_op jit(solution)/shard_map/pallas_call | solution.py:687
  85.0 0.0 copy-start
  85.0 7.8 %shard_map.128 = (f32[1,512,2048]{2,1,0:T(8,128)}, f32[1,2048]{1,0:T(1,128)}, f32[1,2048,512]{2,1,0:T(8,128)}, f32[1,512]{1,0:T(1,128)}, f32[2560,512]{1,0:T(8,128)}) custom-call(bf16[256,512]{1,0:T(8,128)(2,1)} %get-tuple-element.18.source_ref, bf16[256,2048]{1,0:T(8,128)(2,1)} %get-tuple-element.19.hidden_ref, ...), custom_call_target="tpu_custom_call" | custom-call | tf_op jit(solution)/shard_map/pallas_call | solution.py:636
  92.7 0.0 copy-done
  92.7 1.1 %copy.15 = f32[5,16,32,128]{3,2,1,0:T(8,128)} copy(f32[5,16,32,128]{3,2,1,0:T(8,128)S(1)} %copy-done) | data formatting | bytes 2621440
Async XLA Ops:
  85.0 7.8 %copy-start = (f32[5,16,32,128]{3,2,1,0:T(8,128)S(1)}, f32[5,16,32,128]{3,2,1,0:T(8,128)}, u32[]{:S(2)}) copy-start(f32[5,16,32,128]{3,2,1,0:T(8,128)} %get-tuple-element.34) | copy-start | bytes 3932164

commit v5 on v4

--- a/solution.py
+++ b/solution.py
@@ -12,6 +12,7 @@
 STEPS = 3
 BLOCK_ROWS = 2
 PAD = 8
+FACE_TYPE = jnp.float32
 CHUNKS = 2
 BACK_CHUNKS = 2
 HIDDEN_TILE = 512
@@ -85,6 +86,8 @@
     summed_ref,
     valid_out,
     valid_in,
+    side_out,
+    side_in,
     face_out,
     face_in,
     swap,
@@ -186,96 +189,67 @@
         return carry
 
     lax.fori_loop(1, devices, greet, 0)
-    place_of = lax.broadcasted_iota(jnp.int32, (size_z, PATCH * rows), 1)
-    column_of = lax.rem(place_of, rows) // count_z
-    cell_of = column_of * size_z + lax.rem(place_of, count_z) * PATCH + place_of // rows
-    for column in range(columns):
-        row_of = lax.broadcasted_iota(jnp.int32, (size_z, PATCH * rows), 0) + column * size_z
-        swap[pl.ds(column * size_z, size_z), :] = jnp.where(row_of == cell_of, 1.0, 0.0).astype(
-            jnp.bfloat16
-        )
-
-    owner = owner_ref[...].astype(f32)
-    blocks = owner.shape[1]
-    tall = lax.broadcasted_iota(jnp.int32, (devices, blocks), 0).astype(f32)
-    onehot = jnp.where(owner == tall, 1.0, 0.0)
-    before = jnp.where(
-        lax.broadcasted_iota(jnp.int32, (blocks, blocks), 0)
-        < lax.broadcasted_iota(jnp.int32, (blocks, blocks), 1),
-        1.0,
-        0.0,
-    )
-    ahead = jnp.dot(onehot.astype(bf16), before.astype(bf16), preferred_element_type=f32)
-    rank = jnp.sum(ahead * onehot, axis=0, keepdims=True)
-    block_slot = owner * float(slot_rows // BLOCK_ROWS) + rank
-    slots = place.shape[0]
-    slot_block = lax.broadcasted_iota(jnp.int32, (slots, blocks), 0) // BLOCK_ROWS
-    block_place = jnp.where(block_slot == slot_block.astype(f32), 1.0, 0.0)
-    spread_rows = jnp.where(
-        lax.broadcasted_iota(jnp.int32, (blocks, rows), 1) // BLOCK_ROWS
-        == lax.broadcasted_iota(jnp.int32, (blocks, rows), 0),
-        1.0,
-        0.0,
-    )
-    row_place = jnp.dot(
-        block_place.astype(bf16), spread_rows.astype(bf16), preferred_element_type=f32
-    )
-    same = lax.rem(lax.broadcasted_iota(jnp.int32, (slots, rows), 0), BLOCK_ROWS) == lax.rem(
-        lax.broadcasted_iota(jnp.int32, (slots, rows), 1), BLOCK_ROWS
-    )
-    place[...] = jnp.where(same, row_place, 0.0).astype(bf16)
     pl.semaphore_wait(barrier, devices - 1)
 
+    def halo_ends(side):
+        if side < 2:
+            return side_out, side_in, (gx - 1 if side == 0 else gx + 1, gy)
+        return face_out, face_in, (gx, gy - 1 if side == 2 else gy + 1)
+
     def halo_copy(step, side):
-        state = states[step]
-        if side == 0:
-            src, dst = state.at[:, pl.ds(2, 2), inner], state.at[:, pl.ds(size_x + 2, 2), inner]
-            target = (gx - 1, gy)
-        elif side == 1:
-            src, dst = state.at[:, pl.ds(size_x, 2), inner], state.at[:, pl.ds(0, 2), inner]
-            target = (gx + 1, gy)
-        else:
-            src, dst = face_out.at[step, side - 2], face_in.at[step, 3 - side]
-            target = (gx, gy - 1 if side == 2 else gy + 1)
+        out, landing, target = halo_ends(side)
         return remote(
-            src, dst, halo_send.at[step, side], halo_recv.at[step, side ^ 1], *target
+            out.at[step, side % 2],
+            landing.at[step, 1 - side % 2],
+            halo_send.at[step, side],
+            halo_recv.at[step, side ^ 1],
+            *target
         )
 
     def halo_start(step):
         state = states[step]
-        for side in (2, 3):
-            first = PAD if side == 2 else PAD + size_y - 2
-            face_out[step, side - 2] = state[:, pl.ds(2, size_x), pl.ds(first, 2), :]
-        for inside, side in edges:
+        for side, (inside, _) in enumerate(edges):
             @pl.when(inside)
             def _():
+                if side < 2:
+                    first = 2 if side == 0 else size_x
+                    values = state[:, pl.ds(first, 2), inner, :]
+                else:
+                    first = PAD if side == 2 else PAD + size_y - 2
+                    values = state[:, pl.ds(2, size_x), pl.ds(first, 2), :]
+                out = halo_ends(side)[0]
+                out[step, side % 2] = values.astype(out.dtype)
                 halo_copy(step, side).start()
 
     def halo_wait(step):
         state = states[step]
-        for inside, side in edges:
+        for side, (inside, _) in enumerate(edges):
             @pl.when(inside)
             def _():
-                copy = halo_copy(step, side)
-                copy.wait_send()
+                landing = halo_ends(side)[1]
+                block = landing.at[step, side % 2]
                 remote(
-                    face_in.at[step, 0] if side > 1 else state.at[:, pl.ds(0, 2), inner],
-                    face_in.at[step, 0] if side > 1 else state.at[:, pl.ds(0, 2), inner],
-                    halo_send.at[step, side],
-                    halo_recv.at[step, side],
-                    gx,
-                    gy,
+                    block, block, halo_send.at[step, side], halo_recv.at[step, side], gx, gy
                 ).wait_recv()
-                if side > 1:
+                values = landing[step, side % 2].astype(jnp.float32)
+                if side < 2:
+                    state[:, pl.ds(0 if side == 0 else size_x + 2, 2), inner, :] = values
+                else:
                     first = PAD - 2 if side == 2 else PAD + size_y
-                    state[:, pl.ds(2, size_x), pl.ds(first, 2), :] = face_in[step, side - 2]
-
-    def advance_part(step, first_plane, planes, first_row, count):
+                    state[:, pl.ds(2, size_x), pl.ds(first, 2), :] = values
+
+    def advance_part(step, first_plane, planes, pieces_of, count):
         state = states[step]
         lane = lax.broadcasted_iota(jnp.int32, (count, size_z), 1)
-        here = pl.ds(PAD + first_row, count)
 
         def plane(i, carry):
+            for ahead, first_row in pieces_of:
+                piece(i + ahead, first_row)
+            return carry
+
+        def piece(i, first_row):
+            here = pl.ds(PAD + first_row, count)
+
             def pieces(field):
                 middle = state[field, i + 2, here, :]
                 around = []
@@ -316,19 +290,15 @@
             put(4, middle_p + scale * (change_p - spread))
             middle, slopes, change = pieces(0)
             put(0, middle + scale * (change - spread))
-            return carry
 
         lax.fori_loop(first_plane, first_plane + planes, plane, 0)
 
     def advance_inside(step):
-        advance_part(step, 2, size_x - 4, PAD, size_y - 2 * PAD)
+        advance_part(step, 2, size_x - 4, ((0, PAD),), size_y - 2 * PAD)
 
     def advance_edges(step):
-        advance_part(step, 0, 2, 0, size_y)
-        advance_part(step, size_x - 2, 2, 0, size_y)
-        advance_part(step, 2, size_x - 4, 0, PAD)
-        advance_part(step, 2, size_x - 4, size_y - PAD, PAD)
-
+        advance_part(step, 0, 2, ((0, 0), (size_x - 2, 0)), size_y)
+        advance_part(step, 2, size_x - 4, ((0, 0), (0, size_y - PAD)), PAD)
 
     def column_cells(state, offset_x, offset_y, column):
         first_x = offset_x + column // count_y * PATCH
@@ -381,16 +351,56 @@
 
     loads[0].wait()
     halo_start(0)
+    place_of = lax.broadcasted_iota(jnp.int32, (1, PATCH * rows), 1)
+    column_of = lax.rem(place_of, rows) // count_z
+    cell_of = column_of * size_z + lax.rem(place_of, count_z) * PATCH + place_of // rows
+    for column in range(columns):
+        row_of = lax.broadcasted_iota(jnp.int32, (size_z, PATCH * rows), 0) + column * size_z
+        swap[pl.ds(column * size_z, size_z), :] = jnp.where(row_of == cell_of, 1.0, 0.0).astype(
+            jnp.bfloat16
+        )
+
+    owner = owner_ref[...].astype(f32)
+    blocks = owner.shape[1]
+    tall = lax.broadcasted_iota(jnp.int32, (devices, blocks), 0).astype(f32)
+    onehot = jnp.where(owner == tall, 1.0, 0.0)
+    before = jnp.where(
+        lax.broadcasted_iota(jnp.int32, (blocks, blocks), 0)
+        < lax.broadcasted_iota(jnp.int32, (blocks, blocks), 1),
+        1.0,
+        0.0,
+    )
+    ahead = jnp.dot(onehot.astype(bf16), before.astype(bf16), preferred_element_type=f32)
+    rank = jnp.sum(ahead * onehot, axis=0, keepdims=True)
+    block_slot = owner * float(slot_rows // BLOCK_ROWS) + rank
+    slots = place.shape[0]
+    slot_block = lax.broadcasted_iota(jnp.int32, (slots, blocks), 0) // BLOCK_ROWS
+    block_place = jnp.where(block_slot == slot_block.astype(f32), 1.0, 0.0)
+    spread_rows = jnp.where(
+        lax.broadcasted_iota(jnp.int32, (blocks, rows), 1) // BLOCK_ROWS
+        == lax.broadcasted_iota(jnp.int32, (blocks, rows), 0),
+        1.0,
+        0.0,
+    )
+    row_place = jnp.dot(
+        block_place.astype(bf16), spread_rows.astype(bf16), preferred_element_type=f32
+    )
+    same = lax.rem(lax.broadcasted_iota(jnp.int32, (slots, rows), 0), BLOCK_ROWS) == lax.rem(
+        lax.broadcasted_iota(jnp.int32, (slots, rows), 1), BLOCK_ROWS
+    )
+    place[...] = jnp.where(same, row_place, 0.0).astype(bf16)
     filled = jnp.sum(place[...].astype(f32), axis=1, keepdims=True)
     filled = jnp.broadcast_to(filled, (slots, valid_out.shape[2]))
     valid_out[...] = filled.reshape(valid_out.shape).astype(bf16)
     valid_args = (valid_out, valid_in, valid_sems)
     scatter_start(*valid_args)
+    advance_inside(0)
     halo_wait(0)
-    advance_part(0, 0, size_x, 0, size_y)
+    advance_edges(0)
     halo_start(1)
+    advance_inside(1)
     halo_wait(1)
-    advance_part(1, 0, size_x, 0, size_y)
+    advance_edges(1)
     halo_start(2)
     stretch = jnp.where(
         lax.broadcasted_iota(jnp.int32, (count_z, size_z), 1) // PATCH
@@ -426,8 +436,9 @@
             feat_out.at[other], feats.at[gx], feat_send.at[step], feat_recv.at[step], other, gy
         )
 
+    advance_inside(2)
     halo_wait(2)
-    advance_part(2, 0, size_x, 0, size_y)
+    advance_edges(2)
     saves = [pltpu.make_async_copy(out_ref, fields_out_hbm, save_sem.at[4])]
     saves[0].start()
     for column in range(columns):
@@ -611,6 +622,12 @@
         event[1](*event[2:])
     for copy in sends + unsent:
         copy.wait_send()
+    for step in range(STEPS):
+        for inside, side in edges:
+            @pl.when(inside)
+            def _():
+                halo_copy(step, side).wait_send()
+
     for save in saves:
         save.wait()
 
@@ -679,6 +696,7 @@
     whole = pl.BlockSpec(memory_space=pltpu.VMEM)
     anywhere = pl.BlockSpec(memory_space=pl.ANY)
     padded = (fields_n, size_x + 4, size_y + 2 * PAD, size_z)
+    sides = (STEPS, 2, fields_n, 2, size_y, size_z)
     faces = (STEPS, 2, fields_n, size_x, 2, size_z)
     source_shape = (devices, slot_rows, embed)
     valid_shape = (devices, slot_rows, 128)
@@ -704,8 +722,10 @@
             vmem(block_shape, bf16),
             vmem(valid_shape, bf16),
             vmem(valid_shape, bf16),
-            vmem(faces, f32),
-            vmem(faces, f32),
+            vmem(sides, bf16),
+            vmem(sides, bf16),
+            vmem(faces, FACE_TYPE),
+            vmem(faces, FACE_TYPE),
             vmem((columns * size_z, PATCH * rows), bf16),
             vmem((features // PATCH, columns * size_z), bf16),
             vmem((features, rows), f32),

time: 94 us -> 87.9 us (0.935)
  Pallas kernels: 92.1 us -> 85.2 us
    pallas_call x1, Pallas kernels: 84.3 us -> 77.5 us  [per_device(): pl.pallas_call(functools.partial(step_kernel, gx_n, gy_n), out_shape=[jax...]
where the time goes in v5:
time: 87.9 us; the launch traced here: 87 us
  Pallas kernels  85.2 us (97%)
  local copies, waits for them, and re-layouts  1.06 us (1%)
    pallas_call x1, Pallas kernels, per_device(): pl.pallas_call(functools.partial(step_kernel, gx_n, gy_n), out_shape=[jax...  77.5 us
    pallas_call x1, Pallas kernels, finish(): pl.pallas_call(finish_kernel, grid=(steps,), out_shape=[jax.ShapeDtypeStr...  7.75 us

profile of v5, /device:TPU:0, one launch (start us, length us, event | category | flops | bytes accessed | tf_op | source)
XLA Modules:
  0.0 87.0 jit_solution(7116620063039339947)
XLA Ops:
  0.6 77.5 %shard_map.127 = (f32[5,16,32,128]{3,2,1,0:T(8,128)}, bf16[2,8,4,80,256]{4,3,2,1,0:T(8,128)(2,1)}, bf16[256,512]{1,0:T(8,128)(2,1)}, bf16[256,2048]{1,0:T(8,128)...) custom-call(f32[5,16,32,128]{3,2,1,0:T(8,128)} %fields_hbm.1, bf16[2560,512]{1,0:T(8,128)(2,1)} %weight_hbm.1, ...), custom_call_target="tpu_custom_call" | custom-call | tf_op jit(solution)/shard_map/pallas_call | solution.py:705
  78.1 0.0 copy-start
  78.1 7.8 %shard_map.128 = (f32[1,512,2048]{2,1,0:T(8,128)}, f32[1,2048]{1,0:T(1,128)}, f32[1,2048,512]{2,1,0:T(8,128)}, f32[1,512]{1,0:T(1,128)}, f32[2560,512]{1,0:T(8,128)}) custom-call(bf16[256,512]{1,0:T(8,128)(2,1)} %get-tuple-element.18.source_ref, bf16[256,2048]{1,0:T(8,128)(2,1)} %get-tuple-element.19.hidden_ref, ...), custom_call_target="tpu_custom_call" | custom-call | tf_op jit(solution)/shard_map/pallas_call | solution.py:653
  85.9 0.0 copy-done
  85.9 1.1 %copy.15 = f32[5,16,32,128]{3,2,1,0:T(8,128)} copy(f32[5,16,32,128]{3,2,1,0:T(8,128)S(1)} %copy-done) | data formatting | bytes 2621440
Async XLA Ops:
  78.1 7.8 %copy-start = (f32[5,16,32,128]{3,2,1,0:T(8,128)S(1)}, f32[5,16,32,128]{3,2,1,0:T(8,128)}, u32[]{:S(2)}) copy-start(f32[5,16,32,128]{3,2,1,0:T(8,128)} %get-tuple-element.34) | copy-start | bytes 3932164

commit v6 on v5

--- a/solution.py
+++ b/solution.py
@@ -16,6 +16,7 @@
 CHUNKS = 2
 BACK_CHUNKS = 2
 HIDDEN_TILE = 512
+FINISH_STEPS = 4
 
 
 time_step = 0.2
@@ -67,12 +68,12 @@
     gy_n,
     fields_hbm,
     weight_hbm,
-    owner_ref,
-    lag_ref,
+    owner_hbm,
+    lag_hbm,
     first_hbm,
-    first_bias_ref,
+    first_bias_hbm,
     second_hbm,
-    second_bias_ref,
+    second_bias_hbm,
     fields_out_hbm,
     summed_hbm,
     source_hbm,
@@ -84,6 +85,10 @@
     state_2,
     out_ref,
     summed_ref,
+    owner_ref,
+    lag_ref,
+    first_bias_ref,
+    second_bias_ref,
     valid_out,
     valid_in,
     side_out,
@@ -104,6 +109,7 @@
     feat_out,
     feats,
     source_rows,
+    source_turned,
     hidden,
     steep,
     error,
@@ -147,10 +153,23 @@
     columns = count_x * count_y
     kinds = FIELDS * PATCH * PATCH
     rows = turned.shape[1]
-    hidden_n = hidden.shape[1]
+    hidden_n = hidden.shape[0]
     width = embed // CHUNKS
     f32, bf16 = jnp.float32, jnp.bfloat16
 
+    barrier = pltpu.get_barrier_semaphore()
+
+    def greet(step, carry):
+        other = lax.rem(me + step, devices)
+        pl.semaphore_signal(
+            barrier,
+            inc=1,
+            device_id=(other // gy_n, lax.rem(other, gy_n)),
+            device_id_type=pl.DeviceIdType.MESH,
+        )
+        return carry
+
+    lax.fori_loop(1, devices, greet, 0)
     loads = [
         pltpu.make_async_copy(
             fields_hbm, state_0.at[:, pl.ds(2, size_x), inner, :], load_sem.at[0]
@@ -158,37 +177,15 @@
         pltpu.make_async_copy(weight_hbm, weight, load_sem.at[1]),
         pltpu.make_async_copy(first_hbm.at[0], first, load_sem.at[2]),
         pltpu.make_async_copy(second_hbm.at[0], second, load_sem.at[3]),
+        pltpu.make_async_copy(owner_hbm, owner_ref, load_sem.at[4]),
+        pltpu.make_async_copy(lag_hbm, lag_ref, load_sem.at[5]),
+        pltpu.make_async_copy(first_bias_hbm, first_bias_ref, load_sem.at[6]),
+        pltpu.make_async_copy(second_bias_hbm, second_bias_ref, load_sem.at[7]),
     ]
     for load in loads:
         load.start()
 
     edges = ((gx > 0, 0), (gx < gx_n - 1, 1), (gy > 0, 2), (gy < gy_n - 1, 3))
-    for state in states:
-        for inside, side in edges:
-            @pl.when(jnp.logical_not(inside))
-            def _():
-                if side < 2:
-                    plane = pl.ds(0 if side == 0 else size_x + 2, 2)
-                    state[:, plane, inner, :] = jnp.zeros((FIELDS, 2, size_y, size_z), jnp.float32)
-                else:
-                    strip = pl.ds(0 if side == 2 else PAD + size_y, PAD)
-                    state[:, pl.ds(2, size_x), strip, :] = jnp.zeros(
-                        (FIELDS, size_x, PAD, size_z), jnp.float32
-                    )
-
-    barrier = pltpu.get_barrier_semaphore()
-
-    def greet(step, carry):
-        other = lax.rem(me + step, devices)
-        pl.semaphore_signal(
-            barrier,
-            inc=1,
-            device_id=(other // gy_n, lax.rem(other, gy_n)),
-            device_id_type=pl.DeviceIdType.MESH,
-        )
-        return carry
-
-    lax.fori_loop(1, devices, greet, 0)
     pl.semaphore_wait(barrier, devices - 1)
 
     def halo_ends(side):
@@ -351,6 +348,19 @@
 
     loads[0].wait()
     halo_start(0)
+    for state in states:
+        for inside, side in edges:
+            @pl.when(jnp.logical_not(inside))
+            def _():
+                if side < 2:
+                    plane = pl.ds(0 if side == 0 else size_x + 2, 2)
+                    state[:, plane, inner, :] = jnp.zeros((FIELDS, 2, size_y, size_z), jnp.float32)
+                else:
+                    strip = pl.ds(0 if side == 2 else PAD + size_y, PAD)
+                    state[:, pl.ds(2, size_x), strip, :] = jnp.zeros(
+                        (FIELDS, size_x, PAD, size_z), jnp.float32
+                    )
+
     place_of = lax.broadcasted_iota(jnp.int32, (1, PATCH * rows), 1)
     column_of = lax.rem(place_of, rows) // count_z
     cell_of = column_of * size_z + lax.rem(place_of, count_z) * PATCH + place_of // rows
@@ -360,6 +370,7 @@
             jnp.bfloat16
         )
 
+    loads[4].wait()
     owner = owner_ref[...].astype(f32)
     blocks = owner.shape[1]
     tall = lax.broadcasted_iota(jnp.int32, (devices, blocks), 0).astype(f32)
@@ -408,6 +419,7 @@
         1.0,
         0.0,
     ).astype(bf16)
+    loads[5].wait()
     for column_x in range(count_x):
         lag = lag_ref[column_x].astype(f32).astype(bf16)
         lag = jnp.dot(lag, stretch, preferred_element_type=f32)
@@ -455,8 +467,8 @@
     source_rows[...] = source_in[...].astype(f32).reshape(slots, embed).astype(bf16)
     scatter_wait(*valid_args)
     valid = valid_in[...].astype(f32).reshape(slots, valid_in.shape[2])[:, 0:1]
-    loads[2].wait()
-    loads[3].wait()
+    for load in (loads[2], loads[3], loads[6], loads[7]):
+        load.wait()
     predict = jnp.zeros((slots, embed), f32) + second_bias_ref[...]
     for tile in range(0, hidden_n, HIDDEN_TILE):
         part = pl.ds(tile, HIDDEN_TILE)
@@ -464,9 +476,10 @@
         pre = pre + first_bias_ref[:, part]
         sigma = jax.nn.sigmoid(pre)
         units = (pre * sigma).astype(bf16)
-        hidden[:, part] = units
+        hidden[part, :] = units.T
         steep[:, part] = sigma * (1.0 + pre * (1.0 - sigma))
         predict = predict + jnp.dot(units, second[part, :], preferred_element_type=f32)
+    source_turned[...] = source_rows[...].T
     scatter_wait(*target_args)
     wanted = target_in[...].astype(f32).reshape(slots, embed)
     error[...] = (error_weight * (predict - wanted) * valid).astype(bf16)
@@ -479,7 +492,7 @@
         grad_out[group] = grad.reshape(devices, slot_rows, span).astype(bf16)
         scatter_start(grad_out.at[group], back.at[group], back_sems.at[group])
     results = [
-        pltpu.make_async_copy(source_rows, source_hbm, save_sem.at[0]),
+        pltpu.make_async_copy(source_turned, source_hbm, save_sem.at[0]),
         pltpu.make_async_copy(hidden, hidden_hbm, save_sem.at[1]),
         pltpu.make_async_copy(error, error_hbm, save_sem.at[2]),
         pltpu.make_async_copy(slope, slope_hbm, save_sem.at[3]),
@@ -632,49 +645,91 @@
         save.wait()
 
 
-def finish_kernel(source_ref, hidden_ref, error_ref, slope_ref, summed_ref, *outs):
-    first_ref, first_bias_ref, second_ref, second_bias_ref, patch_ref = outs
-    error, slope = error_ref[...], slope_ref[...]
-    first_ref[0] = contract_rows(source_ref[...], slope)
-    first_bias_ref[...] = jnp.sum(slope.astype(jnp.float32), axis=0, keepdims=True)
-    second_ref[0] = contract_rows(hidden_ref[...], error)
-    second_bias_ref[...] = jnp.sum(error.astype(jnp.float32), axis=0, keepdims=True)
-    width = summed_ref.shape[2]
-    for chunk in range(summed_ref.shape[0]):
-        patch_ref[:, chunk * width : (chunk + 1) * width] = summed_ref[chunk].astype(jnp.float32)
-
-
-def finish(source, hidden, error, slope, summed):
-    slots, embed = source.shape
-    hidden_n = hidden.shape[1]
-    features, width = summed.shape[1], summed.shape[2]
-    steps = hidden_n // HIDDEN_TILE
+def finish_kernel(*refs):
+    sources, results, landings, outs = refs[:5], refs[5:10], refs[10:15], refs[15:20]
+    load_sem, save_sem = refs[20:]
+    source, hidden, error, slope, summed = landings
+    first, first_bias, second, second_bias, patch = outs
     f32 = jnp.float32
+    saves = []
+
+    def load(which, index, slot):
+        copy = pltpu.make_async_copy(
+            sources[which].at[index], landings[which].at[index], load_sem.at[slot]
+        )
+        copy.start()
+        return copy
+
+    def save(which, index):
+        copy = pltpu.make_async_copy(
+            outs[which].at[index], results[which].at[index], save_sem.at[len(saves)]
+        )
+        copy.start()
+        saves.append(copy)
+
+    def pieces(size):
+        return [pl.ds(i * (size // FINISH_STEPS), size // FINISH_STEPS) for i in range(FINISH_STEPS)]
+
+    everything = slice(None)
+    hidden_pieces = pieces(hidden.shape[0])
+    patch_pieces = pieces(patch.shape[0])
+    error_load = load(2, everything, 0)
+    hidden_loads = [load(1, piece, 1 + i) for i, piece in enumerate(hidden_pieces)]
+    slope_load = load(3, everything, 1 + FINISH_STEPS)
+    source_load = load(0, everything, 2 + FINISH_STEPS)
+    summed_loads = [
+        load(4, (everything, piece), 3 + FINISH_STEPS + i) for i, piece in enumerate(patch_pieces)
+    ]
+    error_load.wait()
+    for piece, waiting in zip(hidden_pieces, hidden_loads):
+        waiting.wait()
+        second[0, piece, :] = jnp.dot(hidden[piece, :], error[...], preferred_element_type=f32)
+        save(2, (0, piece))
+    second_bias[...] = jnp.sum(error[...].astype(f32), axis=0, keepdims=True)
+    save(3, everything)
+    slope_load.wait()
+    source_load.wait()
+    for piece in pieces(source.shape[0]):
+        first[0, piece, :] = jnp.dot(source[piece, :], slope[...], preferred_element_type=f32)
+        save(0, (0, piece))
+    first_bias[...] = jnp.sum(slope[...].astype(f32), axis=0, keepdims=True)
+    save(1, everything)
+    width = summed.shape[2]
+    for piece, waiting in zip(patch_pieces, summed_loads):
+        waiting.wait()
+        for chunk in range(summed.shape[0]):
+            patch[piece, chunk * width : (chunk + 1) * width] = summed[chunk, piece, :].astype(f32)
+        save(4, piece)
+    for waiting in saves:
+        waiting.wait()
+
+
+def finish(*values):
+    embed, slots = values[0].shape
+    hidden_n = values[1].shape[0]
+    features = values[4].shape[1]
+    f32 = jnp.float32
+    shapes = [
+        (1, embed, hidden_n),
+        (1, hidden_n),
+        (1, hidden_n, embed),
+        (1, embed),
+        (features, embed),
+    ]
+    anywhere = pl.BlockSpec(memory_space=pl.ANY)
     return pl.pallas_call(
         finish_kernel,
-        grid=(steps,),
-        out_shape=[
-            jax.ShapeDtypeStruct((1, embed, hidden_n), f32),
-            jax.ShapeDtypeStruct((1, hidden_n), f32),
-            jax.ShapeDtypeStruct((1, hidden_n, embed), f32),
-            jax.ShapeDtypeStruct((1, embed), f32),
-            jax.ShapeDtypeStruct((features, embed), f32),
+        out_shape=[jax.ShapeDtypeStruct(shape, f32) for shape in shapes],
+        in_specs=[anywhere] * 5,
+        out_specs=[anywhere] * 5,
+        scratch_shapes=[pltpu.VMEM(value.shape, value.dtype) for value in values]
+        + [pltpu.VMEM(shape, f32) for shape in shapes]
+        + [
+            pltpu.SemaphoreType.DMA((3 + 2 * FINISH_STEPS,)),
+            pltpu.SemaphoreType.DMA((2 + 3 * FINISH_STEPS,)),
         ],
-        in_specs=[
-            pl.BlockSpec((slots, embed), lambda i: (0, 0)),
-            pl.BlockSpec((slots, HIDDEN_TILE), lambda i: (0, i)),
-            pl.BlockSpec((slots, embed), lambda i: (0, 0)),
-            pl.BlockSpec((slots, HIDDEN_TILE), lambda i: (0, i)),
-            pl.BlockSpec((CHUNKS, features // steps, width), lambda i: (0, i, 0)),
-        ],
-        out_specs=[
-            pl.BlockSpec((1, embed, HIDDEN_TILE), lambda i: (0, 0, i)),
-            pl.BlockSpec((1, HIDDEN_TILE), lambda i: (0, i)),
-            pl.BlockSpec((1, HIDDEN_TILE, embed), lambda i: (0, i, 0)),
-            pl.BlockSpec((1, embed), lambda i: (0, 0)),
-            pl.BlockSpec((features // steps, embed), lambda i: (i, 0)),
-        ],
-    )(source, hidden, error, slope, summed)
+        compiler_params=pltpu.CompilerParams(vmem_limit_bytes=62 * 1024 * 1024),
+    )(*values)
 
 
 def per_device(fields, patch_weight, trainer_of, lag_index, w_in, b_in, w_out, b_out):
@@ -693,7 +748,6 @@
     bf16, f32 = jnp.bfloat16, jnp.float32
     dma = pltpu.SemaphoreType.DMA
     vmem = pltpu.VMEM
-    whole = pl.BlockSpec(memory_space=pltpu.VMEM)
     anywhere = pl.BlockSpec(memory_space=pl.ANY)
     padded = (fields_n, size_x + 4, size_y + 2 * PAD, size_z)
     sides = (STEPS, 2, fields_n, 2, size_y, size_z)
@@ -707,12 +761,12 @@
         out_shape=[
             jax.ShapeDtypeStruct(fields.shape, f32),
             jax.ShapeDtypeStruct(block_shape, bf16),
-            jax.ShapeDtypeStruct((slots, embed), bf16),
-            jax.ShapeDtypeStruct((slots, hidden_n), bf16),
+            jax.ShapeDtypeStruct((embed, slots), bf16),
+            jax.ShapeDtypeStruct((hidden_n, slots), bf16),
             jax.ShapeDtypeStruct((slots, embed), bf16),
             jax.ShapeDtypeStruct((slots, hidden_n), bf16),
         ],
-        in_specs=[anywhere, anywhere, whole, whole, anywhere, whole, anywhere, whole],
+        in_specs=[anywhere] * 8,
         out_specs=[anywhere] * 6,
         scratch_shapes=[
             vmem(padded, f32),
@@ -720,6 +774,10 @@
             vmem(padded, f32),
             vmem(fields.shape, f32),
             vmem(block_shape, bf16),
+            vmem((1, blocks), jnp.int32),
+            vmem(lag_index.shape, jnp.int32),
+            vmem(b_in.shape, f32),
+            vmem(b_out.shape, f32),
             vmem(valid_shape, bf16),
             vmem(valid_shape, bf16),
             vmem(sides, bf16),
@@ -740,7 +798,8 @@
             vmem(feat_shape, bf16),
             vmem(feat_shape, bf16),
             vmem((slots, embed), bf16),
-            vmem((slots, hidden_n), bf16),
+            vmem((embed, slots), bf16),
+            vmem((hidden_n, slots), bf16),
             vmem((slots, hidden_n), f32),
             vmem((slots, embed), bf16),
             vmem((slots, hidden_n), bf16),
@@ -749,7 +808,7 @@
             vmem((CHUNKS, gx_n, rows, width), bf16),
             vmem((CHUNKS, gy_n, part_rows, width), bf16),
             vmem((CHUNKS, gy_n, part_rows, width), bf16),
-            dma((4,)),
+            dma((8,)),
             dma((5 + CHUNKS,)),
             dma((2,)),
             dma((STEPS, 4)),

time: 87.9 us -> 86.6 us (0.985)
  Pallas kernels: 85.2 us -> 84.1 us
    pallas_call x1, Pallas kernels: 7.75 us -> 6.53 us  [finish(): pl.pallas_call(finish_kernel, out_shape=[jax.ShapeDtypeStruct(shape, f32)...]
where the time goes in v6:
time: 86.6 us; the launch traced here: 85.8 us
  Pallas kernels  84.1 us (97%)
  local copies, waits for them, and re-layouts  1.06 us (1%)
    pallas_call x1, Pallas kernels, per_device(): pl.pallas_call(functools.partial(step_kernel, gx_n, gy_n), out_shape=[jax...  77.5 us
    pallas_call x1, Pallas kernels, finish(): pl.pallas_call(finish_kernel, out_shape=[jax.ShapeDtypeStruct(shape, f32)...  6.53 us

profile of v6, /device:TPU:0, one launch (start us, length us, event | category | flops | bytes accessed | tf_op | source)
XLA Modules:
  0.0 85.8 jit_solution(3492026988469184344)
XLA Ops:
  0.6 77.5 %shard_map.127 = (f32[5,16,32,128]{3,2,1,0:T(8,128)}, bf16[2,8,4,80,256]{4,3,2,1,0:T(8,128)(2,1)}, bf16[512,256]{1,0:T(8,128)(2,1)}, bf16[2048,256]{1,0:T(8,128)...) custom-call(f32[5,16,32,128]{3,2,1,0:T(8,128)} %fields_hbm.1, bf16[2560,512]{1,0:T(8,128)(2,1)} %weight_hbm.1, ...), custom_call_target="tpu_custom_call" | custom-call | tf_op jit(solution)/shard_map/pallas_call | solution.py:759
  78.2 0.0 copy-start
  78.2 6.5 %shard_map.128 = (f32[1,512,2048]{2,1,0:T(8,128)}, f32[1,2048]{1,0:T(1,128)}, f32[1,2048,512]{2,1,0:T(8,128)}, f32[1,512]{1,0:T(1,128)}, f32[2560,512]{1,0:T(8,128)}) custom-call(bf16[512,256]{1,0:T(8,128)(2,1)} %get-tuple-element.18.refs_0_, bf16[2048,256]{1,0:T(8,128)(2,1)} %get-tuple-element.19.refs_1_, bf16[256,512]{1,0:T(8,128)(2,1)} %get-tuple-element.20.refs_2_, ...), custom_call_target="tpu_custom_call" | custom-call | tf_op jit(solution)/shard_map/pallas_call | solution.py:720
  84.7 0.0 copy-done
  84.7 1.1 %copy.15 = f32[5,16,32,128]{3,2,1,0:T(8,128)} copy(f32[5,16,32,128]{3,2,1,0:T(8,128)S(1)} %copy-done) | data formatting | bytes 2621440
Async XLA Ops:
  78.2 6.5 %copy-start = (f32[5,16,32,128]{3,2,1,0:T(8,128)S(1)}, f32[5,16,32,128]{3,2,1,0:T(8,128)}, u32[]{:S(2)}) copy-start(f32[5,16,32,128]{3,2,1,0:T(8,128)} %get-tuple-element.34) | copy-start | bytes 3932164

commit v7 on v6

--- a/solution.py
+++ b/solution.py
@@ -98,6 +98,7 @@
     swap,
     cells,
     turned,
+    turned_late,
     place,
     weight,
     first,
@@ -302,7 +303,7 @@
         first_y = offset_y + column % count_y * PATCH
         return state[:, pl.ds(first_x, PATCH), pl.ds(first_y, PATCH), :].reshape(kinds, size_z)
 
-    def turn_cells():
+    def turn_cells(turned):
         for offset in range(PATCH):
             turned[pl.ds(offset, kinds, stride=PATCH), :] = jnp.dot(
                 cells[...],
@@ -310,7 +311,7 @@
                 preferred_element_type=f32,
             )
 
-    def embed_rows():
+    def embed_rows(turned):
         return contract_rows(turned[...].astype(bf16), weight[...]).astype(bf16)
 
     def scatter(step, stage, landing, sems):
@@ -429,18 +430,12 @@
             late = column_cells(state_2, 2, PAD, column)
             chosen = jnp.where(lag[column_y : column_y + 1, :] > 0.5, late, early)
             cells[:, pl.ds(column * size_z, size_z)] = chosen.astype(bf16)
-    turn_cells()
+    turn_cells(turned)
     loads[1].wait()
-    source = embed_rows()
+    source = embed_rows(turned)
     source_args = (source_out, source_in, source_sems)
     put_rows(source, source_out)
     scatter_start(*source_args)
-
-    part_rows = feats.shape[2]
-    for block in range(devices):
-        feat_out[block // gy_n, block % gy_n] = turned[
-            pl.ds(block * part_rows, part_rows), :
-        ].astype(bf16)
 
     def feat_copy(step):
         other = lax.rem(gx + step, gx_n)
@@ -455,10 +450,15 @@
     saves[0].start()
     for column in range(columns):
         cells[:, pl.ds(column * size_z, size_z)] = column_cells(out_ref, 0, 0, column).astype(bf16)
-    turn_cells()
+    turn_cells(turned_late)
     target_args = (target_out, target_in, target_sems)
-    put_rows(embed_rows(), target_out)
+    put_rows(embed_rows(turned_late), target_out)
     scatter_start(*target_args)
+    part_rows = feats.shape[2]
+    for block in range(devices):
+        feat_out[block // gy_n, block % gy_n] = turned[
+            pl.ds(block * part_rows, part_rows), :
+        ].astype(bf16)
     for step in range(1, gx_n):
         feat_copy(step).start()
     feats[gx] = feat_out[gx]
@@ -787,6 +787,7 @@
             vmem((columns * size_z, PATCH * rows), bf16),
             vmem((features // PATCH, columns * size_z), bf16),
             vmem((features, rows), f32),
+            vmem((features, rows), f32),
             vmem((slots, rows), bf16),
             vmem((features, embed), bf16),
             vmem((embed, hidden_n), bf16),

time: 86.6 us -> 86.1 us (level)
  no operation moved by 1% of the time
where the time goes in v7:
time: 86.1 us; the launch traced here: 85.9 us
  Pallas kernels  84.2 us (98%)
  local copies, waits for them, and re-layouts  1.06 us (1%)
    pallas_call x1, Pallas kernels, per_device(): pl.pallas_call(functools.partial(step_kernel, gx_n, gy_n), out_shape=[jax...  77.6 us
    pallas_call x1, Pallas kernels, finish(): pl.pallas_call(finish_kernel, out_shape=[jax.ShapeDtypeStruct(shape, f32)...  6.54 us

profile of v7, /device:TPU:0, one launch (start us, length us, event | category | flops | bytes accessed | tf_op | source)
XLA Modules:
  0.0 85.9 jit_solution(15417226829297539667)
XLA Ops:
  0.6 77.6 %shard_map.127 = (f32[5,16,32,128]{3,2,1,0:T(8,128)}, bf16[2,8,4,80,256]{4,3,2,1,0:T(8,128)(2,1)}, bf16[512,256]{1,0:T(8,128)(2,1)}, bf16[2048,256]{1,0:T(8,128)...) custom-call(f32[5,16,32,128]{3,2,1,0:T(8,128)} %fields_hbm.1, bf16[2560,512]{1,0:T(8,128)(2,1)} %weight_hbm.1, ...), custom_call_target="tpu_custom_call" | custom-call | tf_op jit(solution)/shard_map/pallas_call | solution.py:759
  78.3 0.0 copy-start
  78.3 6.5 %shard_map.128 = (f32[1,512,2048]{2,1,0:T(8,128)}, f32[1,2048]{1,0:T(1,128)}, f32[1,2048,512]{2,1,0:T(8,128)}, f32[1,512]{1,0:T(1,128)}, f32[2560,512]{1,0:T(8,128)}) custom-call(bf16[512,256]{1,0:T(8,128)(2,1)} %get-tuple-element.18.refs_0_, bf16[2048,256]{1,0:T(8,128)(2,1)} %get-tuple-element.19.refs_1_, bf16[256,512]{1,0:T(8,128)(2,1)} %get-tuple-element.20.refs_2_, ...), custom_call_target="tpu_custom_call" | custom-call | tf_op jit(solution)/shard_map/pallas_call | solution.py:720
  84.8 0.0 copy-done
  84.8 1.1 %copy.15 = f32[5,16,32,128]{3,2,1,0:T(8,128)} copy(f32[5,16,32,128]{3,2,1,0:T(8,128)S(1)} %copy-done) | data formatting | bytes 2621440
Async XLA Ops:
  78.3 6.6 %copy-start = (f32[5,16,32,128]{3,2,1,0:T(8,128)S(1)}, f32[5,16,32,128]{3,2,1,0:T(8,128)}, u32[]{:S(2)}) copy-start(f32[5,16,32,128]{3,2,1,0:T(8,128)} %get-tuple-element.34) | copy-start | bytes 3932164
